TPU v7x, 32 devices: a whole 2x2x4 slice. The times are simulated.
32 devices in a mesh: delay: 4 (over y, core), row: 8 (over z, x).
Axes of the slice: x: 2, y: 2, z: 4, core: 2. Of those that a mesh axis runs over, the one named last changes fastest.
Arguments:
- incident: bfloat16 [64, 4096], P(None, 'row'), may hold values from -12 to 12
- onset: int32 [64], replicated, may hold values from 0 to 2
- beta: float32 [4096], P('delay'), may hold values from 0.05 to 0.5
- inverse_block: bfloat16 [4096, 4096], P('row', 'delay'), may hold values from -0.0625 to 0.0625
- delay_blocks: bfloat16 [4, 4096, 4096], P('delay', None, 'row'), may hold values from -0.09375 to 0.09375
- history_sum: float32 [4, 64, 4096], P('delay', None, 'row'), may hold values from -12 to 12
Outputs:
- currents: bfloat16 [3, 64, 4096], P(None, None, 'delay')
- carried: float32 [4, 64, 4096], P('delay', None, 'row')
All inputs are finite; a program needn't handle non-finite values.
Results may differ from a plain program's by a relative error of at most 0.0056.
Values may be sent and summed in bfloat16 or wider, within the bound.
No kernel may reach another device: no remote copies, remote signals or barrier semaphores. Data moves between devices by JAX's collectives and lax.ppermute only.
A program may use at most 64 MiB of HBM per device.

v0:
```python
import jax
import jax.numpy as jnp
from jax import lax
from jax.sharding import PartitionSpec as P


STEPS = 3


def bits_of(axis):
    return [1 << b for b in range(lax.axis_size(axis).bit_length() - 1)]


def swapped(value, axis, bit):
    return lax.ppermute(value, axis, [(i, i ^ bit) for i in range(lax.axis_size(axis))])


def swapped_both(value, place_bit, row_bit):
    rows = lax.axis_size("row")
    count = rows * lax.axis_size("delay")
    flip = place_bit * rows + row_bit
    return lax.ppermute(value, ("delay", "row"), [(i, i ^ flip) for i in range(count)])


def total_over_delay(value, wires):
    for bit, wire in zip(bits_of("delay"), wires):
        other = swapped(value.astype(wire), "delay", bit)
        value = value + other.astype(value.dtype)
    return value


def summed_over_row(partial_sum):
    bits = bits_of("row")
    odd = (lax.axis_index("row") & 1) == 1
    half = partial_sum.shape[1] // 2
    low, high = partial_sum[:, :half], partial_sum[:, half:]
    other = swapped(jnp.where(odd, low, high).astype(jnp.bfloat16), "row", bits[0])
    value = jnp.where(odd, high, low) + other.astype(jnp.float32)
    for bit in bits[1:]:
        sent = value.astype(jnp.bfloat16)
        other = swapped(sent, "row", bit)
        value = sent.astype(jnp.float32) + other.astype(jnp.float32)
    return value


def joined(mine, other, second):
    return jnp.where(second, other, mine), jnp.where(second, mine, other)


def columns(mine, other, second):
    return jnp.concatenate(joined(mine, other, second), axis=1)


def spread(parts, bits):
    place = lax.axis_index("delay")
    for bit in bits:
        second = (place & bit) != 0
        pairs = [joined(p, swapped(p, "delay", bit), second) for p in parts]
        parts = [q for pair in pairs for q in pair]
    return jnp.concatenate(parts, axis=1)


def after(value, token):
    return lax.optimization_barrier((value, token))[0]


def steps(incident, onset, beta, inverse_block, delay_blocks, history_sum):
    place = lax.axis_index("delay")
    odd = (lax.axis_index("row") & 1) == 1
    lags = lax.axis_size("delay")
    place_bits = bits_of("delay")
    top = place_bits[-1]
    future = history_sum[0]
    matrix = delay_blocks[0]
    chunk = beta.shape[0]
    half = chunk // 2
    beta_half = jnp.where(odd, beta[half:], beta[:half])[None, :]
    wires = [jnp.float32] + [jnp.bfloat16] * (len(place_bits) - 1)
    incident_wide = incident.astype(jnp.float32)
    drives = []
    for step_index in range(STEPS):
        offset_time = (step_index - onset).astype(jnp.float32)
        envelope = jnp.where(offset_time >= 0.0, jnp.exp(-((offset_time - 1.0) ** 2) / 4.0), 0.0)
        drives.append(incident_wide * envelope[:, None])

    residual = jnp.where(place == 0, drives[0] - future, 0.0).astype(jnp.bfloat16)
    first_residual = residual
    residual = total_over_delay(residual, [jnp.bfloat16] * len(wires))

    first_rows = matrix[:chunk]
    for k in reversed(range(1, lags)):
        rows = after(matrix, first_residual[:8, :k])[k * chunk : (k + 1) * chunk]
        sent = lax.ppermute(rows, "delay", [(0, k)])
        first_rows = lax.optimization_barrier(jnp.where(place == k, sent, first_rows))

    outputs = []
    for step_index in range(STEPS):
        partial_sum = jnp.dot(residual, inverse_block, preferred_element_type=jnp.float32)
        solved = summed_over_row(partial_sum)
        piece = (solved / (1.0 + beta_half * solved * solved)).astype(jnp.bfloat16)
        passed = lax.ppermute(future, "delay", [(i, i - 1) for i in range(1, lags)])
        if step_index + 1 < STEPS:
            current = columns(piece, swapped(piece, "row", 1), odd)
            addend = jnp.dot(current, first_rows, preferred_element_type=jnp.float32)
            addend = addend + jnp.where(place == 1, future, 0.0)
            total = total_over_delay(addend, wires)
            residual = (drives[step_index + 1] - total).astype(jnp.bfloat16)
            gathered = spread([current], reversed(place_bits))
        else:
            far = (place & top) != 0
            both = swapped_both(piece, top, 1)
            near = swapped(piece, "row", 1)
            side = swapped(piece, "delay", top)
            current = columns(piece, near, odd)
            parts = list(joined(current, columns(side, both, odd), far))
            gathered = spread(parts, reversed(place_bits[:-1]))
        outputs.append(current)
        contribution = jnp.dot(gathered, matrix, preferred_element_type=jnp.float32)
        future = passed + contribution
    return (jnp.stack(outputs), future[None])


def solution(mesh):
    placed = (
        P(None, "row"),
        P(),
        P("delay"),
        P("row", "delay"),
        P("delay", None, "row"),
        P("delay", None, "row"),
    )
    return jax.shard_map(
        steps,
        mesh=mesh,
        in_specs=placed,
        out_specs=(P(None, None, "delay"), P("delay", None, "row")),
        check_vma=False,
    )
```

profile of v0, /device:TPU:25, one launch (start us, length us, event | category | flops | bytes accessed | tf_op | source)
XLA Modules:
  0.0 106.6 jit_solution(1574534113021831900)
XLA Ops:
  0.7 0.8 compare_select_fusion
  1.4 1.0 fusion.25
  2.4 0.7 collective-permute-start
  3.2 0.9 collective-permute-done
  4.1 1.3 %collective-permute-start.1 = (bf16[64,512]{1,0:T(8,128)(2,1)S(1)}, bf16[64,512]{1,0:T(8,128)(2,1)S(1)}, u32[]{:S(2)}, u32[]{:S(2)}) collective-permute-start(bf16[64,512]{1,0:T(8,128)(2,1)S(1)} %add.72), channel_id=1, source_target_pairs={{0,16},{8,24},{16,0},{24,8},{1,17},{9,25},{17,1},{25,9},{2,18},{10... | collective-permute-start | bytes 196616 | tf_op jit(solution)/shard_map/ppermute | solution.py:15
  5.4 1.9 %collective-permute-done.1 = bf16[64,512]{1,0:T(8,128)(2,1)S(1)} collective-permute-done((bf16[64,512]{1,0:T(8,128)(2,1)S(1)}, bf16[64,512]{1,0:T(8,128)(2,1)S(1)}, u32[]{:S(2)}, u32[]{:S(2)}) %collective-permute-start.1) | collective-permute-done | bytes 65568 | tf_op jit(solution)/shard_map/ppermute | solution.py:15
  7.6 1.3 %collective-permute-start.2 = (bf16[64,512]{1,0:T(8,128)(2,1)S(1)}, bf16[64,512]{1,0:T(8,128)(2,1)S(1)}, u32[]{:S(2)}, u32[]{:S(2)}) collective-permute-start(bf16[64,512]{1,0:T(8,128)(2,1)S(1)} %select_convert_fusion.2), channel_id=1, source_target_pairs={{0,1},{1,0},{2,3},{3,2},{4,5},{5,4},{6,7},{7,6},{8,9},{9,8},{10,11... | collective-permute-start | bytes 196616 | tf_op jit(solution)/shard_map/ppermute | solution.py:15
  8.9 3.6 %fusion.58 = (bf16[1024,512]{1,0:T(8,128)(2,1)}, bf16[1024,512]{1,0:T(8,128)(2,1)}, bf16[1024,512]{1,0:T(8,128)(2,1)}) fusion(bf16[4096,512]{1,0:T(8,128)(2,1)} %bitcast.25), kind=kLoop, calls=%fused_computation.113 | loop fusion | bytes 6291456 | tf_op jit(solution)/shard_map/slice | solution.py:92
  12.5 0.7 collective-permute-start.8
  13.5 1.3 %collective-permute-start.6 = (bf16[1024,512]{1,0:T(8,128)(2,1)}, bf16[1024,512]{1,0:T(8,128)(2,1)S(1)}, u32[]{:S(2)}, u32[]{:S(2)}) collective-permute-start(bf16[1024,512]{1,0:T(8,128)(2,1)} %get-tuple-element.8), channel_id=1, source_target_pairs={{0,8},{1,9},{2,10},{3,11},{4,12},{5,13},{6,14},{7,15}} | collective-permute-start | bytes 3145736 | tf_op jit(solution)/shard_map/ppermute | solution.py:93
  14.8 1.7 %collective-permute-start.7 = (bf16[1024,512]{1,0:T(8,128)(2,1)}, bf16[1024,512]{1,0:T(8,128)(2,1)}, u32[]{:S(2)}, u32[]{:S(2)}) collective-permute-start(bf16[1024,512]{1,0:T(8,128)(2,1)} %get-tuple-element.7), channel_id=1, source_target_pairs={{0,16},{1,17},{2,18},{3,19},{4,20},{5,21},{6,22},{7,23}} | collective-permute-start | bytes 3145736 | tf_op jit(solution)/shard_map/ppermute | solution.py:93
  16.6 4.0 %collective-permute-done.4 = bf16[64,512]{1,0:T(8,128)(2,1)S(1)} collective-permute-done((bf16[64,512]{1,0:T(8,128)(2,1)S(1)}, bf16[64,512]{1,0:T(8,128)(2,1)S(1)}, u32[]{:S(2)}, u32[]{:S(2)}) %collective-permute-start.4) | collective-permute-done | bytes 65568 | tf_op jit(solution)/shard_map/ppermute | solution.py:15
  20.9 2.9 %collective-permute-done.5 = bf16[64,512]{1,0:T(8,128)(2,1)S(1)} collective-permute-done((bf16[64,512]{1,0:T(8,128)(2,1)S(1)}, bf16[64,512]{1,0:T(8,128)(2,1)S(1)}, u32[]{:S(2)}, u32[]{:S(2)}) %collective-permute-start.5) | collective-permute-done | bytes 65568 | tf_op jit(solution)/shard_map/ppermute | solution.py:15
  23.8 1.4 %bitcast_select_fusion = bf16[1024,512]{1,0:T(8,128)(2,1)S(1)} fusion(bf16[1024,512]{1,0:T(8,128)(2,1)S(1)} %collective-permute-done.8, bf16[1,4096,512]{2,1,0:T(8,128)(2,1)} %param.10, pred[]{:T(512)S(6)} %eq.24), kind=kLoop, calls=%fused_computation.3 | loop fusion | flops 524288 | bytes 3145729 | tf_op jit(solution)/shard_map/jit(_where)/select_n | solution.py:94
  25.8 14.7 %collective-permute-start.9 = (f32[64,512]{1,0:T(8,128)S(1)}, f32[64,512]{1,0:T(8,128)S(1)}, u32[]{:S(2)}, u32[]{:S(2)}) collective-permute-start(f32[64,512]{1,0:T(8,128)S(1)} %convolution_add_fusion.2), channel_id=1, source_target_pairs={{0,8},{8,0},{16,24},{24,16},{1,9},{9,1},{17,25},{25,17},{2,10},{10... | collective-permute-start | bytes 393224 | tf_op jit(solution)/shard_map/ppermute | solution.py:15
  40.5 1.9 %collective-permute-start.15 = (f32[64,512]{1,0:T(8,128)S(1)}, f32[64,512]{1,0:T(8,128)S(1)}, u32[]{:S(2)}, u32[]{:S(2)}) collective-permute-start(f32[64,512]{1,0:T(8,128)S(1)} %bitcast.26), channel_id=1, source_target_pairs={{8,0},{16,8},{24,16},{9,1},{17,9},{25,17},{10,2},{18,10},{26,18},{... | collective-permute-start | bytes 393224 | tf_op jit(solution)/shard_map/ppermute | solution.py:101
  42.5 3.5 %collective-permute-start.10 = (bf16[64,512]{1,0:T(8,128)(2,1)S(1)}, bf16[64,512]{1,0:T(8,128)(2,1)S(1)}, u32[]{:S(2)}, u32[]{:S(2)}) collective-permute-start(bf16[64,512]{1,0:T(8,128)(2,1)S(1)} %get-tuple-element.4), channel_id=1, source_target_pairs={{0,16},{8,24},{16,0},{24,8},{1,17},{9,25},{17,1},{25,9},{2,18},{10... | collective-permute-start | bytes 196616 | tf_op jit(solution)/shard_map/ppermute | solution.py:15
  46.1 2.2 %collective-permute-done.10 = bf16[64,512]{1,0:T(8,128)(2,1)S(1)} collective-permute-done((bf16[64,512]{1,0:T(8,128)(2,1)S(1)}, bf16[64,512]{1,0:T(8,128)(2,1)S(1)}, u32[]{:S(2)}, u32[]{:S(2)}) %collective-permute-start.10) | collective-permute-done | bytes 65568 | tf_op jit(solution)/shard_map/ppermute | solution.py:15
  49.0 2.6 %collective-permute-done.16 = bf16[64,1024]{1,0:T(8,128)(2,1)S(1)} collective-permute-done((bf16[64,1024]{1,0:T(8,128)(2,1)S(1)}, bf16[64,1024]{1,0:T(8,128)(2,1)S(1)}, u32[]{:S(2)}, u32[]{:S(2)}) %collective-permute-start.16) | collective-permute-done | bytes 131104 | tf_op jit(solution)/shard_map/ppermute | solution.py:15
  51.6 1.7 %collective-permute-start.18 = (bf16[64,1024]{1,0:T(8,128)(2,1)S(1)}, bf16[64,1024]{1,0:T(8,128)(2,1)S(1)}, u32[]{:S(2)}, u32[]{:S(2)}) collective-permute-start(bf16[64,1024]{1,0:T(8,128)(2,1)S(1)} %get-tuple-element.24), channel_id=1, source_target_pairs={{0,8},{8,0},{16,24},{24,16},{1,9},{9,1},{17,25},{25,17},{2,10},{10... | collective-permute-start | bytes 393224 | tf_op jit(solution)/shard_map/ppermute | solution.py:15
  53.7 0.6 collective-permute-done.18
  54.4 2.3 %collective-permute-done.12 = bf16[64,512]{1,0:T(8,128)(2,1)S(1)} collective-permute-done((bf16[64,512]{1,0:T(8,128)(2,1)S(1)}, bf16[64,512]{1,0:T(8,128)(2,1)S(1)}, u32[]{:S(2)}, u32[]{:S(2)}) %collective-permute-start.12) | collective-permute-done | bytes 65568 | tf_op jit(solution)/shard_map/ppermute | solution.py:15
  56.8 4.5 %collective-permute-done.13 = bf16[64,512]{1,0:T(8,128)(2,1)S(1)} collective-permute-done((bf16[64,512]{1,0:T(8,128)(2,1)S(1)}, bf16[64,512]{1,0:T(8,128)(2,1)S(1)}, u32[]{:S(2)}, u32[]{:S(2)}) %collective-permute-start.13) | collective-permute-done | bytes 65568 | tf_op jit(solution)/shard_map/ppermute | solution.py:15
  61.4 0.7 collective-permute-start.14
  62.1 0.8 convolution_add_fusion
  63.0 1.6 %collective-permute-done.14 = bf16[64,512]{1,0:T(8,128)(2,1)S(1)} collective-permute-done((bf16[64,512]{1,0:T(8,128)(2,1)S(1)}, bf16[64,512]{1,0:T(8,128)(2,1)S(1)}, u32[]{:S(2)}, u32[]{:S(2)}) %collective-permute-start.14) | collective-permute-done | bytes 65568 | tf_op jit(solution)/shard_map/ppermute | solution.py:15
  64.9 6.6 %collective-permute-start.19 = (f32[64,512]{1,0:T(8,128)S(1)}, f32[64,512]{1,0:T(8,128)S(1)}, u32[]{:S(2)}, u32[]{:S(2)}) collective-permute-start(f32[64,512]{1,0:T(8,128)S(1)} %convolution_add_fusion.1), channel_id=1, source_target_pairs={{0,8},{8,0},{16,24},{24,16},{1,9},{9,1},{17,25},{25,17},{2,10},{10... | collective-permute-start | bytes 393224 | tf_op jit(solution)/shard_map/ppermute | solution.py:15
  71.5 1.0 collective-permute-done.19
  72.6 2.3 %collective-permute-start.25 = (f32[64,512]{1,0:T(8,128)S(1)}, f32[64,512]{1,0:T(8,128)S(1)}, u32[]{:S(2)}, u32[]{:S(2)}) collective-permute-start(f32[64,512]{1,0:T(8,128)S(1)} %convolution_add_fusion), channel_id=1, source_target_pairs={{8,0},{16,8},{24,16},{9,1},{17,9},{25,17},{10,2},{18,10},{26,18},{... | collective-permute-start | bytes 393224 | tf_op jit(solution)/shard_map/ppermute | solution.py:101
  74.8 0.8 collective-permute-done.20
  76.4 1.0 collective-permute-start.26
  77.3 1.9 %collective-permute-done.21 = bf16[64,512]{1,0:T(8,128)(2,1)S(1)} collective-permute-done((bf16[64,512]{1,0:T(8,128)(2,1)S(1)}, bf16[64,512]{1,0:T(8,128)(2,1)S(1)}, u32[]{:S(2)}, u32[]{:S(2)}) %collective-permute-start.21) | collective-permute-done | bytes 65568 | tf_op jit(solution)/shard_map/ppermute | solution.py:15
  79.3 1.5 %collective-permute-done.26 = bf16[64,1024]{1,0:T(8,128)(2,1)S(1)} collective-permute-done((bf16[64,1024]{1,0:T(8,128)(2,1)S(1)}, bf16[64,1024]{1,0:T(8,128)(2,1)S(1)}, u32[]{:S(2)}, u32[]{:S(2)}) %collective-permute-start.26) | collective-permute-done | bytes 131104 | tf_op jit(solution)/shard_map/ppermute | solution.py:15
  80.8 2.5 %collective-permute-start.28 = (bf16[64,1024]{1,0:T(8,128)(2,1)S(1)}, bf16[64,1024]{1,0:T(8,128)(2,1)S(1)}, u32[]{:S(2)}, u32[]{:S(2)}) collective-permute-start(bf16[64,1024]{1,0:T(8,128)(2,1)S(1)} %get-tuple-element.18), channel_id=1, source_target_pairs={{0,8},{8,0},{16,24},{24,16},{1,9},{9,1},{17,25},{25,17},{2,10},{10... | collective-permute-start | bytes 393224 | tf_op jit(solution)/shard_map/ppermute | solution.py:15
  83.5 0.8 collective-permute-done.28
  84.3 3.9 %collective-permute-done.23 = bf16[64,512]{1,0:T(8,128)(2,1)S(1)} collective-permute-done((bf16[64,512]{1,0:T(8,128)(2,1)S(1)}, bf16[64,512]{1,0:T(8,128)(2,1)S(1)}, u32[]{:S(2)}, u32[]{:S(2)}) %collective-permute-start.23) | collective-permute-done | bytes 65568 | tf_op jit(solution)/shard_map/ppermute | solution.py:15
  88.3 0.9 collective-permute-start.24
  89.2 0.4 collective-permute-start.30
  89.7 1.4 %collective-permute-start.31 = (bf16[64,512]{1,0:T(8,128)(2,1)S(1)}, bf16[64,512]{1,0:T(8,128)(2,1)S(1)}, u32[]{:S(2)}, u32[]{:S(2)}) collective-permute-start(bf16[64,512]{1,0:T(8,128)(2,1)S(1)} %fusion.36), channel_id=1, source_target_pairs={{0,16},{8,24},{16,0},{24,8},{1,17},{9,25},{17,1},{25,9},{2,18},{10... | collective-permute-start | bytes 196616 | tf_op jit(solution)/shard_map/ppermute | solution.py:15
  91.5 1.9 %collective-permute-done.30 = bf16[64,512]{1,0:T(8,128)(2,1)S(1)} collective-permute-done((bf16[64,512]{1,0:T(8,128)(2,1)S(1)}, bf16[64,512]{1,0:T(8,128)(2,1)S(1)}, u32[]{:S(2)}, u32[]{:S(2)}) %collective-permute-start.30) | collective-permute-done | bytes 65568 | tf_op jit(solution)/shard_map/ppermute | solution.py:22
  93.6 5.2 %collective-permute-start.33 = (bf16[64,1024]{1,0:T(8,128)(2,1)S(1)}, bf16[64,1024]{1,0:T(8,128)(2,1)S(1)}, u32[]{:S(2)}, u32[]{:S(2)}) collective-permute-start(bf16[64,1024]{1,0:T(8,128)(2,1)S(1)} %get-tuple-element.12), channel_id=1, source_target_pairs={{0,8},{8,0},{16,24},{24,16},{1,9},{9,1},{17,25},{25,17},{2,10},{10... | collective-permute-start | bytes 393224 | tf_op jit(solution)/shard_map/ppermute | solution.py:15
  98.8 0.8 fusion.7
  99.7 1.9 %collective-permute-start.29 = (f32[64,512]{1,0:T(8,128)S(1)}, f32[64,512]{1,0:T(8,128)S(1)}, u32[]{:S(2)}, u32[]{:S(2)}) collective-permute-start(f32[64,512]{1,0:T(8,128)S(1)} %add.93), channel_id=1, source_target_pairs={{8,0},{16,8},{24,16},{9,1},{17,9},{25,17},{10,2},{18,10},{26,18},{... | collective-permute-start | bytes 393224 | tf_op jit(solution)/shard_map/ppermute | solution.py:101
  101.7 0.8 pad_maximum_fusion
  102.5 0.5 collective-permute-done.32
  103.0 0.8 fusion.15
  103.9 2.1 %collective-permute-done.29 = f32[64,512]{1,0:T(8,128)S(1)} collective-permute-done((f32[64,512]{1,0:T(8,128)S(1)}, f32[64,512]{1,0:T(8,128)S(1)}, u32[]{:S(2)}, u32[]{:S(2)}) %collective-permute-start.29) | collective-permute-done | bytes 131104 | tf_op jit(solution)/shard_map/ppermute | solution.py:101
  106.0 0.7 add_bitcast_fusion
  (78 shorter events, 5.3 us)
Async XLA Ops:
  0.6 6.7 %copy-start = (bf16[512,1024]{1,0:T(8,128)(2,1)S(1)}, bf16[512,1024]{1,0:T(8,128)(2,1)}, u32[]{:S(2)}) copy-start(bf16[512,1024]{1,0:T(8,128)(2,1)} %param.9) | copy-start | bytes 3145732
  2.4 1.6 %collective-permute-start = (bf16[64,512]{1,0:T(8,128)(2,1)S(1)}, bf16[64,512]{1,0:T(8,128)(2,1)S(1)}, u32[]{:S(2)}, u32[]{:S(2)}) collective-permute-start(bf16[64,512]{1,0:T(8,128)(2,1)S(1)} %fusion.25), channel_id=1, source_target_pairs={{0,8},{8,0},{16,24},{24,16},{1,9},{9,1},{17,25},{25,17},{2,10},{10... | collective-permute-start | bytes 196616 | tf_op jit(solution)/shard_map/ppermute | solution.py:15
  4.1 3.2 %collective-permute-start.1 = (bf16[64,512]{1,0:T(8,128)(2,1)S(1)}, bf16[64,512]{1,0:T(8,128)(2,1)S(1)}, u32[]{:S(2)}, u32[]{:S(2)}) collective-permute-start(bf16[64,512]{1,0:T(8,128)(2,1)S(1)} %add.72), channel_id=1, source_target_pairs={{0,16},{8,24},{16,0},{24,8},{1,17},{9,25},{17,1},{25,9},{2,18},{10... | collective-permute-start | bytes 196616 | tf_op jit(solution)/shard_map/ppermute | solution.py:15
  5.4 11.2 %copy-start.4 = (f32[1024]{0:T(1024)S(1)}, f32[1024]{0:T(1024)}, u32[]{:S(2)}) copy-start(f32[1024]{0:T(1024)} %param.8) | copy-start | bytes 12292
  7.6 5.6 %collective-permute-start.2 = (bf16[64,512]{1,0:T(8,128)(2,1)S(1)}, bf16[64,512]{1,0:T(8,128)(2,1)S(1)}, u32[]{:S(2)}, u32[]{:S(2)}) collective-permute-start(bf16[64,512]{1,0:T(8,128)(2,1)S(1)} %select_convert_fusion.2), channel_id=1, source_target_pairs={{0,1},{1,0},{2,3},{3,2},{4,5},{5,4},{6,7},{7,6},{8,9},{9,8},{10,11... | collective-permute-start | bytes 196616 | tf_op jit(solution)/shard_map/ppermute | solution.py:15
  12.5 11.3 %collective-permute-start.8 = (bf16[1024,512]{1,0:T(8,128)(2,1)}, bf16[1024,512]{1,0:T(8,128)(2,1)S(1)}, u32[]{:S(2)}, u32[]{:S(2)}) collective-permute-start(bf16[1024,512]{1,0:T(8,128)(2,1)} %get-tuple-element.6), channel_id=1, source_target_pairs={{0,24},{1,25},{2,26},{3,27},{4,28},{5,29},{6,30},{7,31}} | collective-permute-start | bytes 3145736 | tf_op jit(solution)/shard_map/ppermute | solution.py:93
  13.3 3.2 %collective-permute-start.3 = (bf16[64,512]{1,0:T(8,128)(2,1)S(1)}, bf16[64,512]{1,0:T(8,128)(2,1)S(1)}, u32[]{:S(2)}, u32[]{:S(2)}) collective-permute-start(bf16[64,512]{1,0:T(8,128)(2,1)S(1)} %add_convert_fusion.5), channel_id=1, source_target_pairs={{0,2},{1,3},{2,0},{3,1},{4,6},{5,7},{6,4},{7,5},{8,10},{9,11},{10,... | collective-permute-start | bytes 196616 | tf_op jit(solution)/shard_map/ppermute | solution.py:15
  13.5 11.9 %collective-permute-start.6 = (bf16[1024,512]{1,0:T(8,128)(2,1)}, bf16[1024,512]{1,0:T(8,128)(2,1)S(1)}, u32[]{:S(2)}, u32[]{:S(2)}) collective-permute-start(bf16[1024,512]{1,0:T(8,128)(2,1)} %get-tuple-element.8), channel_id=1, source_target_pairs={{0,8},{1,9},{2,10},{3,11},{4,12},{5,13},{6,14},{7,15}} | collective-permute-start | bytes 3145736 | tf_op jit(solution)/shard_map/ppermute | solution.py:93
  14.8 10.4 %collective-permute-start.7 = (bf16[1024,512]{1,0:T(8,128)(2,1)}, bf16[1024,512]{1,0:T(8,128)(2,1)}, u32[]{:S(2)}, u32[]{:S(2)}) collective-permute-start(bf16[1024,512]{1,0:T(8,128)(2,1)} %get-tuple-element.7), channel_id=1, source_target_pairs={{0,16},{1,17},{2,18},{3,19},{4,20},{5,21},{6,22},{7,23}} | collective-permute-start | bytes 3145736 | tf_op jit(solution)/shard_map/ppermute | solution.py:93
  16.5 4.1 %collective-permute-start.4 = (bf16[64,512]{1,0:T(8,128)(2,1)S(1)}, bf16[64,512]{1,0:T(8,128)(2,1)S(1)}, u32[]{:S(2)}, u32[]{:S(2)}) collective-permute-start(bf16[64,512]{1,0:T(8,128)(2,1)S(1)} %add_convert_fusion.4), channel_id=1, source_target_pairs={{0,4},{1,5},{2,6},{3,7},{4,0},{5,1},{6,2},{7,3},{8,12},{9,13},{10,... | collective-permute-start | bytes 196616 | tf_op jit(solution)/shard_map/ppermute | solution.py:15
  20.6 3.2 %collective-permute-start.5 = (bf16[64,512]{1,0:T(8,128)(2,1)S(1)}, bf16[64,512]{1,0:T(8,128)(2,1)S(1)}, u32[]{:S(2)}, u32[]{:S(2)}) collective-permute-start(bf16[64,512]{1,0:T(8,128)(2,1)S(1)} %fusion.38), channel_id=1, source_target_pairs={{0,1},{1,0},{2,3},{3,2},{4,5},{5,4},{6,7},{7,6},{8,9},{9,8},{10,11... | collective-permute-start | bytes 196616 | tf_op jit(solution)/shard_map/ppermute | solution.py:15
  23.8 1.7 %copy-start.3 = (f32[1,64,512]{2,1,0:T(8,128)S(1)}, f32[1,64,512]{2,1,0:T(8,128)}, u32[]{:S(2)}) copy-start(f32[1,64,512]{2,1,0:T(8,128)} %param.11) | copy-start | bytes 393220
  25.2 23.1 %copy-start.2 = (bf16[64,512]{1,0:T(8,128)(2,1)S(1)}, bf16[64,512]{1,0:T(8,128)(2,1)}, u32[]{:S(2)}) copy-start(bf16[64,512]{1,0:T(8,128)(2,1)} %param.6) | copy-start | bytes 196612
  25.8 16.7 %collective-permute-start.9 = (f32[64,512]{1,0:T(8,128)S(1)}, f32[64,512]{1,0:T(8,128)S(1)}, u32[]{:S(2)}, u32[]{:S(2)}) collective-permute-start(f32[64,512]{1,0:T(8,128)S(1)} %convolution_add_fusion.2), channel_id=1, source_target_pairs={{0,8},{8,0},{16,24},{24,16},{1,9},{9,1},{17,25},{25,17},{2,10},{10... | collective-permute-start | bytes 393224 | tf_op jit(solution)/shard_map/ppermute | solution.py:15
  40.5 21.6 %collective-permute-start.15 = (f32[64,512]{1,0:T(8,128)S(1)}, f32[64,512]{1,0:T(8,128)S(1)}, u32[]{:S(2)}, u32[]{:S(2)}) collective-permute-start(f32[64,512]{1,0:T(8,128)S(1)} %bitcast.26), channel_id=1, source_target_pairs={{8,0},{16,8},{24,16},{9,1},{17,9},{25,17},{10,2},{18,10},{26,18},{... | collective-permute-start | bytes 393224 | tf_op jit(solution)/shard_map/ppermute | solution.py:101
  42.4 19.7 %copy-start.1 = (bf16[1,4096,512]{2,1,0:T(8,128)(2,1)S(1)}, bf16[1,4096,512]{2,1,0:T(8,128)(2,1)}, u32[]{:S(2)}) copy-start(bf16[1,4096,512]{2,1,0:T(8,128)(2,1)} %param.10) | copy-start | bytes 12582916
  42.5 5.8 %collective-permute-start.10 = (bf16[64,512]{1,0:T(8,128)(2,1)S(1)}, bf16[64,512]{1,0:T(8,128)(2,1)S(1)}, u32[]{:S(2)}, u32[]{:S(2)}) collective-permute-start(bf16[64,512]{1,0:T(8,128)(2,1)S(1)} %get-tuple-element.4), channel_id=1, source_target_pairs={{0,16},{8,24},{16,0},{24,8},{1,17},{9,25},{17,1},{25,9},{2,18},{10... | collective-permute-start | bytes 196616 | tf_op jit(solution)/shard_map/ppermute | solution.py:15
  46.0 5.6 %collective-permute-start.16 = (bf16[64,1024]{1,0:T(8,128)(2,1)S(1)}, bf16[64,1024]{1,0:T(8,128)(2,1)S(1)}, u32[]{:S(2)}, u32[]{:S(2)}) collective-permute-start(bf16[64,1024]{1,0:T(8,128)(2,1)S(1)} %pad_maximum_fusion.1), channel_id=1, source_target_pairs={{0,16},{8,24},{16,0},{24,8},{1,17},{9,25},{17,1},{25,9},{2,18},{10... | collective-permute-start | bytes 393224 | tf_op jit(solution)/shard_map/ppermute | solution.py:15
  48.7 4.8 %collective-permute-start.11 = (bf16[64,512]{1,0:T(8,128)(2,1)S(1)}, bf16[64,512]{1,0:T(8,128)(2,1)S(1)}, u32[]{:S(2)}, u32[]{:S(2)}) collective-permute-start(bf16[64,512]{1,0:T(8,128)(2,1)S(1)} %select_convert_fusion.1), channel_id=1, source_target_pairs={{0,1},{1,0},{2,3},{3,2},{4,5},{5,4},{6,7},{7,6},{8,9},{9,8},{10,11... | collective-permute-start | bytes 196616 | tf_op jit(solution)/shard_map/ppermute | solution.py:15
  51.6 2.7 %collective-permute-start.18 = (bf16[64,1024]{1,0:T(8,128)(2,1)S(1)}, bf16[64,1024]{1,0:T(8,128)(2,1)S(1)}, u32[]{:S(2)}, u32[]{:S(2)}) collective-permute-start(bf16[64,1024]{1,0:T(8,128)(2,1)S(1)} %get-tuple-element.24), channel_id=1, source_target_pairs={{0,8},{8,0},{16,24},{24,16},{1,9},{9,1},{17,25},{25,17},{2,10},{10... | collective-permute-start | bytes 393224 | tf_op jit(solution)/shard_map/ppermute | solution.py:15
  53.4 3.4 %collective-permute-start.17 = (bf16[64,1024]{1,0:T(8,128)(2,1)S(1)}, bf16[64,1024]{1,0:T(8,128)(2,1)S(1)}, u32[]{:S(2)}, u32[]{:S(2)}) collective-permute-start(bf16[64,1024]{1,0:T(8,128)(2,1)S(1)} %get-tuple-element.23), channel_id=1, source_target_pairs={{0,8},{8,0},{16,24},{24,16},{1,9},{9,1},{17,25},{25,17},{2,10},{10... | collective-permute-start | bytes 393224 | tf_op jit(solution)/shard_map/ppermute | solution.py:15
  53.5 3.2 %collective-permute-start.12 = (bf16[64,512]{1,0:T(8,128)(2,1)S(1)}, bf16[64,512]{1,0:T(8,128)(2,1)S(1)}, u32[]{:S(2)}, u32[]{:S(2)}) collective-permute-start(bf16[64,512]{1,0:T(8,128)(2,1)S(1)} %add_convert_fusion.3), channel_id=1, source_target_pairs={{0,2},{1,3},{2,0},{3,1},{4,6},{5,7},{6,4},{7,5},{8,10},{9,11},{10,... | collective-permute-start | bytes 196616 | tf_op jit(solution)/shard_map/ppermute | solution.py:15
  56.7 4.7 %collective-permute-start.13 = (bf16[64,512]{1,0:T(8,128)(2,1)S(1)}, bf16[64,512]{1,0:T(8,128)(2,1)S(1)}, u32[]{:S(2)}, u32[]{:S(2)}) collective-permute-start(bf16[64,512]{1,0:T(8,128)(2,1)S(1)} %add_convert_fusion.2), channel_id=1, source_target_pairs={{0,4},{1,5},{2,6},{3,7},{4,0},{5,1},{6,2},{7,3},{8,12},{9,13},{10,... | collective-permute-start | bytes 196616 | tf_op jit(solution)/shard_map/ppermute | solution.py:15
  61.4 3.2 %collective-permute-start.14 = (bf16[64,512]{1,0:T(8,128)(2,1)S(1)}, bf16[64,512]{1,0:T(8,128)(2,1)S(1)}, u32[]{:S(2)}, u32[]{:S(2)}) collective-permute-start(bf16[64,512]{1,0:T(8,128)(2,1)S(1)} %fusion.37), channel_id=1, source_target_pairs={{0,1},{1,0},{2,3},{3,2},{4,5},{5,4},{6,7},{7,6},{8,9},{9,8},{10,11... | collective-permute-start | bytes 196616 | tf_op jit(solution)/shard_map/ppermute | solution.py:15
  64.9 7.6 %collective-permute-start.19 = (f32[64,512]{1,0:T(8,128)S(1)}, f32[64,512]{1,0:T(8,128)S(1)}, u32[]{:S(2)}, u32[]{:S(2)}) collective-permute-start(f32[64,512]{1,0:T(8,128)S(1)} %convolution_add_fusion.1), channel_id=1, source_target_pairs={{0,8},{8,0},{16,24},{24,16},{1,9},{9,1},{17,25},{25,17},{2,10},{10... | collective-permute-start | bytes 393224 | tf_op jit(solution)/shard_map/ppermute | solution.py:15
  72.5 3.2 %collective-permute-start.20 = (bf16[64,512]{1,0:T(8,128)(2,1)S(1)}, bf16[64,512]{1,0:T(8,128)(2,1)S(1)}, u32[]{:S(2)}, u32[]{:S(2)}) collective-permute-start(bf16[64,512]{1,0:T(8,128)(2,1)S(1)} %get-tuple-element.2), channel_id=1, source_target_pairs={{0,16},{8,24},{16,0},{24,8},{1,17},{9,25},{17,1},{25,9},{2,18},{10... | collective-permute-start | bytes 196616 | tf_op jit(solution)/shard_map/ppermute | solution.py:15
  72.6 27.1 %collective-permute-start.25 = (f32[64,512]{1,0:T(8,128)S(1)}, f32[64,512]{1,0:T(8,128)S(1)}, u32[]{:S(2)}, u32[]{:S(2)}) collective-permute-start(f32[64,512]{1,0:T(8,128)S(1)} %convolution_add_fusion), channel_id=1, source_target_pairs={{8,0},{16,8},{24,16},{9,1},{17,9},{25,17},{10,2},{18,10},{26,18},{... | collective-permute-start | bytes 393224 | tf_op jit(solution)/shard_map/ppermute | solution.py:101
  76.0 3.2 %collective-permute-start.21 = (bf16[64,512]{1,0:T(8,128)(2,1)S(1)}, bf16[64,512]{1,0:T(8,128)(2,1)S(1)}, u32[]{:S(2)}, u32[]{:S(2)}) collective-permute-start(bf16[64,512]{1,0:T(8,128)(2,1)S(1)} %select_convert_fusion), channel_id=1, source_target_pairs={{0,1},{1,0},{2,3},{3,2},{4,5},{5,4},{6,7},{7,6},{8,9},{9,8},{10,11... | collective-permute-start | bytes 196616 | tf_op jit(solution)/shard_map/ppermute | solution.py:15
  76.4 4.4 %collective-permute-start.26 = (bf16[64,1024]{1,0:T(8,128)(2,1)S(1)}, bf16[64,1024]{1,0:T(8,128)(2,1)S(1)}, u32[]{:S(2)}, u32[]{:S(2)}) collective-permute-start(bf16[64,1024]{1,0:T(8,128)(2,1)S(1)} %pad_maximum_fusion.2), channel_id=1, source_target_pairs={{0,16},{8,24},{16,0},{24,8},{1,17},{9,25},{17,1},{25,9},{2,18},{10... | collective-permute-start | bytes 393224 | tf_op jit(solution)/shard_map/ppermute | solution.py:15
  79.2 4.2 %collective-permute-start.22 = (bf16[64,512]{1,0:T(8,128)(2,1)S(1)}, bf16[64,512]{1,0:T(8,128)(2,1)S(1)}, u32[]{:S(2)}, u32[]{:S(2)}) collective-permute-start(bf16[64,512]{1,0:T(8,128)(2,1)S(1)} %add_convert_fusion.1), channel_id=1, source_target_pairs={{0,2},{1,3},{2,0},{3,1},{4,6},{5,7},{6,4},{7,5},{8,10},{9,11},{10,... | collective-permute-start | bytes 196616 | tf_op jit(solution)/shard_map/ppermute | solution.py:15
  80.8 3.5 %collective-permute-start.28 = (bf16[64,1024]{1,0:T(8,128)(2,1)S(1)}, bf16[64,1024]{1,0:T(8,128)(2,1)S(1)}, u32[]{:S(2)}, u32[]{:S(2)}) collective-permute-start(bf16[64,1024]{1,0:T(8,128)(2,1)S(1)} %get-tuple-element.18), channel_id=1, source_target_pairs={{0,8},{8,0},{16,24},{24,16},{1,9},{9,1},{17,25},{25,17},{2,10},{10... | collective-permute-start | bytes 393224 | tf_op jit(solution)/shard_map/ppermute | solution.py:15
  83.3 5.9 %collective-permute-start.27 = (bf16[64,1024]{1,0:T(8,128)(2,1)S(1)}, bf16[64,1024]{1,0:T(8,128)(2,1)S(1)}, u32[]{:S(2)}, u32[]{:S(2)}) collective-permute-start(bf16[64,1024]{1,0:T(8,128)(2,1)S(1)} %get-tuple-element.17), channel_id=1, source_target_pairs={{0,8},{8,0},{16,24},{24,16},{1,9},{9,1},{17,25},{25,17},{2,10},{10... | collective-permute-start | bytes 393224 | tf_op jit(solution)/shard_map/ppermute | solution.py:15
  83.4 4.8 %collective-permute-start.23 = (bf16[64,512]{1,0:T(8,128)(2,1)S(1)}, bf16[64,512]{1,0:T(8,128)(2,1)S(1)}, u32[]{:S(2)}, u32[]{:S(2)}) collective-permute-start(bf16[64,512]{1,0:T(8,128)(2,1)S(1)} %add_convert_fusion), channel_id=1, source_target_pairs={{0,4},{1,5},{2,6},{3,7},{4,0},{5,1},{6,2},{7,3},{8,12},{9,13},{10,... | collective-permute-start | bytes 196616 | tf_op jit(solution)/shard_map/ppermute | solution.py:15
  88.3 3.2 %collective-permute-start.24 = (bf16[64,512]{1,0:T(8,128)(2,1)S(1)}, bf16[64,512]{1,0:T(8,128)(2,1)S(1)}, u32[]{:S(2)}, u32[]{:S(2)}) collective-permute-start(bf16[64,512]{1,0:T(8,128)(2,1)S(1)} %fusion.36), channel_id=1, source_target_pairs={{0,1},{1,0},{2,3},{3,2},{4,5},{5,4},{6,7},{7,6},{8,9},{9,8},{10,11... | collective-permute-start | bytes 196616 | tf_op jit(solution)/shard_map/ppermute | solution.py:15
  89.2 4.2 %collective-permute-start.30 = (bf16[64,512]{1,0:T(8,128)(2,1)S(1)}, bf16[64,512]{1,0:T(8,128)(2,1)S(1)}, u32[]{:S(2)}, u32[]{:S(2)}) collective-permute-start(bf16[64,512]{1,0:T(8,128)(2,1)S(1)} %fusion.36), channel_id=1, source_target_pairs={{0,17},{1,16},{2,19},{3,18},{4,21},{5,20},{6,23},{7,22},{8,25},{9,... | collective-permute-start | bytes 196616 | tf_op jit(solution)/shard_map/ppermute | solution.py:22
  89.7 3.8 %collective-permute-start.31 = (bf16[64,512]{1,0:T(8,128)(2,1)S(1)}, bf16[64,512]{1,0:T(8,128)(2,1)S(1)}, u32[]{:S(2)}, u32[]{:S(2)}) collective-permute-start(bf16[64,512]{1,0:T(8,128)(2,1)S(1)} %fusion.36), channel_id=1, source_target_pairs={{0,16},{8,24},{16,0},{24,8},{1,17},{9,25},{17,1},{25,9},{2,18},{10... | collective-permute-start | bytes 196616 | tf_op jit(solution)/shard_map/ppermute | solution.py:15
  93.6 8.9 %collective-permute-start.33 = (bf16[64,1024]{1,0:T(8,128)(2,1)S(1)}, bf16[64,1024]{1,0:T(8,128)(2,1)S(1)}, u32[]{:S(2)}, u32[]{:S(2)}) collective-permute-start(bf16[64,1024]{1,0:T(8,128)(2,1)S(1)} %get-tuple-element.12), channel_id=1, source_target_pairs={{0,8},{8,0},{16,24},{24,16},{1,9},{9,1},{17,25},{25,17},{2,10},{10... | collective-permute-start | bytes 393224 | tf_op jit(solution)/shard_map/ppermute | solution.py:15
  99.7 6.3 %collective-permute-start.29 = (f32[64,512]{1,0:T(8,128)S(1)}, f32[64,512]{1,0:T(8,128)S(1)}, u32[]{:S(2)}, u32[]{:S(2)}) collective-permute-start(f32[64,512]{1,0:T(8,128)S(1)} %add.93), channel_id=1, source_target_pairs={{8,0},{16,8},{24,16},{9,1},{17,9},{25,17},{10,2},{18,10},{26,18},{... | collective-permute-start | bytes 393224 | tf_op jit(solution)/shard_map/ppermute | solution.py:101
  101.6 1.4 %collective-permute-start.32 = (bf16[64,1024]{1,0:T(8,128)(2,1)S(1)}, bf16[64,1024]{1,0:T(8,128)(2,1)S(1)}, u32[]{:S(2)}, u32[]{:S(2)}) collective-permute-start(bf16[64,1024]{1,0:T(8,128)(2,1)S(1)} %get-tuple-element.11), channel_id=1, source_target_pairs={{0,8},{8,0},{16,24},{24,16},{1,9},{9,1},{17,25},{25,17},{2,10},{10... | collective-permute-start | bytes 393224 | tf_op jit(solution)/shard_map/ppermute | solution.py:15
where the time goes:
time: 107 us
  starting transfers between devices  54 us (50%)
  waiting for transfers between devices  38.3 us (36%)
  other arithmetic  5.61 us (5%)
  matrix products  4.07 us (4%)
  local copies, waits for them, and re-layouts  3.62 us (3%)
    ppermute x27, starting transfers between devices, swapped(): lax.ppermute(value, axis, [(i, i ^ bit) for i in range(lax.axis_size(axis...  43.8 us
    ppermute x27, waiting for transfers between devices, swapped(): lax.ppermute(value, axis, [(i, i ^ bit) for i in range(lax.axis_size(axis...  34.3 us
    ppermute x3, starting transfers between devices, steps(): passed = lax.ppermute(future, 'delay', [(i, i - 1) for i in range(1, lags)])  6.12 us
    ppermute x3, starting transfers between devices, steps(): sent = lax.ppermute(rows, 'delay', [(0, k)])  3.65 us
    slice x1, local copies, waits for them, and re-layouts, steps(): rows = after(matrix, first_residual[:8, :k])[k * chunk:(k + 1) * chunk]  3.59 us
    dot_general x3, matrix products, steps(): contribution = jnp.dot(gathered, matrix, preferred_element_type=jnp.float32)  2.5 us
  transfers between devices with their start and end apart: 34, of which 21 were waited for; matrix products, arithmetic and copies ran while one was open for 9% of the time, Pallas kernels for 0%

commit v1 on v0

--- a/solution.py
+++ b/solution.py
@@ -1,6 +1,8 @@
 import jax
 import jax.numpy as jnp
 from jax import lax
+from jax.experimental import pallas as pl
+from jax.experimental.pallas import tpu as pltpu
 from jax.sharding import PartitionSpec as P
 
 
@@ -60,8 +62,28 @@
     return jnp.concatenate(parts, axis=1)
 
 
-def after(value, token):
-    return lax.optimization_barrier((value, token))[0]
+def cut_in_rows(matrix, chunk, count):
+    def copy_rows(rows, *rest):
+        copied, done = rest[:-1], rest[-1]
+        copies = [
+            pltpu.make_async_copy(rows.at[pl.ds(k * chunk, chunk)], copied[k - 1], done.at[k - 1])
+            for k in range(1, count)
+        ]
+        for copy in copies:
+            copy.start()
+        for copy in copies:
+            copy.wait()
+
+    shape = jax.ShapeDtypeStruct((chunk, matrix.shape[1]), matrix.dtype)
+    return pl.pallas_call(
+        copy_rows,
+        in_specs=[pl.BlockSpec(memory_space=pl.ANY)],
+        out_specs=[pl.BlockSpec(memory_space=pl.ANY)] * (count - 1),
+        out_shape=[shape] * (count - 1),
+        scratch_shapes=[pltpu.SemaphoreType.DMA((count - 1,))],
+        compiler_params=pltpu.CompilerParams(vmem_limit_bytes=1 << 20),
+        name="cut_rows",
+    )(matrix)
 
 
 def steps(incident, onset, beta, inverse_block, delay_blocks, history_sum):
@@ -84,14 +106,15 @@
         drives.append(incident_wide * envelope[:, None])
 
     residual = jnp.where(place == 0, drives[0] - future, 0.0).astype(jnp.bfloat16)
-    first_residual = residual
     residual = total_over_delay(residual, [jnp.bfloat16] * len(wires))
 
+    dealt = {}
+    cut = cut_in_rows(matrix, chunk, lags)
+    for k in range(1, lags):
+        dealt[k] = lax.ppermute(cut[k - 1], "delay", [(0, k)])
     first_rows = matrix[:chunk]
-    for k in reversed(range(1, lags)):
-        rows = after(matrix, first_residual[:8, :k])[k * chunk : (k + 1) * chunk]
-        sent = lax.ppermute(rows, "delay", [(0, k)])
-        first_rows = lax.optimization_barrier(jnp.where(place == k, sent, first_rows))
+    for k in [1] + list(reversed(range(2, lags))):
+        first_rows = lax.optimization_barrier(jnp.where(place == k, dealt[k], first_rows))
 
     outputs = []
     for step_index in range(STEPS):

time: 107 us -> 111 us (1.037)
  the two profiles are of different devices: /device:TPU:25 before, /device:TPU:1 now
where the time goes in v1:
time: 111 us
  starting transfers between devices  63.6 us (57%)
  waiting for transfers between devices  33.2 us (30%)
  other arithmetic  5.94 us (5%)
  matrix products  4.07 us (4%)
  local copies, waits for them, and re-layouts  2.22 us (2%)
    ppermute x27, starting transfers between devices, swapped(): lax.ppermute(value, axis, [(i, i ^ bit) for i in range(lax.axis_size(axis...  52.2 us
    ppermute x27, waiting for transfers between devices, swapped(): lax.ppermute(value, axis, [(i, i ^ bit) for i in range(lax.axis_size(axis...  29.5 us
    ppermute x3, starting transfers between devices, steps(): passed = lax.ppermute(future, 'delay', [(i, i - 1) for i in range(1, lags)])  6.12 us
    ppermute x3, starting transfers between devices, steps(): dealt[k] = lax.ppermute(cut[k - 1], 'delay', [(0, k)])  4.59 us
    dot_general x3, matrix products, steps(): contribution = jnp.dot(gathered, matrix, preferred_element_type=jnp.float32)  2.5 us
    unnamed x12, local copies, waits for them, and re-layouts  2.22 us
  transfers between devices with their start and end apart: 34, of which 20 were waited for; matrix products, arithmetic and copies ran while one was open for 6% of the time, Pallas kernels for 1%

profile of v1, /device:TPU:1, one launch (start us, length us, event | category | flops | bytes accessed | tf_op | source)
XLA Modules:
  0.0 111.2 jit_solution(707033686272429463)
XLA Ops:
  0.7 0.8 compare_select_fusion
  1.4 1.0 fusion.25
  2.5 1.2 %collective-permute-done = bf16[64,512]{1,0:T(8,128)(2,1)S(1)} collective-permute-done((bf16[64,512]{1,0:T(8,128)(2,1)S(1)}, bf16[64,512]{1,0:T(8,128)(2,1)S(1)}, u32[]{:S(2)}, u32[]{:S(2)}) %collective-permute-start) | collective-permute-done | bytes 65568 | tf_op jit(solution)/shard_map/ppermute | solution.py:17
  3.8 2.4 %collective-permute-start.1 = (bf16[64,512]{1,0:T(8,128)(2,1)S(1)}, bf16[64,512]{1,0:T(8,128)(2,1)S(1)}, u32[]{:S(2)}, u32[]{:S(2)}) collective-permute-start(bf16[64,512]{1,0:T(8,128)(2,1)S(1)} %add.72), channel_id=1, source_target_pairs={{0,16},{8,24},{16,0},{24,8},{1,17},{9,25},{17,1},{25,9},{2,18},{10... | collective-permute-start | bytes 196616 | tf_op jit(solution)/shard_map/ppermute | solution.py:17
  6.2 2.1 %collective-permute-done.1 = bf16[64,512]{1,0:T(8,128)(2,1)S(1)} collective-permute-done((bf16[64,512]{1,0:T(8,128)(2,1)S(1)}, bf16[64,512]{1,0:T(8,128)(2,1)S(1)}, u32[]{:S(2)}, u32[]{:S(2)}) %collective-permute-start.1) | collective-permute-done | bytes 65568 | tf_op jit(solution)/shard_map/ppermute | solution.py:17
  8.7 1.0 collective-permute-start.2
  9.7 2.2 %copy-done.1 = bf16[1,4096,512]{2,1,0:T(8,128)(2,1)S(1)} copy-done((bf16[1,4096,512]{2,1,0:T(8,128)(2,1)S(1)}, bf16[1,4096,512]{2,1,0:T(8,128)(2,1)}, u32[]{:S(2)}) %copy-start.1) | copy-done | bytes 4194328
  11.9 1.0 cut_rows.1
  12.9 1.3 %collective-permute-start.8 = (bf16[1024,512]{1,0:T(8,128)(2,1)}, bf16[1024,512]{1,0:T(8,128)(2,1)}, u32[]{:S(2)}, u32[]{:S(2)}) collective-permute-start(bf16[1024,512]{1,0:T(8,128)(2,1)} %get-tuple-element.7), channel_id=1, source_target_pairs={{0,8},{1,9},{2,10},{3,11},{4,12},{5,13},{6,14},{7,15}} | collective-permute-start | bytes 3145736 | tf_op jit(solution)/shard_map/ppermute | solution.py:114
  14.3 1.4 %collective-permute-start.3 = (bf16[64,512]{1,0:T(8,128)(2,1)S(1)}, bf16[64,512]{1,0:T(8,128)(2,1)S(1)}, u32[]{:S(2)}, u32[]{:S(2)}) collective-permute-start(bf16[64,512]{1,0:T(8,128)(2,1)S(1)} %add_convert_fusion.5), channel_id=1, source_target_pairs={{0,2},{1,3},{2,0},{3,1},{4,6},{5,7},{6,4},{7,5},{8,10},{9,11},{10,... | collective-permute-start | bytes 196616 | tf_op jit(solution)/shard_map/ppermute | solution.py:17
  15.6 1.7 %collective-permute-start.6 = (bf16[1024,512]{1,0:T(8,128)(2,1)S(1)}, bf16[1024,512]{1,0:T(8,128)(2,1)}, u32[]{:S(2)}, u32[]{:S(2)}) collective-permute-start(bf16[1024,512]{1,0:T(8,128)(2,1)S(1)} %get-tuple-element.5), channel_id=1, source_target_pairs={{0,16},{1,17},{2,18},{3,19},{4,20},{5,21},{6,22},{7,23}} | collective-permute-start | bytes 3145736 | tf_op jit(solution)/shard_map/ppermute | solution.py:114
  17.3 1.6 %collective-permute-start.7 = (bf16[1024,512]{1,0:T(8,128)(2,1)S(1)}, bf16[1024,512]{1,0:T(8,128)(2,1)}, u32[]{:S(2)}, u32[]{:S(2)}) collective-permute-start(bf16[1024,512]{1,0:T(8,128)(2,1)S(1)} %get-tuple-element.6), channel_id=1, source_target_pairs={{0,24},{1,25},{2,26},{3,27},{4,28},{5,29},{6,30},{7,31}} | collective-permute-start | bytes 3145736 | tf_op jit(solution)/shard_map/ppermute | solution.py:114
  19.0 2.4 %collective-permute-start.4 = (bf16[64,512]{1,0:T(8,128)(2,1)S(1)}, bf16[64,512]{1,0:T(8,128)(2,1)S(1)}, u32[]{:S(2)}, u32[]{:S(2)}) collective-permute-start(bf16[64,512]{1,0:T(8,128)(2,1)S(1)} %add_convert_fusion.4), channel_id=1, source_target_pairs={{0,4},{1,5},{2,6},{3,7},{4,0},{5,1},{6,2},{7,3},{8,12},{9,13},{10,... | collective-permute-start | bytes 196616 | tf_op jit(solution)/shard_map/ppermute | solution.py:17
  21.3 2.3 %collective-permute-done.4 = bf16[64,512]{1,0:T(8,128)(2,1)S(1)} collective-permute-done((bf16[64,512]{1,0:T(8,128)(2,1)S(1)}, bf16[64,512]{1,0:T(8,128)(2,1)S(1)}, u32[]{:S(2)}, u32[]{:S(2)}) %collective-permute-start.4) | collective-permute-done | bytes 65568 | tf_op jit(solution)/shard_map/ppermute | solution.py:17
  24.1 2.8 %collective-permute-done.5 = bf16[64,512]{1,0:T(8,128)(2,1)S(1)} collective-permute-done((bf16[64,512]{1,0:T(8,128)(2,1)S(1)}, bf16[64,512]{1,0:T(8,128)(2,1)S(1)}, u32[]{:S(2)}, u32[]{:S(2)}) %collective-permute-start.5) | collective-permute-done | bytes 65568 | tf_op jit(solution)/shard_map/ppermute | solution.py:17
  27.0 1.7 %bitcast_select_fusion = bf16[1024,512]{1,0:T(8,128)(2,1)S(1)} fusion(bf16[1024,512]{1,0:T(8,128)(2,1)} %collective-permute-done.8, bf16[1,4096,512]{2,1,0:T(8,128)(2,1)} %param.10, pred[]{:T(512)S(6)} %eq.24), kind=kLoop, calls=%fused_computation.3 | loop fusion | flops 524288 | bytes 3145729 | tf_op jit(solution)/shard_map/jit(_where)/select_n | solution.py:117
  29.3 16.4 %collective-permute-start.9 = (f32[64,512]{1,0:T(8,128)S(1)}, f32[64,512]{1,0:T(8,128)S(1)}, u32[]{:S(2)}, u32[]{:S(2)}) collective-permute-start(f32[64,512]{1,0:T(8,128)S(1)} %convolution_add_fusion.2), channel_id=1, source_target_pairs={{0,8},{8,0},{16,24},{24,16},{1,9},{9,1},{17,25},{25,17},{2,10},{10... | collective-permute-start | bytes 393224 | tf_op jit(solution)/shard_map/ppermute | solution.py:17
  45.6 1.9 %collective-permute-start.15 = (f32[64,512]{1,0:T(8,128)S(1)}, f32[64,512]{1,0:T(8,128)S(1)}, u32[]{:S(2)}, u32[]{:S(2)}) collective-permute-start(f32[64,512]{1,0:T(8,128)S(1)} %bitcast.26), channel_id=1, source_target_pairs={{8,0},{16,8},{24,16},{9,1},{17,9},{25,17},{10,2},{18,10},{26,18},{... | collective-permute-start | bytes 393224 | tf_op jit(solution)/shard_map/ppermute | solution.py:124
  47.6 3.4 %collective-permute-start.10 = (bf16[64,512]{1,0:T(8,128)(2,1)S(1)}, bf16[64,512]{1,0:T(8,128)(2,1)S(1)}, u32[]{:S(2)}, u32[]{:S(2)}) collective-permute-start(bf16[64,512]{1,0:T(8,128)(2,1)S(1)} %get-tuple-element.10), channel_id=1, source_target_pairs={{0,16},{8,24},{16,0},{24,8},{1,17},{9,25},{17,1},{25,9},{2,18},{10... | collective-permute-start | bytes 196616 | tf_op jit(solution)/shard_map/ppermute | solution.py:17
  51.1 2.2 %collective-permute-done.10 = bf16[64,512]{1,0:T(8,128)(2,1)S(1)} collective-permute-done((bf16[64,512]{1,0:T(8,128)(2,1)S(1)}, bf16[64,512]{1,0:T(8,128)(2,1)S(1)}, u32[]{:S(2)}, u32[]{:S(2)}) %collective-permute-start.10) | collective-permute-done | bytes 65568 | tf_op jit(solution)/shard_map/ppermute | solution.py:17
  54.0 2.6 %collective-permute-done.16 = bf16[64,1024]{1,0:T(8,128)(2,1)S(1)} collective-permute-done((bf16[64,1024]{1,0:T(8,128)(2,1)S(1)}, bf16[64,1024]{1,0:T(8,128)(2,1)S(1)}, u32[]{:S(2)}, u32[]{:S(2)}) %collective-permute-start.16) | collective-permute-done | bytes 131104 | tf_op jit(solution)/shard_map/ppermute | solution.py:17
  56.7 1.7 %collective-permute-start.18 = (bf16[64,1024]{1,0:T(8,128)(2,1)S(1)}, bf16[64,1024]{1,0:T(8,128)(2,1)S(1)}, u32[]{:S(2)}, u32[]{:S(2)}) collective-permute-start(bf16[64,1024]{1,0:T(8,128)(2,1)S(1)} %get-tuple-element.27), channel_id=1, source_target_pairs={{0,8},{8,0},{16,24},{24,16},{1,9},{9,1},{17,25},{25,17},{2,10},{10... | collective-permute-start | bytes 393224 | tf_op jit(solution)/shard_map/ppermute | solution.py:17
  59.4 2.3 %collective-permute-done.12 = bf16[64,512]{1,0:T(8,128)(2,1)S(1)} collective-permute-done((bf16[64,512]{1,0:T(8,128)(2,1)S(1)}, bf16[64,512]{1,0:T(8,128)(2,1)S(1)}, u32[]{:S(2)}, u32[]{:S(2)}) %collective-permute-start.12) | collective-permute-done | bytes 65568 | tf_op jit(solution)/shard_map/ppermute | solution.py:17
  61.7 2.4 %collective-permute-start.13 = (bf16[64,512]{1,0:T(8,128)(2,1)S(1)}, bf16[64,512]{1,0:T(8,128)(2,1)S(1)}, u32[]{:S(2)}, u32[]{:S(2)}) collective-permute-start(bf16[64,512]{1,0:T(8,128)(2,1)S(1)} %add_convert_fusion.2), channel_id=1, source_target_pairs={{0,4},{1,5},{2,6},{3,7},{4,0},{5,1},{6,2},{7,3},{8,12},{9,13},{10,... | collective-permute-start | bytes 196616 | tf_op jit(solution)/shard_map/ppermute | solution.py:17
  64.1 2.3 %collective-permute-done.13 = bf16[64,512]{1,0:T(8,128)(2,1)S(1)} collective-permute-done((bf16[64,512]{1,0:T(8,128)(2,1)S(1)}, bf16[64,512]{1,0:T(8,128)(2,1)S(1)}, u32[]{:S(2)}, u32[]{:S(2)}) %collective-permute-start.13) | collective-permute-done | bytes 65568 | tf_op jit(solution)/shard_map/ppermute | solution.py:17
  66.4 0.7 collective-permute-start.14
  67.1 0.8 convolution_add_fusion
  68.0 1.6 %collective-permute-done.14 = bf16[64,512]{1,0:T(8,128)(2,1)S(1)} collective-permute-done((bf16[64,512]{1,0:T(8,128)(2,1)S(1)}, bf16[64,512]{1,0:T(8,128)(2,1)S(1)}, u32[]{:S(2)}, u32[]{:S(2)}) %collective-permute-start.14) | collective-permute-done | bytes 65568 | tf_op jit(solution)/shard_map/ppermute | solution.py:17
  69.9 6.5 %collective-permute-start.19 = (f32[64,512]{1,0:T(8,128)S(1)}, f32[64,512]{1,0:T(8,128)S(1)}, u32[]{:S(2)}, u32[]{:S(2)}) collective-permute-start(f32[64,512]{1,0:T(8,128)S(1)} %convolution_add_fusion.1), channel_id=1, source_target_pairs={{0,8},{8,0},{16,24},{24,16},{1,9},{9,1},{17,25},{25,17},{2,10},{10... | collective-permute-start | bytes 393224 | tf_op jit(solution)/shard_map/ppermute | solution.py:17
  76.4 1.0 collective-permute-done.19
  77.5 2.3 %collective-permute-start.25 = (f32[64,512]{1,0:T(8,128)S(1)}, f32[64,512]{1,0:T(8,128)S(1)}, u32[]{:S(2)}, u32[]{:S(2)}) collective-permute-start(f32[64,512]{1,0:T(8,128)S(1)} %convolution_add_fusion), channel_id=1, source_target_pairs={{8,0},{16,8},{24,16},{9,1},{17,9},{25,17},{10,2},{18,10},{26,18},{... | collective-permute-start | bytes 393224 | tf_op jit(solution)/shard_map/ppermute | solution.py:124
  79.8 0.8 collective-permute-done.20
  81.3 1.0 collective-permute-start.26
  82.3 1.9 %collective-permute-done.21 = bf16[64,512]{1,0:T(8,128)(2,1)S(1)} collective-permute-done((bf16[64,512]{1,0:T(8,128)(2,1)S(1)}, bf16[64,512]{1,0:T(8,128)(2,1)S(1)}, u32[]{:S(2)}, u32[]{:S(2)}) %collective-permute-start.21) | collective-permute-done | bytes 65568 | tf_op jit(solution)/shard_map/ppermute | solution.py:17
  84.2 1.5 %collective-permute-done.26 = bf16[64,1024]{1,0:T(8,128)(2,1)S(1)} collective-permute-done((bf16[64,1024]{1,0:T(8,128)(2,1)S(1)}, bf16[64,1024]{1,0:T(8,128)(2,1)S(1)}, u32[]{:S(2)}, u32[]{:S(2)}) %collective-permute-start.26) | collective-permute-done | bytes 131104 | tf_op jit(solution)/shard_map/ppermute | solution.py:17
  85.8 2.5 %collective-permute-start.28 = (bf16[64,1024]{1,0:T(8,128)(2,1)S(1)}, bf16[64,1024]{1,0:T(8,128)(2,1)S(1)}, u32[]{:S(2)}, u32[]{:S(2)}) collective-permute-start(bf16[64,1024]{1,0:T(8,128)(2,1)S(1)} %get-tuple-element.21), channel_id=1, source_target_pairs={{0,8},{8,0},{16,24},{24,16},{1,9},{9,1},{17,25},{25,17},{2,10},{10... | collective-permute-start | bytes 393224 | tf_op jit(solution)/shard_map/ppermute | solution.py:17
  88.4 1.8 %collective-permute-start.23 = (bf16[64,512]{1,0:T(8,128)(2,1)S(1)}, bf16[64,512]{1,0:T(8,128)(2,1)S(1)}, u32[]{:S(2)}, u32[]{:S(2)}) collective-permute-start(bf16[64,512]{1,0:T(8,128)(2,1)S(1)} %add_convert_fusion), channel_id=1, source_target_pairs={{0,4},{1,5},{2,6},{3,7},{4,0},{5,1},{6,2},{7,3},{8,12},{9,13},{10,... | collective-permute-start | bytes 196616 | tf_op jit(solution)/shard_map/ppermute | solution.py:17
  90.2 3.0 %collective-permute-done.23 = bf16[64,512]{1,0:T(8,128)(2,1)S(1)} collective-permute-done((bf16[64,512]{1,0:T(8,128)(2,1)S(1)}, bf16[64,512]{1,0:T(8,128)(2,1)S(1)}, u32[]{:S(2)}, u32[]{:S(2)}) %collective-permute-start.23) | collective-permute-done | bytes 65568 | tf_op jit(solution)/shard_map/ppermute | solution.py:17
  93.8 0.7 collective-permute-start.30
  94.6 1.4 %collective-permute-start.31 = (bf16[64,512]{1,0:T(8,128)(2,1)S(1)}, bf16[64,512]{1,0:T(8,128)(2,1)S(1)}, u32[]{:S(2)}, u32[]{:S(2)}) collective-permute-start(bf16[64,512]{1,0:T(8,128)(2,1)S(1)} %fusion.36), channel_id=1, source_target_pairs={{0,16},{8,24},{16,0},{24,8},{1,17},{9,25},{17,1},{25,9},{2,18},{10... | collective-permute-start | bytes 196616 | tf_op jit(solution)/shard_map/ppermute | solution.py:17
  96.4 1.6 %collective-permute-done.30 = bf16[64,512]{1,0:T(8,128)(2,1)S(1)} collective-permute-done((bf16[64,512]{1,0:T(8,128)(2,1)S(1)}, bf16[64,512]{1,0:T(8,128)(2,1)S(1)}, u32[]{:S(2)}, u32[]{:S(2)}) %collective-permute-start.30) | collective-permute-done | bytes 65568 | tf_op jit(solution)/shard_map/ppermute | solution.py:24
  98.5 4.8 %collective-permute-start.33 = (bf16[64,1024]{1,0:T(8,128)(2,1)S(1)}, bf16[64,1024]{1,0:T(8,128)(2,1)S(1)}, u32[]{:S(2)}, u32[]{:S(2)}) collective-permute-start(bf16[64,1024]{1,0:T(8,128)(2,1)S(1)} %get-tuple-element.15), channel_id=1, source_target_pairs={{0,8},{8,0},{16,24},{24,16},{1,9},{9,1},{17,25},{25,17},{2,10},{10... | collective-permute-start | bytes 393224 | tf_op jit(solution)/shard_map/ppermute | solution.py:17
  103.3 0.8 fusion.7
  104.2 1.9 %collective-permute-start.29 = (f32[64,512]{1,0:T(8,128)S(1)}, f32[64,512]{1,0:T(8,128)S(1)}, u32[]{:S(2)}, u32[]{:S(2)}) collective-permute-start(f32[64,512]{1,0:T(8,128)S(1)} %add.93), channel_id=1, source_target_pairs={{8,0},{16,8},{24,16},{9,1},{17,9},{25,17},{10,2},{18,10},{26,18},{... | collective-permute-start | bytes 393224 | tf_op jit(solution)/shard_map/ppermute | solution.py:124
  106.2 0.8 pad_maximum_fusion
  107.6 0.8 fusion.15
  108.4 2.1 %collective-permute-done.29 = f32[64,512]{1,0:T(8,128)S(1)} collective-permute-done((f32[64,512]{1,0:T(8,128)S(1)}, f32[64,512]{1,0:T(8,128)S(1)}, u32[]{:S(2)}, u32[]{:S(2)}) %collective-permute-start.29) | collective-permute-done | bytes 131104 | tf_op jit(solution)/shard_map/ppermute | solution.py:124
  110.5 0.7 add_bitcast_fusion
  (80 shorter events, 7.0 us)
Async XLA Ops:
  0.6 7.7 %copy-start = (bf16[512,1024]{1,0:T(8,128)(2,1)S(1)}, bf16[512,1024]{1,0:T(8,128)(2,1)}, u32[]{:S(2)}) copy-start(bf16[512,1024]{1,0:T(8,128)(2,1)} %param.9) | copy-start | bytes 3145732
  0.6 20.7 %copy-start.5 = (f32[1024]{0:T(1024)S(1)}, f32[1024]{0:T(1024)}, u32[]{:S(2)}) copy-start(f32[1024]{0:T(1024)} %param.8) | copy-start | bytes 12292
  2.5 1.3 %collective-permute-start = (bf16[64,512]{1,0:T(8,128)(2,1)S(1)}, bf16[64,512]{1,0:T(8,128)(2,1)S(1)}, u32[]{:S(2)}, u32[]{:S(2)}) collective-permute-start(bf16[64,512]{1,0:T(8,128)(2,1)S(1)} %fusion.25), channel_id=1, source_target_pairs={{0,8},{8,0},{16,24},{24,16},{1,9},{9,1},{17,25},{25,17},{2,10},{10... | collective-permute-start | bytes 196616 | tf_op jit(solution)/shard_map/ppermute | solution.py:17
  3.8 4.6 %collective-permute-start.1 = (bf16[64,512]{1,0:T(8,128)(2,1)S(1)}, bf16[64,512]{1,0:T(8,128)(2,1)S(1)}, u32[]{:S(2)}, u32[]{:S(2)}) collective-permute-start(bf16[64,512]{1,0:T(8,128)(2,1)S(1)} %add.72), channel_id=1, source_target_pairs={{0,16},{8,24},{16,0},{24,8},{1,17},{9,25},{17,1},{25,9},{2,18},{10... | collective-permute-start | bytes 196616 | tf_op jit(solution)/shard_map/ppermute | solution.py:17
  8.7 5.5 %collective-permute-start.2 = (bf16[64,512]{1,0:T(8,128)(2,1)S(1)}, bf16[64,512]{1,0:T(8,128)(2,1)S(1)}, u32[]{:S(2)}, u32[]{:S(2)}) collective-permute-start(bf16[64,512]{1,0:T(8,128)(2,1)S(1)} %select_convert_fusion.2), channel_id=1, source_target_pairs={{0,1},{1,0},{2,3},{3,2},{4,5},{5,4},{6,7},{7,6},{8,9},{9,8},{10,11... | collective-permute-start | bytes 196616 | tf_op jit(solution)/shard_map/ppermute | solution.py:17
  9.7 2.2 %copy-start.1 = (bf16[1,4096,512]{2,1,0:T(8,128)(2,1)S(1)}, bf16[1,4096,512]{2,1,0:T(8,128)(2,1)}, u32[]{:S(2)}) copy-start(bf16[1,4096,512]{2,1,0:T(8,128)(2,1)} %param.10) | copy-start | bytes 12582916
  12.9 14.0 %collective-permute-start.8 = (bf16[1024,512]{1,0:T(8,128)(2,1)}, bf16[1024,512]{1,0:T(8,128)(2,1)}, u32[]{:S(2)}, u32[]{:S(2)}) collective-permute-start(bf16[1024,512]{1,0:T(8,128)(2,1)} %get-tuple-element.7), channel_id=1, source_target_pairs={{0,8},{1,9},{2,10},{3,11},{4,12},{5,13},{6,14},{7,15}} | collective-permute-start | bytes 3145736 | tf_op jit(solution)/shard_map/ppermute | solution.py:114
  14.3 4.7 %collective-permute-start.3 = (bf16[64,512]{1,0:T(8,128)(2,1)S(1)}, bf16[64,512]{1,0:T(8,128)(2,1)S(1)}, u32[]{:S(2)}, u32[]{:S(2)}) collective-permute-start(bf16[64,512]{1,0:T(8,128)(2,1)S(1)} %add_convert_fusion.5), channel_id=1, source_target_pairs={{0,2},{1,3},{2,0},{3,1},{4,6},{5,7},{6,4},{7,5},{8,10},{9,11},{10,... | collective-permute-start | bytes 196616 | tf_op jit(solution)/shard_map/ppermute | solution.py:17
  15.6 13.2 %collective-permute-start.6 = (bf16[1024,512]{1,0:T(8,128)(2,1)S(1)}, bf16[1024,512]{1,0:T(8,128)(2,1)}, u32[]{:S(2)}, u32[]{:S(2)}) collective-permute-start(bf16[1024,512]{1,0:T(8,128)(2,1)S(1)} %get-tuple-element.5), channel_id=1, source_target_pairs={{0,16},{1,17},{2,18},{3,19},{4,20},{5,21},{6,22},{7,23}} | collective-permute-start | bytes 3145736 | tf_op jit(solution)/shard_map/ppermute | solution.py:114
  17.3 11.4 %collective-permute-start.7 = (bf16[1024,512]{1,0:T(8,128)(2,1)S(1)}, bf16[1024,512]{1,0:T(8,128)(2,1)}, u32[]{:S(2)}, u32[]{:S(2)}) collective-permute-start(bf16[1024,512]{1,0:T(8,128)(2,1)S(1)} %get-tuple-element.6), channel_id=1, source_target_pairs={{0,24},{1,25},{2,26},{3,27},{4,28},{5,29},{6,30},{7,31}} | collective-permute-start | bytes 3145736 | tf_op jit(solution)/shard_map/ppermute | solution.py:114
  19.0 4.7 %collective-permute-start.4 = (bf16[64,512]{1,0:T(8,128)(2,1)S(1)}, bf16[64,512]{1,0:T(8,128)(2,1)S(1)}, u32[]{:S(2)}, u32[]{:S(2)}) collective-permute-start(bf16[64,512]{1,0:T(8,128)(2,1)S(1)} %add_convert_fusion.4), channel_id=1, source_target_pairs={{0,4},{1,5},{2,6},{3,7},{4,0},{5,1},{6,2},{7,3},{8,12},{9,13},{10,... | collective-permute-start | bytes 196616 | tf_op jit(solution)/shard_map/ppermute | solution.py:17
  23.7 3.2 %collective-permute-start.5 = (bf16[64,512]{1,0:T(8,128)(2,1)S(1)}, bf16[64,512]{1,0:T(8,128)(2,1)S(1)}, u32[]{:S(2)}, u32[]{:S(2)}) collective-permute-start(bf16[64,512]{1,0:T(8,128)(2,1)S(1)} %fusion.38), channel_id=1, source_target_pairs={{0,1},{1,0},{2,3},{3,2},{4,5},{5,4},{6,7},{7,6},{8,9},{9,8},{10,11... | collective-permute-start | bytes 196616 | tf_op jit(solution)/shard_map/ppermute | solution.py:17
  26.9 2.0 %copy-start.4 = (f32[1,64,512]{2,1,0:T(8,128)S(1)}, f32[1,64,512]{2,1,0:T(8,128)}, u32[]{:S(2)}) copy-start(f32[1,64,512]{2,1,0:T(8,128)} %param.11) | copy-start | bytes 393220
  28.7 24.7 %copy-start.3 = (bf16[64,512]{1,0:T(8,128)(2,1)S(1)}, bf16[64,512]{1,0:T(8,128)(2,1)}, u32[]{:S(2)}) copy-start(bf16[64,512]{1,0:T(8,128)(2,1)} %param.6) | copy-start | bytes 196612
  29.3 18.3 %collective-permute-start.9 = (f32[64,512]{1,0:T(8,128)S(1)}, f32[64,512]{1,0:T(8,128)S(1)}, u32[]{:S(2)}, u32[]{:S(2)}) collective-permute-start(f32[64,512]{1,0:T(8,128)S(1)} %convolution_add_fusion.2), channel_id=1, source_target_pairs={{0,8},{8,0},{16,24},{24,16},{1,9},{9,1},{17,25},{25,17},{2,10},{10... | collective-permute-start | bytes 393224 | tf_op jit(solution)/shard_map/ppermute | solution.py:17
  45.6 21.5 %collective-permute-start.15 = (f32[64,512]{1,0:T(8,128)S(1)}, f32[64,512]{1,0:T(8,128)S(1)}, u32[]{:S(2)}, u32[]{:S(2)}) collective-permute-start(f32[64,512]{1,0:T(8,128)S(1)} %bitcast.26), channel_id=1, source_target_pairs={{8,0},{16,8},{24,16},{9,1},{17,9},{25,17},{10,2},{18,10},{26,18},{... | collective-permute-start | bytes 393224 | tf_op jit(solution)/shard_map/ppermute | solution.py:124
  47.6 19.6 %copy-start.2 = (bf16[1,4096,512]{2,1,0:T(8,128)(2,1)S(1)}, bf16[1,4096,512]{2,1,0:T(8,128)(2,1)}, u32[]{:S(2)}) copy-start(bf16[1,4096,512]{2,1,0:T(8,128)(2,1)} %param.10) | copy-start | bytes 12582916
  47.6 5.7 %collective-permute-start.10 = (bf16[64,512]{1,0:T(8,128)(2,1)S(1)}, bf16[64,512]{1,0:T(8,128)(2,1)S(1)}, u32[]{:S(2)}, u32[]{:S(2)}) collective-permute-start(bf16[64,512]{1,0:T(8,128)(2,1)S(1)} %get-tuple-element.10), channel_id=1, source_target_pairs={{0,16},{8,24},{16,0},{24,8},{1,17},{9,25},{17,1},{25,9},{2,18},{10... | collective-permute-start | bytes 196616 | tf_op jit(solution)/shard_map/ppermute | solution.py:17
  51.0 5.6 %collective-permute-start.16 = (bf16[64,1024]{1,0:T(8,128)(2,1)S(1)}, bf16[64,1024]{1,0:T(8,128)(2,1)S(1)}, u32[]{:S(2)}, u32[]{:S(2)}) collective-permute-start(bf16[64,1024]{1,0:T(8,128)(2,1)S(1)} %pad_maximum_fusion.1), channel_id=1, source_target_pairs={{0,16},{8,24},{16,0},{24,8},{1,17},{9,25},{17,1},{25,9},{2,18},{10... | collective-permute-start | bytes 393224 | tf_op jit(solution)/shard_map/ppermute | solution.py:17
  53.7 4.8 %collective-permute-start.11 = (bf16[64,512]{1,0:T(8,128)(2,1)S(1)}, bf16[64,512]{1,0:T(8,128)(2,1)S(1)}, u32[]{:S(2)}, u32[]{:S(2)}) collective-permute-start(bf16[64,512]{1,0:T(8,128)(2,1)S(1)} %select_convert_fusion.1), channel_id=1, source_target_pairs={{0,1},{1,0},{2,3},{3,2},{4,5},{5,4},{6,7},{7,6},{8,9},{9,8},{10,11... | collective-permute-start | bytes 196616 | tf_op jit(solution)/shard_map/ppermute | solution.py:17
  56.7 2.7 %collective-permute-start.18 = (bf16[64,1024]{1,0:T(8,128)(2,1)S(1)}, bf16[64,1024]{1,0:T(8,128)(2,1)S(1)}, u32[]{:S(2)}, u32[]{:S(2)}) collective-permute-start(bf16[64,1024]{1,0:T(8,128)(2,1)S(1)} %get-tuple-element.27), channel_id=1, source_target_pairs={{0,8},{8,0},{16,24},{24,16},{1,9},{9,1},{17,25},{25,17},{2,10},{10... | collective-permute-start | bytes 393224 | tf_op jit(solution)/shard_map/ppermute | solution.py:17
  58.4 5.7 %collective-permute-start.17 = (bf16[64,1024]{1,0:T(8,128)(2,1)S(1)}, bf16[64,1024]{1,0:T(8,128)(2,1)S(1)}, u32[]{:S(2)}, u32[]{:S(2)}) collective-permute-start(bf16[64,1024]{1,0:T(8,128)(2,1)S(1)} %get-tuple-element.26), channel_id=1, source_target_pairs={{0,8},{8,0},{16,24},{24,16},{1,9},{9,1},{17,25},{25,17},{2,10},{10... | collective-permute-start | bytes 393224 | tf_op jit(solution)/shard_map/ppermute | solution.py:17
  58.5 3.2 %collective-permute-start.12 = (bf16[64,512]{1,0:T(8,128)(2,1)S(1)}, bf16[64,512]{1,0:T(8,128)(2,1)S(1)}, u32[]{:S(2)}, u32[]{:S(2)}) collective-permute-start(bf16[64,512]{1,0:T(8,128)(2,1)S(1)} %add_convert_fusion.3), channel_id=1, source_target_pairs={{0,2},{1,3},{2,0},{3,1},{4,6},{5,7},{6,4},{7,5},{8,10},{9,11},{10,... | collective-permute-start | bytes 196616 | tf_op jit(solution)/shard_map/ppermute | solution.py:17
  61.7 4.7 %collective-permute-start.13 = (bf16[64,512]{1,0:T(8,128)(2,1)S(1)}, bf16[64,512]{1,0:T(8,128)(2,1)S(1)}, u32[]{:S(2)}, u32[]{:S(2)}) collective-permute-start(bf16[64,512]{1,0:T(8,128)(2,1)S(1)} %add_convert_fusion.2), channel_id=1, source_target_pairs={{0,4},{1,5},{2,6},{3,7},{4,0},{5,1},{6,2},{7,3},{8,12},{9,13},{10,... | collective-permute-start | bytes 196616 | tf_op jit(solution)/shard_map/ppermute | solution.py:17
  66.4 3.2 %collective-permute-start.14 = (bf16[64,512]{1,0:T(8,128)(2,1)S(1)}, bf16[64,512]{1,0:T(8,128)(2,1)S(1)}, u32[]{:S(2)}, u32[]{:S(2)}) collective-permute-start(bf16[64,512]{1,0:T(8,128)(2,1)S(1)} %fusion.37), channel_id=1, source_target_pairs={{0,1},{1,0},{2,3},{3,2},{4,5},{5,4},{6,7},{7,6},{8,9},{9,8},{10,11... | collective-permute-start | bytes 196616 | tf_op jit(solution)/shard_map/ppermute | solution.py:17
  69.9 7.5 %collective-permute-start.19 = (f32[64,512]{1,0:T(8,128)S(1)}, f32[64,512]{1,0:T(8,128)S(1)}, u32[]{:S(2)}, u32[]{:S(2)}) collective-permute-start(f32[64,512]{1,0:T(8,128)S(1)} %convolution_add_fusion.1), channel_id=1, source_target_pairs={{0,8},{8,0},{16,24},{24,16},{1,9},{9,1},{17,25},{25,17},{2,10},{10... | collective-permute-start | bytes 393224 | tf_op jit(solution)/shard_map/ppermute | solution.py:17
  77.4 3.2 %collective-permute-start.20 = (bf16[64,512]{1,0:T(8,128)(2,1)S(1)}, bf16[64,512]{1,0:T(8,128)(2,1)S(1)}, u32[]{:S(2)}, u32[]{:S(2)}) collective-permute-start(bf16[64,512]{1,0:T(8,128)(2,1)S(1)} %get-tuple-element.8), channel_id=1, source_target_pairs={{0,16},{8,24},{16,0},{24,8},{1,17},{9,25},{17,1},{25,9},{2,18},{10... | collective-permute-start | bytes 196616 | tf_op jit(solution)/shard_map/ppermute | solution.py:17
  77.5 26.7 %collective-permute-start.25 = (f32[64,512]{1,0:T(8,128)S(1)}, f32[64,512]{1,0:T(8,128)S(1)}, u32[]{:S(2)}, u32[]{:S(2)}) collective-permute-start(f32[64,512]{1,0:T(8,128)S(1)} %convolution_add_fusion), channel_id=1, source_target_pairs={{8,0},{16,8},{24,16},{9,1},{17,9},{25,17},{10,2},{18,10},{26,18},{... | collective-permute-start | bytes 393224 | tf_op jit(solution)/shard_map/ppermute | solution.py:124
  81.0 3.2 %collective-permute-start.21 = (bf16[64,512]{1,0:T(8,128)(2,1)S(1)}, bf16[64,512]{1,0:T(8,128)(2,1)S(1)}, u32[]{:S(2)}, u32[]{:S(2)}) collective-permute-start(bf16[64,512]{1,0:T(8,128)(2,1)S(1)} %select_convert_fusion), channel_id=1, source_target_pairs={{0,1},{1,0},{2,3},{3,2},{4,5},{5,4},{6,7},{7,6},{8,9},{9,8},{10,11... | collective-permute-start | bytes 196616 | tf_op jit(solution)/shard_map/ppermute | solution.py:17
  81.3 4.4 %collective-permute-start.26 = (bf16[64,1024]{1,0:T(8,128)(2,1)S(1)}, bf16[64,1024]{1,0:T(8,128)(2,1)S(1)}, u32[]{:S(2)}, u32[]{:S(2)}) collective-permute-start(bf16[64,1024]{1,0:T(8,128)(2,1)S(1)} %pad_maximum_fusion.2), channel_id=1, source_target_pairs={{0,16},{8,24},{16,0},{24,8},{1,17},{9,25},{17,1},{25,9},{2,18},{10... | collective-permute-start | bytes 393224 | tf_op jit(solution)/shard_map/ppermute | solution.py:17
  84.2 4.2 %collective-permute-start.22 = (bf16[64,512]{1,0:T(8,128)(2,1)S(1)}, bf16[64,512]{1,0:T(8,128)(2,1)S(1)}, u32[]{:S(2)}, u32[]{:S(2)}) collective-permute-start(bf16[64,512]{1,0:T(8,128)(2,1)S(1)} %add_convert_fusion.1), channel_id=1, source_target_pairs={{0,2},{1,3},{2,0},{3,1},{4,6},{5,7},{6,4},{7,5},{8,10},{9,11},{10,... | collective-permute-start | bytes 196616 | tf_op jit(solution)/shard_map/ppermute | solution.py:17
  85.8 4.4 %collective-permute-start.28 = (bf16[64,1024]{1,0:T(8,128)(2,1)S(1)}, bf16[64,1024]{1,0:T(8,128)(2,1)S(1)}, u32[]{:S(2)}, u32[]{:S(2)}) collective-permute-start(bf16[64,1024]{1,0:T(8,128)(2,1)S(1)} %get-tuple-element.21), channel_id=1, source_target_pairs={{0,8},{8,0},{16,24},{24,16},{1,9},{9,1},{17,25},{25,17},{2,10},{10... | collective-permute-start | bytes 393224 | tf_op jit(solution)/shard_map/ppermute | solution.py:17
  88.2 5.6 %collective-permute-start.27 = (bf16[64,1024]{1,0:T(8,128)(2,1)S(1)}, bf16[64,1024]{1,0:T(8,128)(2,1)S(1)}, u32[]{:S(2)}, u32[]{:S(2)}) collective-permute-start(bf16[64,1024]{1,0:T(8,128)(2,1)S(1)} %get-tuple-element.20), channel_id=1, source_target_pairs={{0,8},{8,0},{16,24},{24,16},{1,9},{9,1},{17,25},{25,17},{2,10},{10... | collective-permute-start | bytes 393224 | tf_op jit(solution)/shard_map/ppermute | solution.py:17
  88.4 4.8 %collective-permute-start.23 = (bf16[64,512]{1,0:T(8,128)(2,1)S(1)}, bf16[64,512]{1,0:T(8,128)(2,1)S(1)}, u32[]{:S(2)}, u32[]{:S(2)}) collective-permute-start(bf16[64,512]{1,0:T(8,128)(2,1)S(1)} %add_convert_fusion), channel_id=1, source_target_pairs={{0,4},{1,5},{2,6},{3,7},{4,0},{5,1},{6,2},{7,3},{8,12},{9,13},{10,... | collective-permute-start | bytes 196616 | tf_op jit(solution)/shard_map/ppermute | solution.py:17
  93.2 3.2 %collective-permute-start.24 = (bf16[64,512]{1,0:T(8,128)(2,1)S(1)}, bf16[64,512]{1,0:T(8,128)(2,1)S(1)}, u32[]{:S(2)}, u32[]{:S(2)}) collective-permute-start(bf16[64,512]{1,0:T(8,128)(2,1)S(1)} %fusion.36), channel_id=1, source_target_pairs={{0,1},{1,0},{2,3},{3,2},{4,5},{5,4},{6,7},{7,6},{8,9},{9,8},{10,11... | collective-permute-start | bytes 196616 | tf_op jit(solution)/shard_map/ppermute | solution.py:17
  93.8 4.2 %collective-permute-start.30 = (bf16[64,512]{1,0:T(8,128)(2,1)S(1)}, bf16[64,512]{1,0:T(8,128)(2,1)S(1)}, u32[]{:S(2)}, u32[]{:S(2)}) collective-permute-start(bf16[64,512]{1,0:T(8,128)(2,1)S(1)} %fusion.36), channel_id=1, source_target_pairs={{0,17},{1,16},{2,19},{3,18},{4,21},{5,20},{6,23},{7,22},{8,25},{9,... | collective-permute-start | bytes 196616 | tf_op jit(solution)/shard_map/ppermute | solution.py:24
  94.6 3.8 %collective-permute-start.31 = (bf16[64,512]{1,0:T(8,128)(2,1)S(1)}, bf16[64,512]{1,0:T(8,128)(2,1)S(1)}, u32[]{:S(2)}, u32[]{:S(2)}) collective-permute-start(bf16[64,512]{1,0:T(8,128)(2,1)S(1)} %fusion.36), channel_id=1, source_target_pairs={{0,16},{8,24},{16,0},{24,8},{1,17},{9,25},{17,1},{25,9},{2,18},{10... | collective-permute-start | bytes 196616 | tf_op jit(solution)/shard_map/ppermute | solution.py:17
  98.5 8.5 %collective-permute-start.33 = (bf16[64,1024]{1,0:T(8,128)(2,1)S(1)}, bf16[64,1024]{1,0:T(8,128)(2,1)S(1)}, u32[]{:S(2)}, u32[]{:S(2)}) collective-permute-start(bf16[64,1024]{1,0:T(8,128)(2,1)S(1)} %get-tuple-element.15), channel_id=1, source_target_pairs={{0,8},{8,0},{16,24},{24,16},{1,9},{9,1},{17,25},{25,17},{2,10},{10... | collective-permute-start | bytes 393224 | tf_op jit(solution)/shard_map/ppermute | solution.py:17
  104.2 6.3 %collective-permute-start.29 = (f32[64,512]{1,0:T(8,128)S(1)}, f32[64,512]{1,0:T(8,128)S(1)}, u32[]{:S(2)}, u32[]{:S(2)}) collective-permute-start(f32[64,512]{1,0:T(8,128)S(1)} %add.93), channel_id=1, source_target_pairs={{8,0},{16,8},{24,16},{9,1},{17,9},{25,17},{10,2},{18,10},{26,18},{... | collective-permute-start | bytes 393224 | tf_op jit(solution)/shard_map/ppermute | solution.py:124
  106.1 1.4 %collective-permute-start.32 = (bf16[64,1024]{1,0:T(8,128)(2,1)S(1)}, bf16[64,1024]{1,0:T(8,128)(2,1)S(1)}, u32[]{:S(2)}, u32[]{:S(2)}) collective-permute-start(bf16[64,1024]{1,0:T(8,128)(2,1)S(1)} %get-tuple-element.14), channel_id=1, source_target_pairs={{0,8},{8,0},{16,24},{24,16},{1,9},{9,1},{17,25},{25,17},{2,10},{10... | collective-permute-start | bytes 393224 | tf_op jit(solution)/shard_map/ppermute | solution.py:17

commit v2 on v1

--- a/solution.py
+++ b/solution.py
@@ -86,6 +86,13 @@
     )(matrix)
 
 
+def deal_pairs(k, lags):
+    target = {i: i ^ 1 for i in range(lags)}
+    if k > 1:
+        target.update({0: k, k: k ^ 1, k ^ 1: 1, 1: 0})
+    return list(target.items())
+
+
 def steps(incident, onset, beta, inverse_block, delay_blocks, history_sum):
     place = lax.axis_index("delay")
     odd = (lax.axis_index("row") & 1) == 1
@@ -111,7 +118,7 @@
     dealt = {}
     cut = cut_in_rows(matrix, chunk, lags)
     for k in range(1, lags):
-        dealt[k] = lax.ppermute(cut[k - 1], "delay", [(0, k)])
+        dealt[k] = lax.ppermute(cut[k - 1], "delay", deal_pairs(k, lags))
     first_rows = matrix[:chunk]
     for k in [1] + list(reversed(range(2, lags))):
         first_rows = lax.optimization_barrier(jnp.where(place == k, dealt[k], first_rows))

time: 111 us -> 108 us (0.973)
  starting transfers between devices: 63.6 us -> 48.5 us
  waiting for transfers between devices: 33.2 us -> 45.1 us
    ppermute x27, starting transfers between devices: 52.2 us -> 38.2 us  [swapped(): lax.ppermute(value, axis, [(i, i ^ bit) for i in range(lax.axis_size(axis...]
    ppermute x3, waiting for transfers between devices: 0.01 us -> 13.6 us  [steps(): dealt[k] = lax.ppermute(cut[k - 1], 'delay', deal_pairs(k, lags))]
    ppermute x27, waiting for transfers between devices: 29.5 us -> 27.7 us  [swapped(): lax.ppermute(value, axis, [(i, i ^ bit) for i in range(lax.axis_size(axis...]
  transfers between devices with their start and end apart: 34 -> 34, of which waited for: 20 -> 22; matrix products, arithmetic and copies ran while one was open for 6% -> 6% of each run, Pallas kernels for 1% -> 1%
where the time goes in v2:
time: 108 us
  starting transfers between devices  48.5 us (45%)
  waiting for transfers between devices  45.1 us (42%)
  other arithmetic  5.93 us (5%)
  matrix products  4.06 us (4%)
  local copies, waits for them, and re-layouts  2.22 us (2%)
    ppermute x27, starting transfers between devices, swapped(): lax.ppermute(value, axis, [(i, i ^ bit) for i in range(lax.axis_size(axis...  38.2 us
    ppermute x27, waiting for transfers between devices, swapped(): lax.ppermute(value, axis, [(i, i ^ bit) for i in range(lax.axis_size(axis...  27.7 us
    ppermute x3, waiting for transfers between devices, steps(): dealt[k] = lax.ppermute(cut[k - 1], 'delay', deal_pairs(k, lags))  13.6 us
    ppermute x3, starting transfers between devices, steps(): passed = lax.ppermute(future, 'delay', [(i, i - 1) for i in range(1, lags)])  6.21 us
    ppermute x3, starting transfers between devices, steps(): dealt[k] = lax.ppermute(cut[k - 1], 'delay', deal_pairs(k, lags))  3.67 us
    dot_general x3, matrix products, steps(): contribution = jnp.dot(gathered, matrix, preferred_element_type=jnp.float32)  2.5 us
    unnamed x12, local copies, waits for them, and re-layouts  2.22 us
  transfers between devices with their start and end apart: 34, of which 22 were waited for; matrix products, arithmetic and copies ran while one was open for 6% of the time, Pallas kernels for 1%

profile of v2, /device:TPU:1, one launch (start us, length us, event | category | flops | bytes accessed | tf_op | source)
XLA Modules:
  0.0 107.9 jit_solution(3548298652639751533)
XLA Ops:
  0.7 0.8 compare_select_fusion
  1.4 1.0 fusion.25
  2.5 1.2 %collective-permute-done = bf16[64,512]{1,0:T(8,128)(2,1)S(1)} collective-permute-done((bf16[64,512]{1,0:T(8,128)(2,1)S(1)}, bf16[64,512]{1,0:T(8,128)(2,1)S(1)}, u32[]{:S(2)}, u32[]{:S(2)}) %collective-permute-start) | collective-permute-done | bytes 65568 | tf_op jit(solution)/shard_map/ppermute | solution.py:17
  3.8 2.4 %collective-permute-start.1 = (bf16[64,512]{1,0:T(8,128)(2,1)S(1)}, bf16[64,512]{1,0:T(8,128)(2,1)S(1)}, u32[]{:S(2)}, u32[]{:S(2)}) collective-permute-start(bf16[64,512]{1,0:T(8,128)(2,1)S(1)} %add.72), channel_id=1, source_target_pairs={{0,16},{8,24},{16,0},{24,8},{1,17},{9,25},{17,1},{25,9},{2,18},{10... | collective-permute-start | bytes 196616 | tf_op jit(solution)/shard_map/ppermute | solution.py:17
  6.2 2.1 %collective-permute-done.1 = bf16[64,512]{1,0:T(8,128)(2,1)S(1)} collective-permute-done((bf16[64,512]{1,0:T(8,128)(2,1)S(1)}, bf16[64,512]{1,0:T(8,128)(2,1)S(1)}, u32[]{:S(2)}, u32[]{:S(2)}) %collective-permute-start.1) | collective-permute-done | bytes 65568 | tf_op jit(solution)/shard_map/ppermute | solution.py:17
  8.7 1.0 collective-permute-start.2
  9.7 2.2 %copy-done.1 = bf16[1,4096,512]{2,1,0:T(8,128)(2,1)S(1)} copy-done((bf16[1,4096,512]{2,1,0:T(8,128)(2,1)S(1)}, bf16[1,4096,512]{2,1,0:T(8,128)(2,1)}, u32[]{:S(2)}) %copy-start.1) | copy-done | bytes 4194328
  11.9 1.0 cut_rows.1
  12.9 1.8 %collective-permute-start.8 = (bf16[1024,512]{1,0:T(8,128)(2,1)}, bf16[1024,512]{1,0:T(8,128)(2,1)}, u32[]{:S(2)}, u32[]{:S(2)}) collective-permute-start(bf16[1024,512]{1,0:T(8,128)(2,1)} %get-tuple-element.7), channel_id=1, source_target_pairs={{0,8},{8,0},{16,24},{24,16},{1,9},{9,1},{17,25},{25,17},{2,10},{10... | collective-permute-start | bytes 3145736 | tf_op jit(solution)/shard_map/ppermute | solution.py:121
  14.8 1.4 %collective-permute-start.3 = (bf16[64,512]{1,0:T(8,128)(2,1)S(1)}, bf16[64,512]{1,0:T(8,128)(2,1)S(1)}, u32[]{:S(2)}, u32[]{:S(2)}) collective-permute-start(bf16[64,512]{1,0:T(8,128)(2,1)S(1)} %add_convert_fusion.5), channel_id=1, source_target_pairs={{0,2},{1,3},{2,0},{3,1},{4,6},{5,7},{6,4},{7,5},{8,10},{9,11},{10,... | collective-permute-start | bytes 196616 | tf_op jit(solution)/shard_map/ppermute | solution.py:17
  16.5 1.5 %collective-permute-start.7 = (bf16[1024,512]{1,0:T(8,128)(2,1)S(1)}, bf16[1024,512]{1,0:T(8,128)(2,1)}, u32[]{:S(2)}, u32[]{:S(2)}) collective-permute-start(bf16[1024,512]{1,0:T(8,128)(2,1)S(1)} %get-tuple-element.6), channel_id=1, source_target_pairs={{0,24},{8,0},{16,8},{24,16},{1,25},{9,1},{17,9},{25,17},{2,26},{10... | collective-permute-start | bytes 3145736 | tf_op jit(solution)/shard_map/ppermute | solution.py:121
  18.5 2.4 %collective-permute-start.4 = (bf16[64,512]{1,0:T(8,128)(2,1)S(1)}, bf16[64,512]{1,0:T(8,128)(2,1)S(1)}, u32[]{:S(2)}, u32[]{:S(2)}) collective-permute-start(bf16[64,512]{1,0:T(8,128)(2,1)S(1)} %add_convert_fusion.4), channel_id=1, source_target_pairs={{0,4},{1,5},{2,6},{3,7},{4,0},{5,1},{6,2},{7,3},{8,12},{9,13},{10,... | collective-permute-start | bytes 196616 | tf_op jit(solution)/shard_map/ppermute | solution.py:17
  20.9 1.7 %collective-permute-done.4 = bf16[64,512]{1,0:T(8,128)(2,1)S(1)} collective-permute-done((bf16[64,512]{1,0:T(8,128)(2,1)S(1)}, bf16[64,512]{1,0:T(8,128)(2,1)S(1)}, u32[]{:S(2)}, u32[]{:S(2)}) %collective-permute-start.4) | collective-permute-done | bytes 65568 | tf_op jit(solution)/shard_map/ppermute | solution.py:17
  22.6 1.0 collective-permute-start.5
  23.6 2.2 %collective-permute-done.5 = bf16[64,512]{1,0:T(8,128)(2,1)S(1)} collective-permute-done((bf16[64,512]{1,0:T(8,128)(2,1)S(1)}, bf16[64,512]{1,0:T(8,128)(2,1)S(1)}, u32[]{:S(2)}, u32[]{:S(2)}) %collective-permute-start.5) | collective-permute-done | bytes 65568 | tf_op jit(solution)/shard_map/ppermute | solution.py:17
  25.9 1.7 %bitcast_select_fusion = bf16[1024,512]{1,0:T(8,128)(2,1)S(1)} fusion(bf16[1024,512]{1,0:T(8,128)(2,1)} %collective-permute-done.8, bf16[1,4096,512]{2,1,0:T(8,128)(2,1)} %param.10, pred[]{:T(512)S(6)} %eq.24), kind=kLoop, calls=%fused_computation.3 | loop fusion | flops 524288 | bytes 3145729 | tf_op jit(solution)/shard_map/jit(_where)/select_n | solution.py:124
  27.6 13.6 %collective-permute-done.7 = bf16[1024,512]{1,0:T(8,128)(2,1)} collective-permute-done((bf16[1024,512]{1,0:T(8,128)(2,1)S(1)}, bf16[1024,512]{1,0:T(8,128)(2,1)}, u32[]{:S(2)}, u32[]{:S(2)}) %collective-permute-start.7) | collective-permute-done | bytes 1048608 | tf_op jit(solution)/shard_map/ppermute | solution.py:121
  42.2 2.0 %collective-permute-start.15 = (f32[64,512]{1,0:T(8,128)S(1)}, f32[64,512]{1,0:T(8,128)S(1)}, u32[]{:S(2)}, u32[]{:S(2)}) collective-permute-start(f32[64,512]{1,0:T(8,128)S(1)} %bitcast.26), channel_id=1, source_target_pairs={{8,0},{16,8},{24,16},{9,1},{17,9},{25,17},{10,2},{18,10},{26,18},{... | collective-permute-start | bytes 393224 | tf_op jit(solution)/shard_map/ppermute | solution.py:131
  44.3 3.3 %collective-permute-start.10 = (bf16[64,512]{1,0:T(8,128)(2,1)S(1)}, bf16[64,512]{1,0:T(8,128)(2,1)S(1)}, u32[]{:S(2)}, u32[]{:S(2)}) collective-permute-start(bf16[64,512]{1,0:T(8,128)(2,1)S(1)} %get-tuple-element.10), channel_id=1, source_target_pairs={{0,16},{8,24},{16,0},{24,8},{1,17},{9,25},{17,1},{25,9},{2,18},{10... | collective-permute-start | bytes 196616 | tf_op jit(solution)/shard_map/ppermute | solution.py:17
  47.7 2.2 %collective-permute-done.10 = bf16[64,512]{1,0:T(8,128)(2,1)S(1)} collective-permute-done((bf16[64,512]{1,0:T(8,128)(2,1)S(1)}, bf16[64,512]{1,0:T(8,128)(2,1)S(1)}, u32[]{:S(2)}, u32[]{:S(2)}) %collective-permute-start.10) | collective-permute-done | bytes 65568 | tf_op jit(solution)/shard_map/ppermute | solution.py:17
  50.3 0.7 collective-permute-start.11
  51.0 2.2 %collective-permute-done.16 = bf16[64,1024]{1,0:T(8,128)(2,1)S(1)} collective-permute-done((bf16[64,1024]{1,0:T(8,128)(2,1)S(1)}, bf16[64,1024]{1,0:T(8,128)(2,1)S(1)}, u32[]{:S(2)}, u32[]{:S(2)}) %collective-permute-start.16) | collective-permute-done | bytes 131104 | tf_op jit(solution)/shard_map/ppermute | solution.py:17
  53.2 1.7 %collective-permute-start.18 = (bf16[64,1024]{1,0:T(8,128)(2,1)S(1)}, bf16[64,1024]{1,0:T(8,128)(2,1)S(1)}, u32[]{:S(2)}, u32[]{:S(2)}) collective-permute-start(bf16[64,1024]{1,0:T(8,128)(2,1)S(1)} %get-tuple-element.27), channel_id=1, source_target_pairs={{0,8},{8,0},{16,24},{24,16},{1,9},{9,1},{17,25},{25,17},{2,10},{10... | collective-permute-start | bytes 393224 | tf_op jit(solution)/shard_map/ppermute | solution.py:17
  56.0 2.3 %collective-permute-done.12 = bf16[64,512]{1,0:T(8,128)(2,1)S(1)} collective-permute-done((bf16[64,512]{1,0:T(8,128)(2,1)S(1)}, bf16[64,512]{1,0:T(8,128)(2,1)S(1)}, u32[]{:S(2)}, u32[]{:S(2)}) %collective-permute-start.12) | collective-permute-done | bytes 65568 | tf_op jit(solution)/shard_map/ppermute | solution.py:17
  58.3 2.4 %collective-permute-start.13 = (bf16[64,512]{1,0:T(8,128)(2,1)S(1)}, bf16[64,512]{1,0:T(8,128)(2,1)S(1)}, u32[]{:S(2)}, u32[]{:S(2)}) collective-permute-start(bf16[64,512]{1,0:T(8,128)(2,1)S(1)} %add_convert_fusion.2), channel_id=1, source_target_pairs={{0,4},{1,5},{2,6},{3,7},{4,0},{5,1},{6,2},{7,3},{8,12},{9,13},{10,... | collective-permute-start | bytes 196616 | tf_op jit(solution)/shard_map/ppermute | solution.py:17
  60.7 2.3 %collective-permute-done.13 = bf16[64,512]{1,0:T(8,128)(2,1)S(1)} collective-permute-done((bf16[64,512]{1,0:T(8,128)(2,1)S(1)}, bf16[64,512]{1,0:T(8,128)(2,1)S(1)}, u32[]{:S(2)}, u32[]{:S(2)}) %collective-permute-start.13) | collective-permute-done | bytes 65568 | tf_op jit(solution)/shard_map/ppermute | solution.py:17
  63.0 0.7 collective-permute-start.14
  63.7 0.8 convolution_add_fusion
  64.6 1.6 %collective-permute-done.14 = bf16[64,512]{1,0:T(8,128)(2,1)S(1)} collective-permute-done((bf16[64,512]{1,0:T(8,128)(2,1)S(1)}, bf16[64,512]{1,0:T(8,128)(2,1)S(1)}, u32[]{:S(2)}, u32[]{:S(2)}) %collective-permute-start.14) | collective-permute-done | bytes 65568 | tf_op jit(solution)/shard_map/ppermute | solution.py:17
  66.5 6.5 %collective-permute-start.19 = (f32[64,512]{1,0:T(8,128)S(1)}, f32[64,512]{1,0:T(8,128)S(1)}, u32[]{:S(2)}, u32[]{:S(2)}) collective-permute-start(f32[64,512]{1,0:T(8,128)S(1)} %convolution_add_fusion.1), channel_id=1, source_target_pairs={{0,8},{8,0},{16,24},{24,16},{1,9},{9,1},{17,25},{25,17},{2,10},{10... | collective-permute-start | bytes 393224 | tf_op jit(solution)/shard_map/ppermute | solution.py:17
  73.0 1.0 collective-permute-done.19
  74.0 2.3 %collective-permute-start.25 = (f32[64,512]{1,0:T(8,128)S(1)}, f32[64,512]{1,0:T(8,128)S(1)}, u32[]{:S(2)}, u32[]{:S(2)}) collective-permute-start(f32[64,512]{1,0:T(8,128)S(1)} %convolution_add_fusion), channel_id=1, source_target_pairs={{8,0},{16,8},{24,16},{9,1},{17,9},{25,17},{10,2},{18,10},{26,18},{... | collective-permute-start | bytes 393224 | tf_op jit(solution)/shard_map/ppermute | solution.py:131
  76.3 0.8 collective-permute-done.20
  77.5 0.7 collective-permute-start.21
  78.3 1.0 collective-permute-start.26
  79.3 1.4 %collective-permute-done.21 = bf16[64,512]{1,0:T(8,128)(2,1)S(1)} collective-permute-done((bf16[64,512]{1,0:T(8,128)(2,1)S(1)}, bf16[64,512]{1,0:T(8,128)(2,1)S(1)}, u32[]{:S(2)}, u32[]{:S(2)}) %collective-permute-start.21) | collective-permute-done | bytes 65568 | tf_op jit(solution)/shard_map/ppermute | solution.py:17
  80.8 1.7 %collective-permute-done.26 = bf16[64,1024]{1,0:T(8,128)(2,1)S(1)} collective-permute-done((bf16[64,1024]{1,0:T(8,128)(2,1)S(1)}, bf16[64,1024]{1,0:T(8,128)(2,1)S(1)}, u32[]{:S(2)}, u32[]{:S(2)}) %collective-permute-start.26) | collective-permute-done | bytes 131104 | tf_op jit(solution)/shard_map/ppermute | solution.py:17
  82.5 2.7 %collective-permute-start.28 = (bf16[64,1024]{1,0:T(8,128)(2,1)S(1)}, bf16[64,1024]{1,0:T(8,128)(2,1)S(1)}, u32[]{:S(2)}, u32[]{:S(2)}) collective-permute-start(bf16[64,1024]{1,0:T(8,128)(2,1)S(1)} %get-tuple-element.21), channel_id=1, source_target_pairs={{0,8},{8,0},{16,24},{24,16},{1,9},{9,1},{17,25},{25,17},{2,10},{10... | collective-permute-start | bytes 393224 | tf_op jit(solution)/shard_map/ppermute | solution.py:17
  85.3 1.8 %collective-permute-start.23 = (bf16[64,512]{1,0:T(8,128)(2,1)S(1)}, bf16[64,512]{1,0:T(8,128)(2,1)S(1)}, u32[]{:S(2)}, u32[]{:S(2)}) collective-permute-start(bf16[64,512]{1,0:T(8,128)(2,1)S(1)} %add_convert_fusion), channel_id=1, source_target_pairs={{0,4},{1,5},{2,6},{3,7},{4,0},{5,1},{6,2},{7,3},{8,12},{9,13},{10,... | collective-permute-start | bytes 196616 | tf_op jit(solution)/shard_map/ppermute | solution.py:17
  87.1 2.8 %collective-permute-done.23 = bf16[64,512]{1,0:T(8,128)(2,1)S(1)} collective-permute-done((bf16[64,512]{1,0:T(8,128)(2,1)S(1)}, bf16[64,512]{1,0:T(8,128)(2,1)S(1)}, u32[]{:S(2)}, u32[]{:S(2)}) %collective-permute-start.23) | collective-permute-done | bytes 65568 | tf_op jit(solution)/shard_map/ppermute | solution.py:17
  91.2 1.6 %collective-permute-start.31 = (bf16[64,512]{1,0:T(8,128)(2,1)S(1)}, bf16[64,512]{1,0:T(8,128)(2,1)S(1)}, u32[]{:S(2)}, u32[]{:S(2)}) collective-permute-start(bf16[64,512]{1,0:T(8,128)(2,1)S(1)} %fusion.36), channel_id=1, source_target_pairs={{0,16},{8,24},{16,0},{24,8},{1,17},{9,25},{17,1},{25,9},{2,18},{10... | collective-permute-start | bytes 196616 | tf_op jit(solution)/shard_map/ppermute | solution.py:17
  93.2 1.8 %collective-permute-done.30 = bf16[64,512]{1,0:T(8,128)(2,1)S(1)} collective-permute-done((bf16[64,512]{1,0:T(8,128)(2,1)S(1)}, bf16[64,512]{1,0:T(8,128)(2,1)S(1)}, u32[]{:S(2)}, u32[]{:S(2)}) %collective-permute-start.30) | collective-permute-done | bytes 65568 | tf_op jit(solution)/shard_map/ppermute | solution.py:24
  95.2 4.8 %collective-permute-start.33 = (bf16[64,1024]{1,0:T(8,128)(2,1)S(1)}, bf16[64,1024]{1,0:T(8,128)(2,1)S(1)}, u32[]{:S(2)}, u32[]{:S(2)}) collective-permute-start(bf16[64,1024]{1,0:T(8,128)(2,1)S(1)} %get-tuple-element.15), channel_id=1, source_target_pairs={{0,8},{8,0},{16,24},{24,16},{1,9},{9,1},{17,25},{25,17},{2,10},{10... | collective-permute-start | bytes 393224 | tf_op jit(solution)/shard_map/ppermute | solution.py:17
  100.1 0.8 fusion.7
  100.9 1.9 %collective-permute-start.29 = (f32[64,512]{1,0:T(8,128)S(1)}, f32[64,512]{1,0:T(8,128)S(1)}, u32[]{:S(2)}, u32[]{:S(2)}) collective-permute-start(f32[64,512]{1,0:T(8,128)S(1)} %add.93), channel_id=1, source_target_pairs={{8,0},{16,8},{24,16},{9,1},{17,9},{25,17},{10,2},{18,10},{26,18},{... | collective-permute-start | bytes 393224 | tf_op jit(solution)/shard_map/ppermute | solution.py:131
  102.9 0.8 pad_maximum_fusion
  104.3 0.8 fusion.15
  105.1 2.1 %collective-permute-done.29 = f32[64,512]{1,0:T(8,128)S(1)} collective-permute-done((f32[64,512]{1,0:T(8,128)S(1)}, f32[64,512]{1,0:T(8,128)S(1)}, u32[]{:S(2)}, u32[]{:S(2)}) %collective-permute-start.29) | collective-permute-done | bytes 131104 | tf_op jit(solution)/shard_map/ppermute | solution.py:131
  (80 shorter events, 8.3 us)
Async XLA Ops:
  0.6 7.7 %copy-start = (bf16[512,1024]{1,0:T(8,128)(2,1)S(1)}, bf16[512,1024]{1,0:T(8,128)(2,1)}, u32[]{:S(2)}) copy-start(bf16[512,1024]{1,0:T(8,128)(2,1)} %param.9) | copy-start | bytes 3145732
  0.6 20.2 %copy-start.5 = (f32[1024]{0:T(1024)S(1)}, f32[1024]{0:T(1024)}, u32[]{:S(2)}) copy-start(f32[1024]{0:T(1024)} %param.8) | copy-start | bytes 12292
  2.5 1.3 %collective-permute-start = (bf16[64,512]{1,0:T(8,128)(2,1)S(1)}, bf16[64,512]{1,0:T(8,128)(2,1)S(1)}, u32[]{:S(2)}, u32[]{:S(2)}) collective-permute-start(bf16[64,512]{1,0:T(8,128)(2,1)S(1)} %fusion.25), channel_id=1, source_target_pairs={{0,8},{8,0},{16,24},{24,16},{1,9},{9,1},{17,25},{25,17},{2,10},{10... | collective-permute-start | bytes 196616 | tf_op jit(solution)/shard_map/ppermute | solution.py:17
  3.8 4.6 %collective-permute-start.1 = (bf16[64,512]{1,0:T(8,128)(2,1)S(1)}, bf16[64,512]{1,0:T(8,128)(2,1)S(1)}, u32[]{:S(2)}, u32[]{:S(2)}) collective-permute-start(bf16[64,512]{1,0:T(8,128)(2,1)S(1)} %add.72), channel_id=1, source_target_pairs={{0,16},{8,24},{16,0},{24,8},{1,17},{9,25},{17,1},{25,9},{2,18},{10... | collective-permute-start | bytes 196616 | tf_op jit(solution)/shard_map/ppermute | solution.py:17
  8.7 6.1 %collective-permute-start.2 = (bf16[64,512]{1,0:T(8,128)(2,1)S(1)}, bf16[64,512]{1,0:T(8,128)(2,1)S(1)}, u32[]{:S(2)}, u32[]{:S(2)}) collective-permute-start(bf16[64,512]{1,0:T(8,128)(2,1)S(1)} %select_convert_fusion.2), channel_id=1, source_target_pairs={{0,1},{1,0},{2,3},{3,2},{4,5},{5,4},{6,7},{7,6},{8,9},{9,8},{10,11... | collective-permute-start | bytes 196616 | tf_op jit(solution)/shard_map/ppermute | solution.py:17
  9.7 2.2 %copy-start.1 = (bf16[1,4096,512]{2,1,0:T(8,128)(2,1)S(1)}, bf16[1,4096,512]{2,1,0:T(8,128)(2,1)}, u32[]{:S(2)}) copy-start(bf16[1,4096,512]{2,1,0:T(8,128)(2,1)} %param.10) | copy-start | bytes 12582916
  12.9 12.9 %collective-permute-start.8 = (bf16[1024,512]{1,0:T(8,128)(2,1)}, bf16[1024,512]{1,0:T(8,128)(2,1)}, u32[]{:S(2)}, u32[]{:S(2)}) collective-permute-start(bf16[1024,512]{1,0:T(8,128)(2,1)} %get-tuple-element.7), channel_id=1, source_target_pairs={{0,8},{8,0},{16,24},{24,16},{1,9},{9,1},{17,25},{25,17},{2,10},{10... | collective-permute-start | bytes 3145736 | tf_op jit(solution)/shard_map/ppermute | solution.py:121
  14.8 3.7 %collective-permute-start.3 = (bf16[64,512]{1,0:T(8,128)(2,1)S(1)}, bf16[64,512]{1,0:T(8,128)(2,1)S(1)}, u32[]{:S(2)}, u32[]{:S(2)}) collective-permute-start(bf16[64,512]{1,0:T(8,128)(2,1)S(1)} %add_convert_fusion.5), channel_id=1, source_target_pairs={{0,2},{1,3},{2,0},{3,1},{4,6},{5,7},{6,4},{7,5},{8,10},{9,11},{10,... | collective-permute-start | bytes 196616 | tf_op jit(solution)/shard_map/ppermute | solution.py:17
  16.2 25.1 %collective-permute-start.6 = (bf16[1024,512]{1,0:T(8,128)(2,1)S(1)}, bf16[1024,512]{1,0:T(8,128)(2,1)}, u32[]{:S(2)}, u32[]{:S(2)}) collective-permute-start(bf16[1024,512]{1,0:T(8,128)(2,1)S(1)} %get-tuple-element.5), channel_id=1, source_target_pairs={{0,16},{8,0},{16,24},{24,8},{1,17},{9,1},{17,25},{25,9},{2,18},{10... | collective-permute-start | bytes 3145736 | tf_op jit(solution)/shard_map/ppermute | solution.py:121
  16.5 24.7 %collective-permute-start.7 = (bf16[1024,512]{1,0:T(8,128)(2,1)S(1)}, bf16[1024,512]{1,0:T(8,128)(2,1)}, u32[]{:S(2)}, u32[]{:S(2)}) collective-permute-start(bf16[1024,512]{1,0:T(8,128)(2,1)S(1)} %get-tuple-element.6), channel_id=1, source_target_pairs={{0,24},{8,0},{16,8},{24,16},{1,25},{9,1},{17,9},{25,17},{2,26},{10... | collective-permute-start | bytes 3145736 | tf_op jit(solution)/shard_map/ppermute | solution.py:121
  18.5 4.1 %collective-permute-start.4 = (bf16[64,512]{1,0:T(8,128)(2,1)S(1)}, bf16[64,512]{1,0:T(8,128)(2,1)S(1)}, u32[]{:S(2)}, u32[]{:S(2)}) collective-permute-start(bf16[64,512]{1,0:T(8,128)(2,1)S(1)} %add_convert_fusion.4), channel_id=1, source_target_pairs={{0,4},{1,5},{2,6},{3,7},{4,0},{5,1},{6,2},{7,3},{8,12},{9,13},{10,... | collective-permute-start | bytes 196616 | tf_op jit(solution)/shard_map/ppermute | solution.py:17
  22.6 3.2 %collective-permute-start.5 = (bf16[64,512]{1,0:T(8,128)(2,1)S(1)}, bf16[64,512]{1,0:T(8,128)(2,1)S(1)}, u32[]{:S(2)}, u32[]{:S(2)}) collective-permute-start(bf16[64,512]{1,0:T(8,128)(2,1)S(1)} %fusion.38), channel_id=1, source_target_pairs={{0,1},{1,0},{2,3},{3,2},{4,5},{5,4},{6,7},{7,6},{8,9},{9,8},{10,11... | collective-permute-start | bytes 196616 | tf_op jit(solution)/shard_map/ppermute | solution.py:17
  25.8 15.6 %copy-start.4 = (f32[1,64,512]{2,1,0:T(8,128)S(1)}, f32[1,64,512]{2,1,0:T(8,128)}, u32[]{:S(2)}) copy-start(f32[1,64,512]{2,1,0:T(8,128)} %param.11) | copy-start | bytes 393220
  27.6 22.3 %copy-start.3 = (bf16[64,512]{1,0:T(8,128)(2,1)S(1)}, bf16[64,512]{1,0:T(8,128)(2,1)}, u32[]{:S(2)}) copy-start(bf16[64,512]{1,0:T(8,128)(2,1)} %param.6) | copy-start | bytes 196612
  41.7 2.5 %collective-permute-start.9 = (f32[64,512]{1,0:T(8,128)S(1)}, f32[64,512]{1,0:T(8,128)S(1)}, u32[]{:S(2)}, u32[]{:S(2)}) collective-permute-start(f32[64,512]{1,0:T(8,128)S(1)} %convolution_add_fusion.2), channel_id=1, source_target_pairs={{0,8},{8,0},{16,24},{24,16},{1,9},{9,1},{17,25},{25,17},{2,10},{10... | collective-permute-start | bytes 393224 | tf_op jit(solution)/shard_map/ppermute | solution.py:17
  42.2 21.5 %collective-permute-start.15 = (f32[64,512]{1,0:T(8,128)S(1)}, f32[64,512]{1,0:T(8,128)S(1)}, u32[]{:S(2)}, u32[]{:S(2)}) collective-permute-start(f32[64,512]{1,0:T(8,128)S(1)} %bitcast.26), channel_id=1, source_target_pairs={{8,0},{16,8},{24,16},{9,1},{17,9},{25,17},{10,2},{18,10},{26,18},{... | collective-permute-start | bytes 393224 | tf_op jit(solution)/shard_map/ppermute | solution.py:131
  44.2 19.5 %copy-start.2 = (bf16[1,4096,512]{2,1,0:T(8,128)(2,1)S(1)}, bf16[1,4096,512]{2,1,0:T(8,128)(2,1)}, u32[]{:S(2)}) copy-start(bf16[1,4096,512]{2,1,0:T(8,128)(2,1)} %param.10) | copy-start | bytes 12582916
  44.3 5.6 %collective-permute-start.10 = (bf16[64,512]{1,0:T(8,128)(2,1)S(1)}, bf16[64,512]{1,0:T(8,128)(2,1)S(1)}, u32[]{:S(2)}, u32[]{:S(2)}) collective-permute-start(bf16[64,512]{1,0:T(8,128)(2,1)S(1)} %get-tuple-element.10), channel_id=1, source_target_pairs={{0,16},{8,24},{16,0},{24,8},{1,17},{9,25},{17,1},{25,9},{2,18},{10... | collective-permute-start | bytes 196616 | tf_op jit(solution)/shard_map/ppermute | solution.py:17
  47.6 5.6 %collective-permute-start.16 = (bf16[64,1024]{1,0:T(8,128)(2,1)S(1)}, bf16[64,1024]{1,0:T(8,128)(2,1)S(1)}, u32[]{:S(2)}, u32[]{:S(2)}) collective-permute-start(bf16[64,1024]{1,0:T(8,128)(2,1)S(1)} %pad_maximum_fusion.1), channel_id=1, source_target_pairs={{0,16},{8,24},{16,0},{24,8},{1,17},{9,25},{17,1},{25,9},{2,18},{10... | collective-permute-start | bytes 393224 | tf_op jit(solution)/shard_map/ppermute | solution.py:17
  50.3 4.8 %collective-permute-start.11 = (bf16[64,512]{1,0:T(8,128)(2,1)S(1)}, bf16[64,512]{1,0:T(8,128)(2,1)S(1)}, u32[]{:S(2)}, u32[]{:S(2)}) collective-permute-start(bf16[64,512]{1,0:T(8,128)(2,1)S(1)} %select_convert_fusion.1), channel_id=1, source_target_pairs={{0,1},{1,0},{2,3},{3,2},{4,5},{5,4},{6,7},{7,6},{8,9},{9,8},{10,11... | collective-permute-start | bytes 196616 | tf_op jit(solution)/shard_map/ppermute | solution.py:17
  53.2 2.7 %collective-permute-start.18 = (bf16[64,1024]{1,0:T(8,128)(2,1)S(1)}, bf16[64,1024]{1,0:T(8,128)(2,1)S(1)}, u32[]{:S(2)}, u32[]{:S(2)}) collective-permute-start(bf16[64,1024]{1,0:T(8,128)(2,1)S(1)} %get-tuple-element.27), channel_id=1, source_target_pairs={{0,8},{8,0},{16,24},{24,16},{1,9},{9,1},{17,25},{25,17},{2,10},{10... | collective-permute-start | bytes 393224 | tf_op jit(solution)/shard_map/ppermute | solution.py:17
  54.9 5.7 %collective-permute-start.17 = (bf16[64,1024]{1,0:T(8,128)(2,1)S(1)}, bf16[64,1024]{1,0:T(8,128)(2,1)S(1)}, u32[]{:S(2)}, u32[]{:S(2)}) collective-permute-start(bf16[64,1024]{1,0:T(8,128)(2,1)S(1)} %get-tuple-element.26), channel_id=1, source_target_pairs={{0,8},{8,0},{16,24},{24,16},{1,9},{9,1},{17,25},{25,17},{2,10},{10... | collective-permute-start | bytes 393224 | tf_op jit(solution)/shard_map/ppermute | solution.py:17
  55.1 3.2 %collective-permute-start.12 = (bf16[64,512]{1,0:T(8,128)(2,1)S(1)}, bf16[64,512]{1,0:T(8,128)(2,1)S(1)}, u32[]{:S(2)}, u32[]{:S(2)}) collective-permute-start(bf16[64,512]{1,0:T(8,128)(2,1)S(1)} %add_convert_fusion.3), channel_id=1, source_target_pairs={{0,2},{1,3},{2,0},{3,1},{4,6},{5,7},{6,4},{7,5},{8,10},{9,11},{10,... | collective-permute-start | bytes 196616 | tf_op jit(solution)/shard_map/ppermute | solution.py:17
  58.3 4.7 %collective-permute-start.13 = (bf16[64,512]{1,0:T(8,128)(2,1)S(1)}, bf16[64,512]{1,0:T(8,128)(2,1)S(1)}, u32[]{:S(2)}, u32[]{:S(2)}) collective-permute-start(bf16[64,512]{1,0:T(8,128)(2,1)S(1)} %add_convert_fusion.2), channel_id=1, source_target_pairs={{0,4},{1,5},{2,6},{3,7},{4,0},{5,1},{6,2},{7,3},{8,12},{9,13},{10,... | collective-permute-start | bytes 196616 | tf_op jit(solution)/shard_map/ppermute | solution.py:17
  63.0 3.2 %collective-permute-start.14 = (bf16[64,512]{1,0:T(8,128)(2,1)S(1)}, bf16[64,512]{1,0:T(8,128)(2,1)S(1)}, u32[]{:S(2)}, u32[]{:S(2)}) collective-permute-start(bf16[64,512]{1,0:T(8,128)(2,1)S(1)} %fusion.37), channel_id=1, source_target_pairs={{0,1},{1,0},{2,3},{3,2},{4,5},{5,4},{6,7},{7,6},{8,9},{9,8},{10,11... | collective-permute-start | bytes 196616 | tf_op jit(solution)/shard_map/ppermute | solution.py:17
  66.5 7.5 %collective-permute-start.19 = (f32[64,512]{1,0:T(8,128)S(1)}, f32[64,512]{1,0:T(8,128)S(1)}, u32[]{:S(2)}, u32[]{:S(2)}) collective-permute-start(f32[64,512]{1,0:T(8,128)S(1)} %convolution_add_fusion.1), channel_id=1, source_target_pairs={{0,8},{8,0},{16,24},{24,16},{1,9},{9,1},{17,25},{25,17},{2,10},{10... | collective-permute-start | bytes 393224 | tf_op jit(solution)/shard_map/ppermute | solution.py:17
  74.0 3.2 %collective-permute-start.20 = (bf16[64,512]{1,0:T(8,128)(2,1)S(1)}, bf16[64,512]{1,0:T(8,128)(2,1)S(1)}, u32[]{:S(2)}, u32[]{:S(2)}) collective-permute-start(bf16[64,512]{1,0:T(8,128)(2,1)S(1)} %get-tuple-element.8), channel_id=1, source_target_pairs={{0,16},{8,24},{16,0},{24,8},{1,17},{9,25},{17,1},{25,9},{2,18},{10... | collective-permute-start | bytes 196616 | tf_op jit(solution)/shard_map/ppermute | solution.py:17
  74.0 26.9 %collective-permute-start.25 = (f32[64,512]{1,0:T(8,128)S(1)}, f32[64,512]{1,0:T(8,128)S(1)}, u32[]{:S(2)}, u32[]{:S(2)}) collective-permute-start(f32[64,512]{1,0:T(8,128)S(1)} %convolution_add_fusion), channel_id=1, source_target_pairs={{8,0},{16,8},{24,16},{9,1},{17,9},{25,17},{10,2},{18,10},{26,18},{... | collective-permute-start | bytes 393224 | tf_op jit(solution)/shard_map/ppermute | solution.py:131
  77.5 3.2 %collective-permute-start.21 = (bf16[64,512]{1,0:T(8,128)(2,1)S(1)}, bf16[64,512]{1,0:T(8,128)(2,1)S(1)}, u32[]{:S(2)}, u32[]{:S(2)}) collective-permute-start(bf16[64,512]{1,0:T(8,128)(2,1)S(1)} %select_convert_fusion), channel_id=1, source_target_pairs={{0,1},{1,0},{2,3},{3,2},{4,5},{5,4},{6,7},{7,6},{8,9},{9,8},{10,11... | collective-permute-start | bytes 196616 | tf_op jit(solution)/shard_map/ppermute | solution.py:17
  78.3 4.2 %collective-permute-start.26 = (bf16[64,1024]{1,0:T(8,128)(2,1)S(1)}, bf16[64,1024]{1,0:T(8,128)(2,1)S(1)}, u32[]{:S(2)}, u32[]{:S(2)}) collective-permute-start(bf16[64,1024]{1,0:T(8,128)(2,1)S(1)} %pad_maximum_fusion.2), channel_id=1, source_target_pairs={{0,16},{8,24},{16,0},{24,8},{1,17},{9,25},{17,1},{25,9},{2,18},{10... | collective-permute-start | bytes 393224 | tf_op jit(solution)/shard_map/ppermute | solution.py:17
  80.7 4.6 %collective-permute-start.22 = (bf16[64,512]{1,0:T(8,128)(2,1)S(1)}, bf16[64,512]{1,0:T(8,128)(2,1)S(1)}, u32[]{:S(2)}, u32[]{:S(2)}) collective-permute-start(bf16[64,512]{1,0:T(8,128)(2,1)S(1)} %add_convert_fusion.1), channel_id=1, source_target_pairs={{0,2},{1,3},{2,0},{3,1},{4,6},{5,7},{6,4},{7,5},{8,10},{9,11},{10,... | collective-permute-start | bytes 196616 | tf_op jit(solution)/shard_map/ppermute | solution.py:17
  82.5 4.6 %collective-permute-start.28 = (bf16[64,1024]{1,0:T(8,128)(2,1)S(1)}, bf16[64,1024]{1,0:T(8,128)(2,1)S(1)}, u32[]{:S(2)}, u32[]{:S(2)}) collective-permute-start(bf16[64,1024]{1,0:T(8,128)(2,1)S(1)} %get-tuple-element.21), channel_id=1, source_target_pairs={{0,8},{8,0},{16,24},{24,16},{1,9},{9,1},{17,25},{25,17},{2,10},{10... | collective-permute-start | bytes 393224 | tf_op jit(solution)/shard_map/ppermute | solution.py:17
  85.2 5.5 %collective-permute-start.27 = (bf16[64,1024]{1,0:T(8,128)(2,1)S(1)}, bf16[64,1024]{1,0:T(8,128)(2,1)S(1)}, u32[]{:S(2)}, u32[]{:S(2)}) collective-permute-start(bf16[64,1024]{1,0:T(8,128)(2,1)S(1)} %get-tuple-element.20), channel_id=1, source_target_pairs={{0,8},{8,0},{16,24},{24,16},{1,9},{9,1},{17,25},{25,17},{2,10},{10... | collective-permute-start | bytes 393224 | tf_op jit(solution)/shard_map/ppermute | solution.py:17
  85.3 4.6 %collective-permute-start.23 = (bf16[64,512]{1,0:T(8,128)(2,1)S(1)}, bf16[64,512]{1,0:T(8,128)(2,1)S(1)}, u32[]{:S(2)}, u32[]{:S(2)}) collective-permute-start(bf16[64,512]{1,0:T(8,128)(2,1)S(1)} %add_convert_fusion), channel_id=1, source_target_pairs={{0,4},{1,5},{2,6},{3,7},{4,0},{5,1},{6,2},{7,3},{8,12},{9,13},{10,... | collective-permute-start | bytes 196616 | tf_op jit(solution)/shard_map/ppermute | solution.py:17
  90.0 3.2 %collective-permute-start.24 = (bf16[64,512]{1,0:T(8,128)(2,1)S(1)}, bf16[64,512]{1,0:T(8,128)(2,1)S(1)}, u32[]{:S(2)}, u32[]{:S(2)}) collective-permute-start(bf16[64,512]{1,0:T(8,128)(2,1)S(1)} %fusion.36), channel_id=1, source_target_pairs={{0,1},{1,0},{2,3},{3,2},{4,5},{5,4},{6,7},{7,6},{8,9},{9,8},{10,11... | collective-permute-start | bytes 196616 | tf_op jit(solution)/shard_map/ppermute | solution.py:17
  90.8 4.2 %collective-permute-start.30 = (bf16[64,512]{1,0:T(8,128)(2,1)S(1)}, bf16[64,512]{1,0:T(8,128)(2,1)S(1)}, u32[]{:S(2)}, u32[]{:S(2)}) collective-permute-start(bf16[64,512]{1,0:T(8,128)(2,1)S(1)} %fusion.36), channel_id=1, source_target_pairs={{0,17},{1,16},{2,19},{3,18},{4,21},{5,20},{6,23},{7,22},{8,25},{9,... | collective-permute-start | bytes 196616 | tf_op jit(solution)/shard_map/ppermute | solution.py:24
  91.2 3.9 %collective-permute-start.31 = (bf16[64,512]{1,0:T(8,128)(2,1)S(1)}, bf16[64,512]{1,0:T(8,128)(2,1)S(1)}, u32[]{:S(2)}, u32[]{:S(2)}) collective-permute-start(bf16[64,512]{1,0:T(8,128)(2,1)S(1)} %fusion.36), channel_id=1, source_target_pairs={{0,16},{8,24},{16,0},{24,8},{1,17},{9,25},{17,1},{25,9},{2,18},{10... | collective-permute-start | bytes 196616 | tf_op jit(solution)/shard_map/ppermute | solution.py:17
  95.2 8.5 %collective-permute-start.33 = (bf16[64,1024]{1,0:T(8,128)(2,1)S(1)}, bf16[64,1024]{1,0:T(8,128)(2,1)S(1)}, u32[]{:S(2)}, u32[]{:S(2)}) collective-permute-start(bf16[64,1024]{1,0:T(8,128)(2,1)S(1)} %get-tuple-element.15), channel_id=1, source_target_pairs={{0,8},{8,0},{16,24},{24,16},{1,9},{9,1},{17,25},{25,17},{2,10},{10... | collective-permute-start | bytes 393224 | tf_op jit(solution)/shard_map/ppermute | solution.py:17
  100.9 6.3 %collective-permute-start.29 = (f32[64,512]{1,0:T(8,128)S(1)}, f32[64,512]{1,0:T(8,128)S(1)}, u32[]{:S(2)}, u32[]{:S(2)}) collective-permute-start(f32[64,512]{1,0:T(8,128)S(1)} %add.93), channel_id=1, source_target_pairs={{8,0},{16,8},{24,16},{9,1},{17,9},{25,17},{10,2},{18,10},{26,18},{... | collective-permute-start | bytes 393224 | tf_op jit(solution)/shard_map/ppermute | solution.py:131
  102.9 1.4 %collective-permute-start.32 = (bf16[64,1024]{1,0:T(8,128)(2,1)S(1)}, bf16[64,1024]{1,0:T(8,128)(2,1)S(1)}, u32[]{:S(2)}, u32[]{:S(2)}) collective-permute-start(bf16[64,1024]{1,0:T(8,128)(2,1)S(1)} %get-tuple-element.14), channel_id=1, source_target_pairs={{0,8},{8,0},{16,24},{24,16},{1,9},{9,1},{17,25},{25,17},{2,10},{10... | collective-permute-start | bytes 393224 | tf_op jit(solution)/shard_map/ppermute | solution.py:17

commit v3 on v2

--- a/solution.py
+++ b/solution.py
@@ -113,7 +113,8 @@
         drives.append(incident_wide * envelope[:, None])
 
     residual = jnp.where(place == 0, drives[0] - future, 0.0).astype(jnp.bfloat16)
-    residual = total_over_delay(residual, [jnp.bfloat16] * len(wires))
+    for bit in reversed(place_bits):
+        residual = residual + swapped(residual, "delay", bit)
 
     dealt = {}
     cut = cut_in_rows(matrix, chunk, lags)
@@ -128,7 +129,8 @@
         partial_sum = jnp.dot(residual, inverse_block, preferred_element_type=jnp.float32)
         solved = summed_over_row(partial_sum)
         piece = (solved / (1.0 + beta_half * solved * solved)).astype(jnp.bfloat16)
-        passed = lax.ppermute(future, "delay", [(i, i - 1) for i in range(1, lags)])
+        passed = lax.ppermute(future, "delay", [(i, (i - 1) % lags) for i in range(lags)])
+        passed = jnp.where(place == lags - 1, 0.0, passed)
         if step_index + 1 < STEPS:
             current = columns(piece, swapped(piece, "row", 1), odd)
             addend = jnp.dot(current, first_rows, preferred_element_type=jnp.float32)

time: 108 us -> 105 us (0.972)
  the two profiles are of different devices: /device:TPU:1 before, /device:TPU:0 now
where the time goes in v3:
time: 105 us; the launch traced here: 104 us
  waiting for transfers between devices  55.3 us (53%)
  starting transfers between devices  35.1 us (33%)
  other arithmetic  4.92 us (5%)
  matrix products  4.74 us (5%)
  local copies, waits for them, and re-layouts  2.22 us (2%)
    ppermute x27, waiting for transfers between devices, swapped(): lax.ppermute(value, axis, [(i, i ^ bit) for i in range(lax.axis_size(axis...  41.5 us
    ppermute x27, starting transfers between devices, swapped(): lax.ppermute(value, axis, [(i, i ^ bit) for i in range(lax.axis_size(axis...  26.9 us
    ppermute x3, waiting for transfers between devices, steps(): dealt[k] = lax.ppermute(cut[k - 1], 'delay', deal_pairs(k, lags))  10.7 us
    ppermute x3, starting transfers between devices, steps(): lax.ppermute(future, 'delay', [(i, (i - 1) % lags) for i in range(lags)])  4.27 us
    dot_general x3, matrix products, steps(): contribution = jnp.dot(gathered, matrix, preferred_element_type=jnp.float32)  3.17 us
    ppermute x1, starting transfers between devices, swapped_both(): lax.ppermute(value, ('delay', 'row'), [(i, i ^ flip) for i in range(count)])  2.35 us
    unnamed x12, local copies, waits for them, and re-layouts  2.22 us
  transfers between devices with their start and end apart: 34, of which 23 were waited for; matrix products, arithmetic and copies ran while one was open for 5% of the time, Pallas kernels for 1%

profile of v3, /device:TPU:0, one launch (start us, length us, event | category | flops | bytes accessed | tf_op | source)
XLA Modules:
  0.0 104.3 jit_solution(14690611847160982954)
XLA Ops:
  0.7 0.8 compare_select_fusion
  1.4 1.0 fusion.26
  2.5 3.1 %collective-permute-start = (bf16[64,512]{1,0:T(8,128)(2,1)S(1)}, bf16[64,512]{1,0:T(8,128)(2,1)S(1)}, u32[]{:S(2)}, u32[]{:S(2)}) collective-permute-start(bf16[64,512]{1,0:T(8,128)(2,1)S(1)} %fusion.26), channel_id=1, source_target_pairs={{0,16},{8,24},{16,0},{24,8},{1,17},{9,25},{17,1},{25,9},{2,18},{10... | collective-permute-start | bytes 196616 | tf_op jit(solution)/shard_map/ppermute | solution.py:17
  5.5 2.2 %collective-permute-done = bf16[64,512]{1,0:T(8,128)(2,1)S(1)} collective-permute-done((bf16[64,512]{1,0:T(8,128)(2,1)S(1)}, bf16[64,512]{1,0:T(8,128)(2,1)S(1)}, u32[]{:S(2)}, u32[]{:S(2)}) %collective-permute-start) | collective-permute-done | bytes 65568 | tf_op jit(solution)/shard_map/ppermute | solution.py:17
  7.9 1.2 %collective-permute-done.1 = bf16[64,512]{1,0:T(8,128)(2,1)S(1)} collective-permute-done((bf16[64,512]{1,0:T(8,128)(2,1)S(1)}, bf16[64,512]{1,0:T(8,128)(2,1)S(1)}, u32[]{:S(2)}, u32[]{:S(2)}) %collective-permute-start.1) | collective-permute-done | bytes 65568 | tf_op jit(solution)/shard_map/ppermute | solution.py:17
  9.4 2.1 %collective-permute-start.2 = (bf16[64,512]{1,0:T(8,128)(2,1)S(1)}, bf16[64,512]{1,0:T(8,128)(2,1)S(1)}, u32[]{:S(2)}, u32[]{:S(2)}) collective-permute-start(bf16[64,512]{1,0:T(8,128)(2,1)S(1)} %select_convert_fusion.2), channel_id=1, source_target_pairs={{0,1},{1,0},{2,3},{3,2},{4,5},{5,4},{6,7},{7,6},{8,9},{9,8},{10,11... | collective-permute-start | bytes 196616 | tf_op jit(solution)/shard_map/ppermute | solution.py:17
  11.5 2.2 %copy-done.1 = bf16[1,4096,512]{2,1,0:T(8,128)(2,1)S(1)} copy-done((bf16[1,4096,512]{2,1,0:T(8,128)(2,1)S(1)}, bf16[1,4096,512]{2,1,0:T(8,128)(2,1)}, u32[]{:S(2)}) %copy-start.1) | copy-done | bytes 4194328
  13.7 1.0 cut_rows.1
  14.8 1.6 %collective-permute-start.3 = (bf16[64,512]{1,0:T(8,128)(2,1)S(1)}, bf16[64,512]{1,0:T(8,128)(2,1)S(1)}, u32[]{:S(2)}, u32[]{:S(2)}) collective-permute-start(bf16[64,512]{1,0:T(8,128)(2,1)S(1)} %add_convert_fusion.5), channel_id=1, source_target_pairs={{0,2},{1,3},{2,0},{3,1},{4,6},{5,7},{6,4},{7,5},{8,10},{9,11},{10,... | collective-permute-start | bytes 196616 | tf_op jit(solution)/shard_map/ppermute | solution.py:17
  16.5 1.5 %collective-permute-start.6 = (bf16[1024,512]{1,0:T(8,128)(2,1)S(1)}, bf16[1024,512]{1,0:T(8,128)(2,1)}, u32[]{:S(2)}, u32[]{:S(2)}) collective-permute-start(bf16[1024,512]{1,0:T(8,128)(2,1)S(1)} %get-tuple-element.5), channel_id=1, source_target_pairs={{0,16},{8,0},{16,24},{24,8},{1,17},{9,1},{17,25},{25,9},{2,18},{10... | collective-permute-start | bytes 3145736 | tf_op jit(solution)/shard_map/ppermute | solution.py:122
  18.0 1.3 %collective-permute-done.3 = bf16[64,512]{1,0:T(8,128)(2,1)S(1)} collective-permute-done((bf16[64,512]{1,0:T(8,128)(2,1)S(1)}, bf16[64,512]{1,0:T(8,128)(2,1)S(1)}, u32[]{:S(2)}, u32[]{:S(2)}) %collective-permute-start.3) | collective-permute-done | bytes 65568 | tf_op jit(solution)/shard_map/ppermute | solution.py:17
  19.4 2.7 %collective-permute-start.4 = (bf16[64,512]{1,0:T(8,128)(2,1)S(1)}, bf16[64,512]{1,0:T(8,128)(2,1)S(1)}, u32[]{:S(2)}, u32[]{:S(2)}) collective-permute-start(bf16[64,512]{1,0:T(8,128)(2,1)S(1)} %add_convert_fusion.4), channel_id=1, source_target_pairs={{0,4},{1,5},{2,6},{3,7},{4,0},{5,1},{6,2},{7,3},{8,12},{9,13},{10,... | collective-permute-start | bytes 196616 | tf_op jit(solution)/shard_map/ppermute | solution.py:17
  22.0 3.0 %collective-permute-done.4 = bf16[64,512]{1,0:T(8,128)(2,1)S(1)} collective-permute-done((bf16[64,512]{1,0:T(8,128)(2,1)S(1)}, bf16[64,512]{1,0:T(8,128)(2,1)S(1)}, u32[]{:S(2)}, u32[]{:S(2)}) %collective-permute-start.4) | collective-permute-done | bytes 65568 | tf_op jit(solution)/shard_map/ppermute | solution.py:17
  25.5 3.9 %collective-permute-done.5 = bf16[64,512]{1,0:T(8,128)(2,1)S(1)} collective-permute-done((bf16[64,512]{1,0:T(8,128)(2,1)S(1)}, bf16[64,512]{1,0:T(8,128)(2,1)S(1)}, u32[]{:S(2)}, u32[]{:S(2)}) %collective-permute-start.5) | collective-permute-done | bytes 65568 | tf_op jit(solution)/shard_map/ppermute | solution.py:17
  29.4 1.4 %bitcast_select_fusion = bf16[1024,512]{1,0:T(8,128)(2,1)S(1)} fusion(bf16[1024,512]{1,0:T(8,128)(2,1)} %collective-permute-done.8, bf16[1,4096,512]{2,1,0:T(8,128)(2,1)} %param.10, pred[]{:T(512)S(6)} %eq.27), kind=kLoop, calls=%fused_computation.2 | loop fusion | flops 524288 | bytes 3145729 | tf_op jit(solution)/shard_map/jit(_where)/select_n | solution.py:125
  30.8 10.7 %collective-permute-done.7 = bf16[1024,512]{1,0:T(8,128)(2,1)} collective-permute-done((bf16[1024,512]{1,0:T(8,128)(2,1)S(1)}, bf16[1024,512]{1,0:T(8,128)(2,1)}, u32[]{:S(2)}, u32[]{:S(2)}) %collective-permute-start.7) | collective-permute-done | bytes 1048608 | tf_op jit(solution)/shard_map/ppermute | solution.py:122
  42.3 3.2 %collective-permute-start.15 = (f32[64,512]{1,0:T(8,128)S(1)}, f32[64,512]{1,0:T(8,128)S(1)}, u32[]{:S(2)}, u32[]{:S(2)}) collective-permute-start(f32[64,512]{1,0:T(8,128)S(1)} %bitcast.26), channel_id=1, source_target_pairs={{0,24},{8,0},{16,8},{24,16},{1,25},{9,1},{17,9},{25,17},{2,26},{10... | collective-permute-start | bytes 393224 | tf_op jit(solution)/shard_map/ppermute | solution.py:132
  45.5 1.4 %collective-permute-start.10 = (bf16[64,512]{1,0:T(8,128)(2,1)S(1)}, bf16[64,512]{1,0:T(8,128)(2,1)S(1)}, u32[]{:S(2)}, u32[]{:S(2)}) collective-permute-start(bf16[64,512]{1,0:T(8,128)(2,1)S(1)} %get-tuple-element.10), channel_id=1, source_target_pairs={{0,16},{8,24},{16,0},{24,8},{1,17},{9,25},{17,1},{25,9},{2,18},{10... | collective-permute-start | bytes 196616 | tf_op jit(solution)/shard_map/ppermute | solution.py:17
  46.9 0.8 collective-permute-start.16
  47.7 3.0 %collective-permute-done.10 = bf16[64,512]{1,0:T(8,128)(2,1)S(1)} collective-permute-done((bf16[64,512]{1,0:T(8,128)(2,1)S(1)}, bf16[64,512]{1,0:T(8,128)(2,1)S(1)}, u32[]{:S(2)}, u32[]{:S(2)}) %collective-permute-start.10) | collective-permute-done | bytes 65568 | tf_op jit(solution)/shard_map/ppermute | solution.py:17
  51.0 1.0 collective-permute-start.11
  52.1 0.9 collective-permute-done.16
  53.6 1.8 %collective-permute-done.11 = bf16[64,512]{1,0:T(8,128)(2,1)S(1)} collective-permute-done((bf16[64,512]{1,0:T(8,128)(2,1)S(1)}, bf16[64,512]{1,0:T(8,128)(2,1)S(1)}, u32[]{:S(2)}, u32[]{:S(2)}) %collective-permute-start.11) | collective-permute-done | bytes 65568 | tf_op jit(solution)/shard_map/ppermute | solution.py:17
  55.9 3.8 %collective-permute-done.12 = bf16[64,512]{1,0:T(8,128)(2,1)S(1)} collective-permute-done((bf16[64,512]{1,0:T(8,128)(2,1)S(1)}, bf16[64,512]{1,0:T(8,128)(2,1)S(1)}, u32[]{:S(2)}, u32[]{:S(2)}) %collective-permute-start.12) | collective-permute-done | bytes 65568 | tf_op jit(solution)/shard_map/ppermute | solution.py:17
  59.7 2.7 %collective-permute-start.13 = (bf16[64,512]{1,0:T(8,128)(2,1)S(1)}, bf16[64,512]{1,0:T(8,128)(2,1)S(1)}, u32[]{:S(2)}, u32[]{:S(2)}) collective-permute-start(bf16[64,512]{1,0:T(8,128)(2,1)S(1)} %add_convert_fusion.2), channel_id=1, source_target_pairs={{0,4},{1,5},{2,6},{3,7},{4,0},{5,1},{6,2},{7,3},{8,12},{9,13},{10,... | collective-permute-start | bytes 196616 | tf_op jit(solution)/shard_map/ppermute | solution.py:17
  62.4 3.1 %collective-permute-done.13 = bf16[64,512]{1,0:T(8,128)(2,1)S(1)} collective-permute-done((bf16[64,512]{1,0:T(8,128)(2,1)S(1)}, bf16[64,512]{1,0:T(8,128)(2,1)S(1)}, u32[]{:S(2)}, u32[]{:S(2)}) %collective-permute-start.13) | collective-permute-done | bytes 65568 | tf_op jit(solution)/shard_map/ppermute | solution.py:17
  65.6 1.0 collective-permute-start.14
  66.6 0.8 select_add_fusion.1
  67.5 2.4 %collective-permute-done.14 = bf16[64,512]{1,0:T(8,128)(2,1)S(1)} collective-permute-done((bf16[64,512]{1,0:T(8,128)(2,1)S(1)}, bf16[64,512]{1,0:T(8,128)(2,1)S(1)}, u32[]{:S(2)}, u32[]{:S(2)}) %collective-permute-start.14) | collective-permute-done | bytes 65568 | tf_op jit(solution)/shard_map/ppermute | solution.py:17
  70.3 1.3 %collective-permute-done.19 = f32[64,512]{1,0:T(8,128)S(1)} collective-permute-done((f32[64,512]{1,0:T(8,128)S(1)}, f32[64,512]{1,0:T(8,128)S(1)}, u32[]{:S(2)}, u32[]{:S(2)}) %collective-permute-start.19) | collective-permute-done | bytes 131104 | tf_op jit(solution)/shard_map/ppermute | solution.py:17
  71.7 1.9 %collective-permute-start.20 = (bf16[64,512]{1,0:T(8,128)(2,1)S(1)}, bf16[64,512]{1,0:T(8,128)(2,1)S(1)}, u32[]{:S(2)}, u32[]{:S(2)}) collective-permute-start(bf16[64,512]{1,0:T(8,128)(2,1)S(1)} %get-tuple-element.8), channel_id=1, source_target_pairs={{0,16},{8,24},{16,0},{24,8},{1,17},{9,25},{17,1},{25,9},{2,18},{10... | collective-permute-start | bytes 196616 | tf_op jit(solution)/shard_map/ppermute | solution.py:17
  73.6 2.5 %collective-permute-done.20 = bf16[64,512]{1,0:T(8,128)(2,1)S(1)} collective-permute-done((bf16[64,512]{1,0:T(8,128)(2,1)S(1)}, bf16[64,512]{1,0:T(8,128)(2,1)S(1)}, u32[]{:S(2)}, u32[]{:S(2)}) %collective-permute-start.20) | collective-permute-done | bytes 65568 | tf_op jit(solution)/shard_map/ppermute | solution.py:17
  76.4 1.0 collective-permute-start.21
  77.4 1.8 %collective-permute-start.26 = (bf16[64,1024]{1,0:T(8,128)(2,1)S(1)}, bf16[64,1024]{1,0:T(8,128)(2,1)S(1)}, u32[]{:S(2)}, u32[]{:S(2)}) collective-permute-start(bf16[64,1024]{1,0:T(8,128)(2,1)S(1)} %pad_maximum_fusion.2), channel_id=1, source_target_pairs={{0,16},{8,24},{16,0},{24,8},{1,17},{9,25},{17,1},{25,9},{2,18},{10... | collective-permute-start | bytes 393224 | tf_op jit(solution)/shard_map/ppermute | solution.py:17
  79.3 1.4 %collective-permute-done.21 = bf16[64,512]{1,0:T(8,128)(2,1)S(1)} collective-permute-done((bf16[64,512]{1,0:T(8,128)(2,1)S(1)}, bf16[64,512]{1,0:T(8,128)(2,1)S(1)}, u32[]{:S(2)}, u32[]{:S(2)}) %collective-permute-start.21) | collective-permute-done | bytes 65568 | tf_op jit(solution)/shard_map/ppermute | solution.py:17
  80.8 1.6 %collective-permute-done.26 = bf16[64,1024]{1,0:T(8,128)(2,1)S(1)} collective-permute-done((bf16[64,1024]{1,0:T(8,128)(2,1)S(1)}, bf16[64,1024]{1,0:T(8,128)(2,1)S(1)}, u32[]{:S(2)}, u32[]{:S(2)}) %collective-permute-start.26) | collective-permute-done | bytes 131104 | tf_op jit(solution)/shard_map/ppermute | solution.py:17
  83.1 2.0 %collective-permute-done.22 = bf16[64,512]{1,0:T(8,128)(2,1)S(1)} collective-permute-done((bf16[64,512]{1,0:T(8,128)(2,1)S(1)}, bf16[64,512]{1,0:T(8,128)(2,1)S(1)}, u32[]{:S(2)}, u32[]{:S(2)}) %collective-permute-start.22) | collective-permute-done | bytes 65568 | tf_op jit(solution)/shard_map/ppermute | solution.py:17
  85.1 2.1 %collective-permute-start.23 = (bf16[64,512]{1,0:T(8,128)(2,1)S(1)}, bf16[64,512]{1,0:T(8,128)(2,1)S(1)}, u32[]{:S(2)}, u32[]{:S(2)}) collective-permute-start(bf16[64,512]{1,0:T(8,128)(2,1)S(1)} %add_convert_fusion), channel_id=1, source_target_pairs={{0,4},{1,5},{2,6},{3,7},{4,0},{5,1},{6,2},{7,3},{8,12},{9,13},{10,... | collective-permute-start | bytes 196616 | tf_op jit(solution)/shard_map/ppermute | solution.py:17
  87.2 3.3 %collective-permute-done.23 = bf16[64,512]{1,0:T(8,128)(2,1)S(1)} collective-permute-done((bf16[64,512]{1,0:T(8,128)(2,1)S(1)}, bf16[64,512]{1,0:T(8,128)(2,1)S(1)}, u32[]{:S(2)}, u32[]{:S(2)}) %collective-permute-start.23) | collective-permute-done | bytes 65568 | tf_op jit(solution)/shard_map/ppermute | solution.py:17
  90.5 1.0 collective-permute-start.24
  91.6 2.3 %collective-permute-start.30 = (bf16[64,512]{1,0:T(8,128)(2,1)S(1)}, bf16[64,512]{1,0:T(8,128)(2,1)S(1)}, u32[]{:S(2)}, u32[]{:S(2)}) collective-permute-start(bf16[64,512]{1,0:T(8,128)(2,1)S(1)} %fusion.37), channel_id=1, source_target_pairs={{0,17},{1,16},{2,19},{3,18},{4,21},{5,20},{6,23},{7,22},{8,25},{9,... | collective-permute-start | bytes 196616 | tf_op jit(solution)/shard_map/ppermute | solution.py:24
  94.9 1.9 %collective-permute-done.30 = bf16[64,512]{1,0:T(8,128)(2,1)S(1)} collective-permute-done((bf16[64,512]{1,0:T(8,128)(2,1)S(1)}, bf16[64,512]{1,0:T(8,128)(2,1)S(1)}, u32[]{:S(2)}, u32[]{:S(2)}) %collective-permute-start.30) | collective-permute-done | bytes 65568 | tf_op jit(solution)/shard_map/ppermute | solution.py:24
  96.8 1.4 %collective-permute-done.31 = bf16[64,512]{1,0:T(8,128)(2,1)S(1)} collective-permute-done((bf16[64,512]{1,0:T(8,128)(2,1)S(1)}, bf16[64,512]{1,0:T(8,128)(2,1)S(1)}, u32[]{:S(2)}, u32[]{:S(2)}) %collective-permute-start.31) | collective-permute-done | bytes 65568 | tf_op jit(solution)/shard_map/ppermute | solution.py:17
  98.4 0.8 select_add_fusion
  99.2 1.1 %collective-permute-start.29 = (f32[64,512]{1,0:T(8,128)S(1)}, f32[64,512]{1,0:T(8,128)S(1)}, u32[]{:S(2)}, u32[]{:S(2)}) collective-permute-start(f32[64,512]{1,0:T(8,128)S(1)} %select_add_fusion), channel_id=1, source_target_pairs={{0,24},{8,0},{16,8},{24,16},{1,25},{9,1},{17,9},{25,17},{2,26},{10... | collective-permute-start | bytes 393224 | tf_op jit(solution)/shard_map/ppermute | solution.py:132
  100.3 0.8 pad_maximum_fusion
  101.7 1.1 %collective-permute-done.29 = f32[64,512]{1,0:T(8,128)S(1)} collective-permute-done((f32[64,512]{1,0:T(8,128)S(1)}, f32[64,512]{1,0:T(8,128)S(1)}, u32[]{:S(2)}, u32[]{:S(2)}) %collective-permute-start.29) | collective-permute-done | bytes 131104 | tf_op jit(solution)/shard_map/ppermute | solution.py:132
  102.8 1.5 %add_bitcast_fusion = f32[1,64,512]{2,1,0:T(8,128)} fusion(f32[64,512]{1,0:T(8,128)S(1)} %collective-permute-done.29, pred[]{:T(512)S(6)} %eq.26, bf16[64,1024]{1,0:T(8,128)(2,1)S(1)} %get-tuple-element.17, bf16[64,1024]{1,0:T(8,128)(2,1)S(1)} %get-tuple-element.16, bf16[64,1024]{1,0:T(8,128)(2,1)S(1)} %get-tuple-element.13, ...), kind=kOutput, calls=%fused_computation.53 | convolution fusion | flops 270598144 | bytes 4980737 | tf_op jit(solution)/shard_map/dot_general | solution.py:150
  (78 shorter events, 6.7 us)
Async XLA Ops:
  0.6 8.5 %copy-start = (bf16[512,1024]{1,0:T(8,128)(2,1)S(1)}, bf16[512,1024]{1,0:T(8,128)(2,1)}, u32[]{:S(2)}) copy-start(bf16[512,1024]{1,0:T(8,128)(2,1)} %param.9) | copy-start | bytes 3145732
  0.6 21.4 %copy-start.5 = (f32[1024]{0:T(1024)S(1)}, f32[1024]{0:T(1024)}, u32[]{:S(2)}) copy-start(f32[1024]{0:T(1024)} %param.8) | copy-start | bytes 12292
  2.5 5.3 %collective-permute-start = (bf16[64,512]{1,0:T(8,128)(2,1)S(1)}, bf16[64,512]{1,0:T(8,128)(2,1)S(1)}, u32[]{:S(2)}, u32[]{:S(2)}) collective-permute-start(bf16[64,512]{1,0:T(8,128)(2,1)S(1)} %fusion.26), channel_id=1, source_target_pairs={{0,16},{8,24},{16,0},{24,8},{1,17},{9,25},{17,1},{25,9},{2,18},{10... | collective-permute-start | bytes 196616 | tf_op jit(solution)/shard_map/ppermute | solution.py:17
  7.8 1.3 %collective-permute-start.1 = (bf16[64,512]{1,0:T(8,128)(2,1)S(1)}, bf16[64,512]{1,0:T(8,128)(2,1)S(1)}, u32[]{:S(2)}, u32[]{:S(2)}) collective-permute-start(bf16[64,512]{1,0:T(8,128)(2,1)S(1)} %add.72), channel_id=1, source_target_pairs={{0,8},{8,0},{16,24},{24,16},{1,9},{9,1},{17,25},{25,17},{2,10},{10... | collective-permute-start | bytes 196616 | tf_op jit(solution)/shard_map/ppermute | solution.py:17
  9.4 5.3 %collective-permute-start.2 = (bf16[64,512]{1,0:T(8,128)(2,1)S(1)}, bf16[64,512]{1,0:T(8,128)(2,1)S(1)}, u32[]{:S(2)}, u32[]{:S(2)}) collective-permute-start(bf16[64,512]{1,0:T(8,128)(2,1)S(1)} %select_convert_fusion.2), channel_id=1, source_target_pairs={{0,1},{1,0},{2,3},{3,2},{4,5},{5,4},{6,7},{7,6},{8,9},{9,8},{10,11... | collective-permute-start | bytes 196616 | tf_op jit(solution)/shard_map/ppermute | solution.py:17
  11.5 2.2 %copy-start.1 = (bf16[1,4096,512]{2,1,0:T(8,128)(2,1)S(1)}, bf16[1,4096,512]{2,1,0:T(8,128)(2,1)}, u32[]{:S(2)}) copy-start(bf16[1,4096,512]{2,1,0:T(8,128)(2,1)} %param.10) | copy-start | bytes 12582916
  14.7 14.7 %collective-permute-start.8 = (bf16[1024,512]{1,0:T(8,128)(2,1)}, bf16[1024,512]{1,0:T(8,128)(2,1)}, u32[]{:S(2)}, u32[]{:S(2)}) collective-permute-start(bf16[1024,512]{1,0:T(8,128)(2,1)} %get-tuple-element.7), channel_id=1, source_target_pairs={{0,8},{8,0},{16,24},{24,16},{1,9},{9,1},{17,25},{25,17},{2,10},{10... | collective-permute-start | bytes 3145736 | tf_op jit(solution)/shard_map/ppermute | solution.py:122
  14.8 4.5 %collective-permute-start.3 = (bf16[64,512]{1,0:T(8,128)(2,1)S(1)}, bf16[64,512]{1,0:T(8,128)(2,1)S(1)}, u32[]{:S(2)}, u32[]{:S(2)}) collective-permute-start(bf16[64,512]{1,0:T(8,128)(2,1)S(1)} %add_convert_fusion.5), channel_id=1, source_target_pairs={{0,2},{1,3},{2,0},{3,1},{4,6},{5,7},{6,4},{7,5},{8,10},{9,11},{10,... | collective-permute-start | bytes 196616 | tf_op jit(solution)/shard_map/ppermute | solution.py:17
  16.5 25.2 %collective-permute-start.6 = (bf16[1024,512]{1,0:T(8,128)(2,1)S(1)}, bf16[1024,512]{1,0:T(8,128)(2,1)}, u32[]{:S(2)}, u32[]{:S(2)}) collective-permute-start(bf16[1024,512]{1,0:T(8,128)(2,1)S(1)} %get-tuple-element.5), channel_id=1, source_target_pairs={{0,16},{8,0},{16,24},{24,8},{1,17},{9,1},{17,25},{25,9},{2,18},{10... | collective-permute-start | bytes 3145736 | tf_op jit(solution)/shard_map/ppermute | solution.py:122
  18.0 23.6 %collective-permute-start.7 = (bf16[1024,512]{1,0:T(8,128)(2,1)S(1)}, bf16[1024,512]{1,0:T(8,128)(2,1)}, u32[]{:S(2)}, u32[]{:S(2)}) collective-permute-start(bf16[1024,512]{1,0:T(8,128)(2,1)S(1)} %get-tuple-element.6), channel_id=1, source_target_pairs={{0,24},{8,0},{16,8},{24,16},{1,25},{9,1},{17,9},{25,17},{2,26},{10... | collective-permute-start | bytes 3145736 | tf_op jit(solution)/shard_map/ppermute | solution.py:122
  19.4 5.6 %collective-permute-start.4 = (bf16[64,512]{1,0:T(8,128)(2,1)S(1)}, bf16[64,512]{1,0:T(8,128)(2,1)S(1)}, u32[]{:S(2)}, u32[]{:S(2)}) collective-permute-start(bf16[64,512]{1,0:T(8,128)(2,1)S(1)} %add_convert_fusion.4), channel_id=1, source_target_pairs={{0,4},{1,5},{2,6},{3,7},{4,0},{5,1},{6,2},{7,3},{8,12},{9,13},{10,... | collective-permute-start | bytes 196616 | tf_op jit(solution)/shard_map/ppermute | solution.py:17
  25.0 4.3 %collective-permute-start.5 = (bf16[64,512]{1,0:T(8,128)(2,1)S(1)}, bf16[64,512]{1,0:T(8,128)(2,1)S(1)}, u32[]{:S(2)}, u32[]{:S(2)}) collective-permute-start(bf16[64,512]{1,0:T(8,128)(2,1)S(1)} %fusion.39), channel_id=1, source_target_pairs={{0,1},{1,0},{2,3},{3,2},{4,5},{5,4},{6,7},{7,6},{8,9},{9,8},{10,11... | collective-permute-start | bytes 196616 | tf_op jit(solution)/shard_map/ppermute | solution.py:17
  29.4 12.4 %copy-start.4 = (f32[1,64,512]{2,1,0:T(8,128)S(1)}, f32[1,64,512]{2,1,0:T(8,128)}, u32[]{:S(2)}) copy-start(f32[1,64,512]{2,1,0:T(8,128)} %param.11) | copy-start | bytes 393220
  30.8 19.9 %copy-start.3 = (bf16[64,512]{1,0:T(8,128)(2,1)S(1)}, bf16[64,512]{1,0:T(8,128)(2,1)}, u32[]{:S(2)}) copy-start(bf16[64,512]{1,0:T(8,128)(2,1)} %param.6) | copy-start | bytes 196612
  42.1 3.4 %collective-permute-start.9 = (f32[64,512]{1,0:T(8,128)S(1)}, f32[64,512]{1,0:T(8,128)S(1)}, u32[]{:S(2)}, u32[]{:S(2)}) collective-permute-start(f32[64,512]{1,0:T(8,128)S(1)} %convolution_add_fusion.1), channel_id=1, source_target_pairs={{0,8},{8,0},{16,24},{24,16},{1,9},{9,1},{17,25},{25,17},{2,10},{10... | collective-permute-start | bytes 393224 | tf_op jit(solution)/shard_map/ppermute | solution.py:17
  42.3 24.4 %collective-permute-start.15 = (f32[64,512]{1,0:T(8,128)S(1)}, f32[64,512]{1,0:T(8,128)S(1)}, u32[]{:S(2)}, u32[]{:S(2)}) collective-permute-start(f32[64,512]{1,0:T(8,128)S(1)} %bitcast.26), channel_id=1, source_target_pairs={{0,24},{8,0},{16,8},{24,16},{1,25},{9,1},{17,9},{25,17},{2,26},{10... | collective-permute-start | bytes 393224 | tf_op jit(solution)/shard_map/ppermute | solution.py:132
  45.5 21.2 %copy-start.2 = (bf16[1,4096,512]{2,1,0:T(8,128)(2,1)S(1)}, bf16[1,4096,512]{2,1,0:T(8,128)(2,1)}, u32[]{:S(2)}) copy-start(bf16[1,4096,512]{2,1,0:T(8,128)(2,1)} %param.10) | copy-start | bytes 12582916
  45.5 5.2 %collective-permute-start.10 = (bf16[64,512]{1,0:T(8,128)(2,1)S(1)}, bf16[64,512]{1,0:T(8,128)(2,1)S(1)}, u32[]{:S(2)}, u32[]{:S(2)}) collective-permute-start(bf16[64,512]{1,0:T(8,128)(2,1)S(1)} %get-tuple-element.10), channel_id=1, source_target_pairs={{0,16},{8,24},{16,0},{24,8},{1,17},{9,25},{17,1},{25,9},{2,18},{10... | collective-permute-start | bytes 196616 | tf_op jit(solution)/shard_map/ppermute | solution.py:17
  46.9 6.1 %collective-permute-start.16 = (bf16[64,1024]{1,0:T(8,128)(2,1)S(1)}, bf16[64,1024]{1,0:T(8,128)(2,1)S(1)}, u32[]{:S(2)}, u32[]{:S(2)}) collective-permute-start(bf16[64,1024]{1,0:T(8,128)(2,1)S(1)} %pad_maximum_fusion.1), channel_id=1, source_target_pairs={{0,16},{8,24},{16,0},{24,8},{1,17},{9,25},{17,1},{25,9},{2,18},{10... | collective-permute-start | bytes 393224 | tf_op jit(solution)/shard_map/ppermute | solution.py:17
  51.0 4.3 %collective-permute-start.11 = (bf16[64,512]{1,0:T(8,128)(2,1)S(1)}, bf16[64,512]{1,0:T(8,128)(2,1)S(1)}, u32[]{:S(2)}, u32[]{:S(2)}) collective-permute-start(bf16[64,512]{1,0:T(8,128)(2,1)S(1)} %select_convert_fusion.1), channel_id=1, source_target_pairs={{0,1},{1,0},{2,3},{3,2},{4,5},{5,4},{6,7},{7,6},{8,9},{9,8},{10,11... | collective-permute-start | bytes 196616 | tf_op jit(solution)/shard_map/ppermute | solution.py:17
  53.0 2.9 %collective-permute-start.18 = (bf16[64,1024]{1,0:T(8,128)(2,1)S(1)}, bf16[64,1024]{1,0:T(8,128)(2,1)S(1)}, u32[]{:S(2)}, u32[]{:S(2)}) collective-permute-start(bf16[64,1024]{1,0:T(8,128)(2,1)S(1)} %get-tuple-element.27), channel_id=1, source_target_pairs={{0,8},{8,0},{16,24},{24,16},{1,9},{9,1},{17,25},{25,17},{2,10},{10... | collective-permute-start | bytes 393224 | tf_op jit(solution)/shard_map/ppermute | solution.py:17
  53.1 9.3 %collective-permute-start.17 = (bf16[64,1024]{1,0:T(8,128)(2,1)S(1)}, bf16[64,1024]{1,0:T(8,128)(2,1)S(1)}, u32[]{:S(2)}, u32[]{:S(2)}) collective-permute-start(bf16[64,1024]{1,0:T(8,128)(2,1)S(1)} %get-tuple-element.26), channel_id=1, source_target_pairs={{0,8},{8,0},{16,24},{24,16},{1,9},{9,1},{17,25},{25,17},{2,10},{10... | collective-permute-start | bytes 393224 | tf_op jit(solution)/shard_map/ppermute | solution.py:17
  55.4 4.3 %collective-permute-start.12 = (bf16[64,512]{1,0:T(8,128)(2,1)S(1)}, bf16[64,512]{1,0:T(8,128)(2,1)S(1)}, u32[]{:S(2)}, u32[]{:S(2)}) collective-permute-start(bf16[64,512]{1,0:T(8,128)(2,1)S(1)} %add_convert_fusion.3), channel_id=1, source_target_pairs={{0,2},{1,3},{2,0},{3,1},{4,6},{5,7},{6,4},{7,5},{8,10},{9,11},{10,... | collective-permute-start | bytes 196616 | tf_op jit(solution)/shard_map/ppermute | solution.py:17
  59.7 5.8 %collective-permute-start.13 = (bf16[64,512]{1,0:T(8,128)(2,1)S(1)}, bf16[64,512]{1,0:T(8,128)(2,1)S(1)}, u32[]{:S(2)}, u32[]{:S(2)}) collective-permute-start(bf16[64,512]{1,0:T(8,128)(2,1)S(1)} %add_convert_fusion.2), channel_id=1, source_target_pairs={{0,4},{1,5},{2,6},{3,7},{4,0},{5,1},{6,2},{7,3},{8,12},{9,13},{10,... | collective-permute-start | bytes 196616 | tf_op jit(solution)/shard_map/ppermute | solution.py:17
  65.6 4.3 %collective-permute-start.14 = (bf16[64,512]{1,0:T(8,128)(2,1)S(1)}, bf16[64,512]{1,0:T(8,128)(2,1)S(1)}, u32[]{:S(2)}, u32[]{:S(2)}) collective-permute-start(bf16[64,512]{1,0:T(8,128)(2,1)S(1)} %fusion.38), channel_id=1, source_target_pairs={{0,1},{1,0},{2,3},{3,2},{4,5},{5,4},{6,7},{7,6},{8,9},{9,8},{10,11... | collective-permute-start | bytes 196616 | tf_op jit(solution)/shard_map/ppermute | solution.py:17
  70.3 1.4 %collective-permute-start.19 = (f32[64,512]{1,0:T(8,128)S(1)}, f32[64,512]{1,0:T(8,128)S(1)}, u32[]{:S(2)}, u32[]{:S(2)}) collective-permute-start(f32[64,512]{1,0:T(8,128)S(1)} %convolution_add_fusion), channel_id=1, source_target_pairs={{0,8},{8,0},{16,24},{24,16},{1,9},{9,1},{17,25},{25,17},{2,10},{10... | collective-permute-start | bytes 393224 | tf_op jit(solution)/shard_map/ppermute | solution.py:17
  71.7 4.3 %collective-permute-start.20 = (bf16[64,512]{1,0:T(8,128)(2,1)S(1)}, bf16[64,512]{1,0:T(8,128)(2,1)S(1)}, u32[]{:S(2)}, u32[]{:S(2)}) collective-permute-start(bf16[64,512]{1,0:T(8,128)(2,1)S(1)} %get-tuple-element.8), channel_id=1, source_target_pairs={{0,16},{8,24},{16,0},{24,8},{1,17},{9,25},{17,1},{25,9},{2,18},{10... | collective-permute-start | bytes 196616 | tf_op jit(solution)/shard_map/ppermute | solution.py:17
  73.6 24.8 %collective-permute-start.25 = (f32[64,512]{1,0:T(8,128)S(1)}, f32[64,512]{1,0:T(8,128)S(1)}, u32[]{:S(2)}, u32[]{:S(2)}) collective-permute-start(f32[64,512]{1,0:T(8,128)S(1)} %select_add_fusion.1), channel_id=1, source_target_pairs={{0,24},{8,0},{16,8},{24,16},{1,25},{9,1},{17,9},{25,17},{2,26},{10... | collective-permute-start | bytes 393224 | tf_op jit(solution)/shard_map/ppermute | solution.py:132
  76.4 4.3 %collective-permute-start.21 = (bf16[64,512]{1,0:T(8,128)(2,1)S(1)}, bf16[64,512]{1,0:T(8,128)(2,1)S(1)}, u32[]{:S(2)}, u32[]{:S(2)}) collective-permute-start(bf16[64,512]{1,0:T(8,128)(2,1)S(1)} %select_convert_fusion), channel_id=1, source_target_pairs={{0,1},{1,0},{2,3},{3,2},{4,5},{5,4},{6,7},{7,6},{8,9},{9,8},{10,11... | collective-permute-start | bytes 196616 | tf_op jit(solution)/shard_map/ppermute | solution.py:17
  77.4 5.0 %collective-permute-start.26 = (bf16[64,1024]{1,0:T(8,128)(2,1)S(1)}, bf16[64,1024]{1,0:T(8,128)(2,1)S(1)}, u32[]{:S(2)}, u32[]{:S(2)}) collective-permute-start(bf16[64,1024]{1,0:T(8,128)(2,1)S(1)} %pad_maximum_fusion.2), channel_id=1, source_target_pairs={{0,16},{8,24},{16,0},{24,8},{1,17},{9,25},{17,1},{25,9},{2,18},{10... | collective-permute-start | bytes 393224 | tf_op jit(solution)/shard_map/ppermute | solution.py:17
  80.8 4.3 %collective-permute-start.22 = (bf16[64,512]{1,0:T(8,128)(2,1)S(1)}, bf16[64,512]{1,0:T(8,128)(2,1)S(1)}, u32[]{:S(2)}, u32[]{:S(2)}) collective-permute-start(bf16[64,512]{1,0:T(8,128)(2,1)S(1)} %add_convert_fusion.1), channel_id=1, source_target_pairs={{0,2},{1,3},{2,0},{3,1},{4,6},{5,7},{6,4},{7,5},{8,10},{9,11},{10,... | collective-permute-start | bytes 196616 | tf_op jit(solution)/shard_map/ppermute | solution.py:17
  82.5 4.6 %collective-permute-start.28 = (bf16[64,1024]{1,0:T(8,128)(2,1)S(1)}, bf16[64,1024]{1,0:T(8,128)(2,1)S(1)}, u32[]{:S(2)}, u32[]{:S(2)}) collective-permute-start(bf16[64,1024]{1,0:T(8,128)(2,1)S(1)} %get-tuple-element.21), channel_id=1, source_target_pairs={{0,8},{8,0},{16,24},{24,16},{1,9},{9,1},{17,25},{25,17},{2,10},{10... | collective-permute-start | bytes 393224 | tf_op jit(solution)/shard_map/ppermute | solution.py:17
  82.6 9.0 %collective-permute-start.27 = (bf16[64,1024]{1,0:T(8,128)(2,1)S(1)}, bf16[64,1024]{1,0:T(8,128)(2,1)S(1)}, u32[]{:S(2)}, u32[]{:S(2)}) collective-permute-start(bf16[64,1024]{1,0:T(8,128)(2,1)S(1)} %get-tuple-element.20), channel_id=1, source_target_pairs={{0,8},{8,0},{16,24},{24,16},{1,9},{9,1},{17,25},{25,17},{2,10},{10... | collective-permute-start | bytes 393224 | tf_op jit(solution)/shard_map/ppermute | solution.py:17
  85.1 5.4 %collective-permute-start.23 = (bf16[64,512]{1,0:T(8,128)(2,1)S(1)}, bf16[64,512]{1,0:T(8,128)(2,1)S(1)}, u32[]{:S(2)}, u32[]{:S(2)}) collective-permute-start(bf16[64,512]{1,0:T(8,128)(2,1)S(1)} %add_convert_fusion), channel_id=1, source_target_pairs={{0,4},{1,5},{2,6},{3,7},{4,0},{5,1},{6,2},{7,3},{8,12},{9,13},{10,... | collective-permute-start | bytes 196616 | tf_op jit(solution)/shard_map/ppermute | solution.py:17
  90.5 4.3 %collective-permute-start.24 = (bf16[64,512]{1,0:T(8,128)(2,1)S(1)}, bf16[64,512]{1,0:T(8,128)(2,1)S(1)}, u32[]{:S(2)}, u32[]{:S(2)}) collective-permute-start(bf16[64,512]{1,0:T(8,128)(2,1)S(1)} %fusion.37), channel_id=1, source_target_pairs={{0,1},{1,0},{2,3},{3,2},{4,5},{5,4},{6,7},{7,6},{8,9},{9,8},{10,11... | collective-permute-start | bytes 196616 | tf_op jit(solution)/shard_map/ppermute | solution.py:17
  91.6 5.2 %collective-permute-start.30 = (bf16[64,512]{1,0:T(8,128)(2,1)S(1)}, bf16[64,512]{1,0:T(8,128)(2,1)S(1)}, u32[]{:S(2)}, u32[]{:S(2)}) collective-permute-start(bf16[64,512]{1,0:T(8,128)(2,1)S(1)} %fusion.37), channel_id=1, source_target_pairs={{0,17},{1,16},{2,19},{3,18},{4,21},{5,20},{6,23},{7,22},{8,25},{9,... | collective-permute-start | bytes 196616 | tf_op jit(solution)/shard_map/ppermute | solution.py:24
  93.9 4.3 %collective-permute-start.31 = (bf16[64,512]{1,0:T(8,128)(2,1)S(1)}, bf16[64,512]{1,0:T(8,128)(2,1)S(1)}, u32[]{:S(2)}, u32[]{:S(2)}) collective-permute-start(bf16[64,512]{1,0:T(8,128)(2,1)S(1)} %fusion.37), channel_id=1, source_target_pairs={{0,16},{8,24},{16,0},{24,8},{1,17},{9,25},{17,1},{25,9},{2,18},{10... | collective-permute-start | bytes 196616 | tf_op jit(solution)/shard_map/ppermute | solution.py:17
  98.3 2.8 %collective-permute-start.33 = (bf16[64,1024]{1,0:T(8,128)(2,1)S(1)}, bf16[64,1024]{1,0:T(8,128)(2,1)S(1)}, u32[]{:S(2)}, u32[]{:S(2)}) collective-permute-start(bf16[64,1024]{1,0:T(8,128)(2,1)S(1)} %get-tuple-element.15), channel_id=1, source_target_pairs={{0,8},{8,0},{16,24},{24,16},{1,9},{9,1},{17,25},{25,17},{2,10},{10... | collective-permute-start | bytes 393224 | tf_op jit(solution)/shard_map/ppermute | solution.py:17
  99.2 3.6 %collective-permute-start.29 = (f32[64,512]{1,0:T(8,128)S(1)}, f32[64,512]{1,0:T(8,128)S(1)}, u32[]{:S(2)}, u32[]{:S(2)}) collective-permute-start(f32[64,512]{1,0:T(8,128)S(1)} %select_add_fusion), channel_id=1, source_target_pairs={{0,24},{8,0},{16,8},{24,16},{1,25},{9,1},{17,9},{25,17},{2,26},{10... | collective-permute-start | bytes 393224 | tf_op jit(solution)/shard_map/ppermute | solution.py:132
  100.3 1.3 %collective-permute-start.32 = (bf16[64,1024]{1,0:T(8,128)(2,1)S(1)}, bf16[64,1024]{1,0:T(8,128)(2,1)S(1)}, u32[]{:S(2)}, u32[]{:S(2)}) collective-permute-start(bf16[64,1024]{1,0:T(8,128)(2,1)S(1)} %get-tuple-element.14), channel_id=1, source_target_pairs={{0,8},{8,0},{16,24},{24,16},{1,9},{9,1},{17,25},{25,17},{2,10},{10... | collective-permute-start | bytes 393224 | tf_op jit(solution)/shard_map/ppermute | solution.py:17

commit v4 on v3

--- a/solution.py
+++ b/solution.py
@@ -62,12 +62,12 @@
     return jnp.concatenate(parts, axis=1)
 
 
-def cut_in_rows(matrix, chunk, count):
+def cut_in_rows(matrix, chunk, wanted):
     def copy_rows(rows, *rest):
         copied, done = rest[:-1], rest[-1]
         copies = [
-            pltpu.make_async_copy(rows.at[pl.ds(k * chunk, chunk)], copied[k - 1], done.at[k - 1])
-            for k in range(1, count)
+            pltpu.make_async_copy(rows.at[pl.ds(k * chunk, chunk)], copied[n], done.at[n])
+            for n, k in enumerate(wanted)
         ]
         for copy in copies:
             copy.start()
@@ -78,11 +78,10 @@
     return pl.pallas_call(
         copy_rows,
         in_specs=[pl.BlockSpec(memory_space=pl.ANY)],
-        out_specs=[pl.BlockSpec(memory_space=pl.ANY)] * (count - 1),
-        out_shape=[shape] * (count - 1),
-        scratch_shapes=[pltpu.SemaphoreType.DMA((count - 1,))],
+        out_specs=[pl.BlockSpec(memory_space=pl.ANY)] * len(wanted),
+        out_shape=[shape] * len(wanted),
+        scratch_shapes=[pltpu.SemaphoreType.DMA((len(wanted),))],
         compiler_params=pltpu.CompilerParams(vmem_limit_bytes=1 << 20),
-        name="cut_rows",
     )(matrix)
 
 
@@ -117,11 +116,13 @@
         residual = residual + swapped(residual, "delay", bit)
 
     dealt = {}
-    cut = cut_in_rows(matrix, chunk, lags)
+    others = [1] + list(range(3, lags))
+    cut = dict(zip(others, cut_in_rows(matrix, chunk, others)))
+    cut[2] = cut_in_rows(matrix, chunk, [2])[0]
     for k in range(1, lags):
-        dealt[k] = lax.ppermute(cut[k - 1], "delay", deal_pairs(k, lags))
+        dealt[k] = lax.ppermute(cut[k], "delay", deal_pairs(k, lags))
     first_rows = matrix[:chunk]
-    for k in [1] + list(reversed(range(2, lags))):
+    for k in range(1, lags):
         first_rows = lax.optimization_barrier(jnp.where(place == k, dealt[k], first_rows))
 
     outputs = []

time: 105 us -> 106 us (level)
    unnamed x12 -> x14, local copies, waits for them, and re-layouts: 2.22 us -> 2.22 us
where the time goes in v4:
time: 106 us; the launch traced here: 105 us
  waiting for transfers between devices  55.6 us (52%)
  starting transfers between devices  35.2 us (33%)
  other arithmetic  4.92 us (5%)
  matrix products  4.74 us (4%)
  local copies, waits for them, and re-layouts  2.22 us (2%)
  Pallas kernels  1.08 us (1%)
    ppermute x27, waiting for transfers between devices, swapped(): lax.ppermute(value, axis, [(i, i ^ bit) for i in range(lax.axis_size(axis...  41.9 us
    ppermute x27, starting transfers between devices, swapped(): lax.ppermute(value, axis, [(i, i ^ bit) for i in range(lax.axis_size(axis...  26.3 us
    ppermute x3, waiting for transfers between devices, steps(): dealt[k] = lax.ppermute(cut[k], 'delay', deal_pairs(k, lags))  10.5 us
    ppermute x3, starting transfers between devices, steps(): lax.ppermute(future, 'delay', [(i, (i - 1) % lags) for i in range(lags)])  4.15 us
    dot_general x3, matrix products, steps(): contribution = jnp.dot(gathered, matrix, preferred_element_type=jnp.float32)  3.17 us
    ppermute x1, starting transfers between devices, swapped_both(): lax.ppermute(value, ('delay', 'row'), [(i, i ^ flip) for i in range(count)])  2.86 us
    unnamed x14, local copies, waits for them, and re-layouts  2.22 us
  transfers between devices with their start and end apart: 34, of which 23 were waited for; matrix products, arithmetic and copies ran while one was open for 5% of the time, Pallas kernels for 1%

profile of v4, /device:TPU:0, one launch (start us, length us, event | category | flops | bytes accessed | tf_op | source)
XLA Modules:
  0.0 104.8 jit_solution(8316521839641171412)
XLA Ops:
  0.7 0.8 compare_select_fusion
  1.4 1.0 fusion.26
  2.4 3.1 %collective-permute-start = (bf16[64,512]{1,0:T(8,128)(2,1)S(1)}, bf16[64,512]{1,0:T(8,128)(2,1)S(1)}, u32[]{:S(2)}, u32[]{:S(2)}) collective-permute-start(bf16[64,512]{1,0:T(8,128)(2,1)S(1)} %fusion.26), channel_id=1, source_target_pairs={{0,16},{8,24},{16,0},{24,8},{1,17},{9,25},{17,1},{25,9},{2,18},{10... | collective-permute-start | bytes 196616 | tf_op jit(solution)/shard_map/ppermute | solution.py:17
  5.5 2.2 %collective-permute-done = bf16[64,512]{1,0:T(8,128)(2,1)S(1)} collective-permute-done((bf16[64,512]{1,0:T(8,128)(2,1)S(1)}, bf16[64,512]{1,0:T(8,128)(2,1)S(1)}, u32[]{:S(2)}, u32[]{:S(2)}) %collective-permute-start) | collective-permute-done | bytes 65568 | tf_op jit(solution)/shard_map/ppermute | solution.py:17
  7.9 1.2 %collective-permute-done.1 = bf16[64,512]{1,0:T(8,128)(2,1)S(1)} collective-permute-done((bf16[64,512]{1,0:T(8,128)(2,1)S(1)}, bf16[64,512]{1,0:T(8,128)(2,1)S(1)}, u32[]{:S(2)}, u32[]{:S(2)}) %collective-permute-start.1) | collective-permute-done | bytes 65568 | tf_op jit(solution)/shard_map/ppermute | solution.py:17
  9.4 2.1 %collective-permute-start.2 = (bf16[64,512]{1,0:T(8,128)(2,1)S(1)}, bf16[64,512]{1,0:T(8,128)(2,1)S(1)}, u32[]{:S(2)}, u32[]{:S(2)}) collective-permute-start(bf16[64,512]{1,0:T(8,128)(2,1)S(1)} %select_convert_fusion.2), channel_id=1, source_target_pairs={{0,1},{1,0},{2,3},{3,2},{4,5},{5,4},{6,7},{7,6},{8,9},{9,8},{10,11... | collective-permute-start | bytes 196616 | tf_op jit(solution)/shard_map/ppermute | solution.py:17
  11.5 2.2 %copy-done.1 = bf16[1,4096,512]{2,1,0:T(8,128)(2,1)S(1)} copy-done((bf16[1,4096,512]{2,1,0:T(8,128)(2,1)S(1)}, bf16[1,4096,512]{2,1,0:T(8,128)(2,1)}, u32[]{:S(2)}) %copy-start.1) | copy-done | bytes 4194328
  13.7 1.0 shard_map.77
  14.8 1.6 %collective-permute-start.3 = (bf16[64,512]{1,0:T(8,128)(2,1)S(1)}, bf16[64,512]{1,0:T(8,128)(2,1)S(1)}, u32[]{:S(2)}, u32[]{:S(2)}) collective-permute-start(bf16[64,512]{1,0:T(8,128)(2,1)S(1)} %add_convert_fusion.5), channel_id=1, source_target_pairs={{0,2},{1,3},{2,0},{3,1},{4,6},{5,7},{6,4},{7,5},{8,10},{9,11},{10,... | collective-permute-start | bytes 196616 | tf_op jit(solution)/shard_map/ppermute | solution.py:17
  16.4 1.3 %collective-permute-start.6 = (bf16[1024,512]{1,0:T(8,128)(2,1)S(1)}, bf16[1024,512]{1,0:T(8,128)(2,1)}, u32[]{:S(2)}, u32[]{:S(2)}) collective-permute-start(bf16[1024,512]{1,0:T(8,128)(2,1)S(1)} %get-tuple-element.4), channel_id=1, source_target_pairs={{0,24},{8,0},{16,8},{24,16},{1,25},{9,1},{17,9},{25,17},{2,26},{10... | collective-permute-start | bytes 3145736 | tf_op jit(solution)/shard_map/ppermute | solution.py:123
  18.4 1.0 collective-permute-done.3
  19.4 2.7 %collective-permute-start.4 = (bf16[64,512]{1,0:T(8,128)(2,1)S(1)}, bf16[64,512]{1,0:T(8,128)(2,1)S(1)}, u32[]{:S(2)}, u32[]{:S(2)}) collective-permute-start(bf16[64,512]{1,0:T(8,128)(2,1)S(1)} %add_convert_fusion.4), channel_id=1, source_target_pairs={{0,4},{1,5},{2,6},{3,7},{4,0},{5,1},{6,2},{7,3},{8,12},{9,13},{10,... | collective-permute-start | bytes 196616 | tf_op jit(solution)/shard_map/ppermute | solution.py:17
  22.0 3.0 %collective-permute-done.4 = bf16[64,512]{1,0:T(8,128)(2,1)S(1)} collective-permute-done((bf16[64,512]{1,0:T(8,128)(2,1)S(1)}, bf16[64,512]{1,0:T(8,128)(2,1)S(1)}, u32[]{:S(2)}, u32[]{:S(2)}) %collective-permute-start.4) | collective-permute-done | bytes 65568 | tf_op jit(solution)/shard_map/ppermute | solution.py:17
  25.5 3.9 %collective-permute-done.5 = bf16[64,512]{1,0:T(8,128)(2,1)S(1)} collective-permute-done((bf16[64,512]{1,0:T(8,128)(2,1)S(1)}, bf16[64,512]{1,0:T(8,128)(2,1)S(1)}, u32[]{:S(2)}, u32[]{:S(2)}) %collective-permute-start.5) | collective-permute-done | bytes 65568 | tf_op jit(solution)/shard_map/ppermute | solution.py:17
  29.4 1.4 %bitcast_select_fusion = bf16[1024,512]{1,0:T(8,128)(2,1)S(1)} fusion(bf16[1024,512]{1,0:T(8,128)(2,1)} %collective-permute-done.8, bf16[1,4096,512]{2,1,0:T(8,128)(2,1)} %param.10, pred[]{:T(512)S(6)} %eq.27), kind=kLoop, calls=%fused_computation.2 | loop fusion | flops 524288 | bytes 3145729 | tf_op jit(solution)/shard_map/jit(_where)/select_n | solution.py:126
  30.8 10.5 %collective-permute-done.7 = bf16[1024,512]{1,0:T(8,128)(2,1)} collective-permute-done((bf16[1024,512]{1,0:T(8,128)(2,1)S(1)}, bf16[1024,512]{1,0:T(8,128)(2,1)}, u32[]{:S(2)}, u32[]{:S(2)}) %collective-permute-start.7) | collective-permute-done | bytes 1048608 | tf_op jit(solution)/shard_map/ppermute | solution.py:123
  41.9 0.7 collective-permute-start.9
  42.5 3.3 %collective-permute-start.15 = (f32[64,512]{1,0:T(8,128)S(1)}, f32[64,512]{1,0:T(8,128)S(1)}, u32[]{:S(2)}, u32[]{:S(2)}) collective-permute-start(f32[64,512]{1,0:T(8,128)S(1)} %bitcast.27), channel_id=1, source_target_pairs={{0,24},{8,0},{16,8},{24,16},{1,25},{9,1},{17,9},{25,17},{2,26},{10... | collective-permute-start | bytes 393224 | tf_op jit(solution)/shard_map/ppermute | solution.py:133
  45.9 1.3 %collective-permute-start.10 = (bf16[64,512]{1,0:T(8,128)(2,1)S(1)}, bf16[64,512]{1,0:T(8,128)(2,1)S(1)}, u32[]{:S(2)}, u32[]{:S(2)}) collective-permute-start(bf16[64,512]{1,0:T(8,128)(2,1)S(1)} %get-tuple-element.8), channel_id=1, source_target_pairs={{0,16},{8,24},{16,0},{24,8},{1,17},{9,25},{17,1},{25,9},{2,18},{10... | collective-permute-start | bytes 196616 | tf_op jit(solution)/shard_map/ppermute | solution.py:17
  47.2 0.9 collective-permute-start.16
  48.1 2.7 %collective-permute-done.10 = bf16[64,512]{1,0:T(8,128)(2,1)S(1)} collective-permute-done((bf16[64,512]{1,0:T(8,128)(2,1)S(1)}, bf16[64,512]{1,0:T(8,128)(2,1)S(1)}, u32[]{:S(2)}, u32[]{:S(2)}) %collective-permute-start.10) | collective-permute-done | bytes 65568 | tf_op jit(solution)/shard_map/ppermute | solution.py:17
  51.1 0.6 collective-permute-start.11
  51.7 1.3 %collective-permute-done.16 = bf16[64,1024]{1,0:T(8,128)(2,1)S(1)} collective-permute-done((bf16[64,1024]{1,0:T(8,128)(2,1)S(1)}, bf16[64,1024]{1,0:T(8,128)(2,1)S(1)}, u32[]{:S(2)}, u32[]{:S(2)}) %collective-permute-start.16) | collective-permute-done | bytes 131104 | tf_op jit(solution)/shard_map/ppermute | solution.py:17
  53.7 1.8 %collective-permute-done.11 = bf16[64,512]{1,0:T(8,128)(2,1)S(1)} collective-permute-done((bf16[64,512]{1,0:T(8,128)(2,1)S(1)}, bf16[64,512]{1,0:T(8,128)(2,1)S(1)}, u32[]{:S(2)}, u32[]{:S(2)}) %collective-permute-start.11) | collective-permute-done | bytes 65568 | tf_op jit(solution)/shard_map/ppermute | solution.py:17
  56.0 3.8 %collective-permute-done.12 = bf16[64,512]{1,0:T(8,128)(2,1)S(1)} collective-permute-done((bf16[64,512]{1,0:T(8,128)(2,1)S(1)}, bf16[64,512]{1,0:T(8,128)(2,1)S(1)}, u32[]{:S(2)}, u32[]{:S(2)}) %collective-permute-start.12) | collective-permute-done | bytes 65568 | tf_op jit(solution)/shard_map/ppermute | solution.py:17
  59.8 2.7 %collective-permute-start.13 = (bf16[64,512]{1,0:T(8,128)(2,1)S(1)}, bf16[64,512]{1,0:T(8,128)(2,1)S(1)}, u32[]{:S(2)}, u32[]{:S(2)}) collective-permute-start(bf16[64,512]{1,0:T(8,128)(2,1)S(1)} %add_convert_fusion.2), channel_id=1, source_target_pairs={{0,4},{1,5},{2,6},{3,7},{4,0},{5,1},{6,2},{7,3},{8,12},{9,13},{10,... | collective-permute-start | bytes 196616 | tf_op jit(solution)/shard_map/ppermute | solution.py:17
  62.5 3.1 %collective-permute-done.13 = bf16[64,512]{1,0:T(8,128)(2,1)S(1)} collective-permute-done((bf16[64,512]{1,0:T(8,128)(2,1)S(1)}, bf16[64,512]{1,0:T(8,128)(2,1)S(1)}, u32[]{:S(2)}, u32[]{:S(2)}) %collective-permute-start.13) | collective-permute-done | bytes 65568 | tf_op jit(solution)/shard_map/ppermute | solution.py:17
  65.7 0.6 collective-permute-start.14
  66.3 0.8 select_add_fusion.1
  67.1 2.9 %collective-permute-done.14 = bf16[64,512]{1,0:T(8,128)(2,1)S(1)} collective-permute-done((bf16[64,512]{1,0:T(8,128)(2,1)S(1)}, bf16[64,512]{1,0:T(8,128)(2,1)S(1)}, u32[]{:S(2)}, u32[]{:S(2)}) %collective-permute-start.14) | collective-permute-done | bytes 65568 | tf_op jit(solution)/shard_map/ppermute | solution.py:17
  70.4 1.3 %collective-permute-done.19 = f32[64,512]{1,0:T(8,128)S(1)} collective-permute-done((f32[64,512]{1,0:T(8,128)S(1)}, f32[64,512]{1,0:T(8,128)S(1)}, u32[]{:S(2)}, u32[]{:S(2)}) %collective-permute-start.19) | collective-permute-done | bytes 131104 | tf_op jit(solution)/shard_map/ppermute | solution.py:17
  71.8 2.5 %collective-permute-start.20 = (bf16[64,512]{1,0:T(8,128)(2,1)S(1)}, bf16[64,512]{1,0:T(8,128)(2,1)S(1)}, u32[]{:S(2)}, u32[]{:S(2)}) collective-permute-start(bf16[64,512]{1,0:T(8,128)(2,1)S(1)} %get-tuple-element.6), channel_id=1, source_target_pairs={{0,16},{8,24},{16,0},{24,8},{1,17},{9,25},{17,1},{25,9},{2,18},{10... | collective-permute-start | bytes 196616 | tf_op jit(solution)/shard_map/ppermute | solution.py:17
  74.3 2.4 %collective-permute-done.20 = bf16[64,512]{1,0:T(8,128)(2,1)S(1)} collective-permute-done((bf16[64,512]{1,0:T(8,128)(2,1)S(1)}, bf16[64,512]{1,0:T(8,128)(2,1)S(1)}, u32[]{:S(2)}, u32[]{:S(2)}) %collective-permute-start.20) | collective-permute-done | bytes 65568 | tf_op jit(solution)/shard_map/ppermute | solution.py:17
  77.6 1.9 %collective-permute-start.26 = (bf16[64,1024]{1,0:T(8,128)(2,1)S(1)}, bf16[64,1024]{1,0:T(8,128)(2,1)S(1)}, u32[]{:S(2)}, u32[]{:S(2)}) collective-permute-start(bf16[64,1024]{1,0:T(8,128)(2,1)S(1)} %pad_maximum_fusion.2), channel_id=1, source_target_pairs={{0,16},{8,24},{16,0},{24,8},{1,17},{9,25},{17,1},{25,9},{2,18},{10... | collective-permute-start | bytes 393224 | tf_op jit(solution)/shard_map/ppermute | solution.py:17
  79.6 1.8 %collective-permute-done.21 = bf16[64,512]{1,0:T(8,128)(2,1)S(1)} collective-permute-done((bf16[64,512]{1,0:T(8,128)(2,1)S(1)}, bf16[64,512]{1,0:T(8,128)(2,1)S(1)}, u32[]{:S(2)}, u32[]{:S(2)}) %collective-permute-start.21) | collective-permute-done | bytes 65568 | tf_op jit(solution)/shard_map/ppermute | solution.py:17
  81.5 1.2 %collective-permute-done.26 = bf16[64,1024]{1,0:T(8,128)(2,1)S(1)} collective-permute-done((bf16[64,1024]{1,0:T(8,128)(2,1)S(1)}, bf16[64,1024]{1,0:T(8,128)(2,1)S(1)}, u32[]{:S(2)}, u32[]{:S(2)}) %collective-permute-start.26) | collective-permute-done | bytes 131104 | tf_op jit(solution)/shard_map/ppermute | solution.py:17
  83.3 2.4 %collective-permute-done.22 = bf16[64,512]{1,0:T(8,128)(2,1)S(1)} collective-permute-done((bf16[64,512]{1,0:T(8,128)(2,1)S(1)}, bf16[64,512]{1,0:T(8,128)(2,1)S(1)}, u32[]{:S(2)}, u32[]{:S(2)}) %collective-permute-start.22) | collective-permute-done | bytes 65568 | tf_op jit(solution)/shard_map/ppermute | solution.py:17
  85.7 2.1 %collective-permute-start.23 = (bf16[64,512]{1,0:T(8,128)(2,1)S(1)}, bf16[64,512]{1,0:T(8,128)(2,1)S(1)}, u32[]{:S(2)}, u32[]{:S(2)}) collective-permute-start(bf16[64,512]{1,0:T(8,128)(2,1)S(1)} %add_convert_fusion), channel_id=1, source_target_pairs={{0,4},{1,5},{2,6},{3,7},{4,0},{5,1},{6,2},{7,3},{8,12},{9,13},{10,... | collective-permute-start | bytes 196616 | tf_op jit(solution)/shard_map/ppermute | solution.py:17
  87.8 3.3 %collective-permute-done.23 = bf16[64,512]{1,0:T(8,128)(2,1)S(1)} collective-permute-done((bf16[64,512]{1,0:T(8,128)(2,1)S(1)}, bf16[64,512]{1,0:T(8,128)(2,1)S(1)}, u32[]{:S(2)}, u32[]{:S(2)}) %collective-permute-start.23) | collective-permute-done | bytes 65568 | tf_op jit(solution)/shard_map/ppermute | solution.py:17
  91.8 2.9 %collective-permute-start.30 = (bf16[64,512]{1,0:T(8,128)(2,1)S(1)}, bf16[64,512]{1,0:T(8,128)(2,1)S(1)}, u32[]{:S(2)}, u32[]{:S(2)}) collective-permute-start(bf16[64,512]{1,0:T(8,128)(2,1)S(1)} %fusion.37), channel_id=1, source_target_pairs={{0,17},{1,16},{2,19},{3,18},{4,21},{5,20},{6,23},{7,22},{8,25},{9,... | collective-permute-start | bytes 196616 | tf_op jit(solution)/shard_map/ppermute | solution.py:24
  94.8 0.7 collective-permute-done.24
  95.5 2.0 %collective-permute-done.30 = bf16[64,512]{1,0:T(8,128)(2,1)S(1)} collective-permute-done((bf16[64,512]{1,0:T(8,128)(2,1)S(1)}, bf16[64,512]{1,0:T(8,128)(2,1)S(1)}, u32[]{:S(2)}, u32[]{:S(2)}) %collective-permute-start.30) | collective-permute-done | bytes 65568 | tf_op jit(solution)/shard_map/ppermute | solution.py:24
  97.5 1.4 %collective-permute-done.31 = bf16[64,512]{1,0:T(8,128)(2,1)S(1)} collective-permute-done((bf16[64,512]{1,0:T(8,128)(2,1)S(1)}, bf16[64,512]{1,0:T(8,128)(2,1)S(1)}, u32[]{:S(2)}, u32[]{:S(2)}) %collective-permute-start.31) | collective-permute-done | bytes 65568 | tf_op jit(solution)/shard_map/ppermute | solution.py:17
  99.1 0.8 select_add_fusion
  99.9 0.8 collective-permute-start.29
  100.7 0.8 pad_maximum_fusion
  102.1 1.1 %collective-permute-done.29 = f32[64,512]{1,0:T(8,128)S(1)} collective-permute-done((f32[64,512]{1,0:T(8,128)S(1)}, f32[64,512]{1,0:T(8,128)S(1)}, u32[]{:S(2)}, u32[]{:S(2)}) %collective-permute-start.29) | collective-permute-done | bytes 131104 | tf_op jit(solution)/shard_map/ppermute | solution.py:133
  103.3 1.5 %add_bitcast_fusion = f32[1,64,512]{2,1,0:T(8,128)} fusion(f32[64,512]{1,0:T(8,128)S(1)} %collective-permute-done.29, pred[]{:T(512)S(6)} %eq.12, bf16[64,1024]{1,0:T(8,128)(2,1)S(1)} %get-tuple-element.15, bf16[64,1024]{1,0:T(8,128)(2,1)S(1)} %get-tuple-element.14, bf16[64,1024]{1,0:T(8,128)(2,1)S(1)} %get-tuple-element.11, ...), kind=kOutput, calls=%fused_computation.53 | convolution fusion | flops 270598144 | bytes 4980737 | tf_op jit(solution)/shard_map/dot_general | solution.py:151
  (81 shorter events, 7.5 us)
Async XLA Ops:
  0.6 8.5 %copy-start = (bf16[512,1024]{1,0:T(8,128)(2,1)S(1)}, bf16[512,1024]{1,0:T(8,128)(2,1)}, u32[]{:S(2)}) copy-start(bf16[512,1024]{1,0:T(8,128)(2,1)} %param.9) | copy-start | bytes 3145732
  2.4 5.3 %collective-permute-start = (bf16[64,512]{1,0:T(8,128)(2,1)S(1)}, bf16[64,512]{1,0:T(8,128)(2,1)S(1)}, u32[]{:S(2)}, u32[]{:S(2)}) collective-permute-start(bf16[64,512]{1,0:T(8,128)(2,1)S(1)} %fusion.26), channel_id=1, source_target_pairs={{0,16},{8,24},{16,0},{24,8},{1,17},{9,25},{17,1},{25,9},{2,18},{10... | collective-permute-start | bytes 196616 | tf_op jit(solution)/shard_map/ppermute | solution.py:17
  7.8 1.3 %collective-permute-start.1 = (bf16[64,512]{1,0:T(8,128)(2,1)S(1)}, bf16[64,512]{1,0:T(8,128)(2,1)S(1)}, u32[]{:S(2)}, u32[]{:S(2)}) collective-permute-start(bf16[64,512]{1,0:T(8,128)(2,1)S(1)} %add.72), channel_id=1, source_target_pairs={{0,8},{8,0},{16,24},{24,16},{1,9},{9,1},{17,25},{25,17},{2,10},{10... | collective-permute-start | bytes 196616 | tf_op jit(solution)/shard_map/ppermute | solution.py:17
  9.4 5.3 %collective-permute-start.2 = (bf16[64,512]{1,0:T(8,128)(2,1)S(1)}, bf16[64,512]{1,0:T(8,128)(2,1)S(1)}, u32[]{:S(2)}, u32[]{:S(2)}) collective-permute-start(bf16[64,512]{1,0:T(8,128)(2,1)S(1)} %select_convert_fusion.2), channel_id=1, source_target_pairs={{0,1},{1,0},{2,3},{3,2},{4,5},{5,4},{6,7},{7,6},{8,9},{9,8},{10,11... | collective-permute-start | bytes 196616 | tf_op jit(solution)/shard_map/ppermute | solution.py:17
  11.5 2.2 %copy-start.1 = (bf16[1,4096,512]{2,1,0:T(8,128)(2,1)S(1)}, bf16[1,4096,512]{2,1,0:T(8,128)(2,1)}, u32[]{:S(2)}) copy-start(bf16[1,4096,512]{2,1,0:T(8,128)(2,1)} %param.10) | copy-start | bytes 12582916
  13.7 4.1 %copy-start.2 = (bf16[1,4096,512]{2,1,0:T(8,128)(2,1)S(1)}, bf16[1,4096,512]{2,1,0:T(8,128)(2,1)}, u32[]{:S(2)}) copy-start(bf16[1,4096,512]{2,1,0:T(8,128)(2,1)} %param.10) | copy-start | bytes 12582916
  13.7 8.4 %copy-start.6 = (f32[1024]{0:T(1024)S(1)}, f32[1024]{0:T(1024)}, u32[]{:S(2)}) copy-start(f32[1024]{0:T(1024)} %param.8) | copy-start | bytes 12292
  14.7 14.7 %collective-permute-start.8 = (bf16[1024,512]{1,0:T(8,128)(2,1)}, bf16[1024,512]{1,0:T(8,128)(2,1)}, u32[]{:S(2)}, u32[]{:S(2)}) collective-permute-start(bf16[1024,512]{1,0:T(8,128)(2,1)} %get-tuple-element.5), channel_id=1, source_target_pairs={{0,8},{8,0},{16,24},{24,16},{1,9},{9,1},{17,25},{25,17},{2,10},{10... | collective-permute-start | bytes 3145736 | tf_op jit(solution)/shard_map/ppermute | solution.py:123
  14.8 4.5 %collective-permute-start.3 = (bf16[64,512]{1,0:T(8,128)(2,1)S(1)}, bf16[64,512]{1,0:T(8,128)(2,1)S(1)}, u32[]{:S(2)}, u32[]{:S(2)}) collective-permute-start(bf16[64,512]{1,0:T(8,128)(2,1)S(1)} %add_convert_fusion.5), channel_id=1, source_target_pairs={{0,2},{1,3},{2,0},{3,1},{4,6},{5,7},{6,4},{7,5},{8,10},{9,11},{10,... | collective-permute-start | bytes 196616 | tf_op jit(solution)/shard_map/ppermute | solution.py:17
  16.4 25.0 %collective-permute-start.6 = (bf16[1024,512]{1,0:T(8,128)(2,1)S(1)}, bf16[1024,512]{1,0:T(8,128)(2,1)}, u32[]{:S(2)}, u32[]{:S(2)}) collective-permute-start(bf16[1024,512]{1,0:T(8,128)(2,1)S(1)} %get-tuple-element.4), channel_id=1, source_target_pairs={{0,24},{8,0},{16,8},{24,16},{1,25},{9,1},{17,9},{25,17},{2,26},{10... | collective-permute-start | bytes 3145736 | tf_op jit(solution)/shard_map/ppermute | solution.py:123
  17.9 23.5 %collective-permute-start.7 = (bf16[1024,512]{1,0:T(8,128)(2,1)S(1)}, bf16[1024,512]{1,0:T(8,128)(2,1)}, u32[]{:S(2)}, u32[]{:S(2)}) collective-permute-start(bf16[1024,512]{1,0:T(8,128)(2,1)S(1)} %shard_map.78), channel_id=1, source_target_pairs={{0,16},{8,0},{16,24},{24,8},{1,17},{9,1},{17,25},{25,9},{2,18},{10... | collective-permute-start | bytes 3145736 | tf_op jit(solution)/shard_map/ppermute | solution.py:123
  19.4 5.6 %collective-permute-start.4 = (bf16[64,512]{1,0:T(8,128)(2,1)S(1)}, bf16[64,512]{1,0:T(8,128)(2,1)S(1)}, u32[]{:S(2)}, u32[]{:S(2)}) collective-permute-start(bf16[64,512]{1,0:T(8,128)(2,1)S(1)} %add_convert_fusion.4), channel_id=1, source_target_pairs={{0,4},{1,5},{2,6},{3,7},{4,0},{5,1},{6,2},{7,3},{8,12},{9,13},{10,... | collective-permute-start | bytes 196616 | tf_op jit(solution)/shard_map/ppermute | solution.py:17
  25.0 4.3 %collective-permute-start.5 = (bf16[64,512]{1,0:T(8,128)(2,1)S(1)}, bf16[64,512]{1,0:T(8,128)(2,1)S(1)}, u32[]{:S(2)}, u32[]{:S(2)}) collective-permute-start(bf16[64,512]{1,0:T(8,128)(2,1)S(1)} %fusion.39), channel_id=1, source_target_pairs={{0,1},{1,0},{2,3},{3,2},{4,5},{5,4},{6,7},{7,6},{8,9},{9,8},{10,11... | collective-permute-start | bytes 196616 | tf_op jit(solution)/shard_map/ppermute | solution.py:17
  29.4 12.2 %copy-start.5 = (f32[1,64,512]{2,1,0:T(8,128)S(1)}, f32[1,64,512]{2,1,0:T(8,128)}, u32[]{:S(2)}) copy-start(f32[1,64,512]{2,1,0:T(8,128)} %param.11) | copy-start | bytes 393220
  30.8 20.0 %copy-start.4 = (bf16[64,512]{1,0:T(8,128)(2,1)S(1)}, bf16[64,512]{1,0:T(8,128)(2,1)}, u32[]{:S(2)}) copy-start(bf16[64,512]{1,0:T(8,128)(2,1)} %param.6) | copy-start | bytes 196612
  41.9 4.0 %collective-permute-start.9 = (f32[64,512]{1,0:T(8,128)S(1)}, f32[64,512]{1,0:T(8,128)S(1)}, u32[]{:S(2)}, u32[]{:S(2)}) collective-permute-start(f32[64,512]{1,0:T(8,128)S(1)} %convolution_add_fusion.1), channel_id=1, source_target_pairs={{0,8},{8,0},{16,24},{24,16},{1,9},{9,1},{17,25},{25,17},{2,10},{10... | collective-permute-start | bytes 393224 | tf_op jit(solution)/shard_map/ppermute | solution.py:17
  42.5 23.7 %collective-permute-start.15 = (f32[64,512]{1,0:T(8,128)S(1)}, f32[64,512]{1,0:T(8,128)S(1)}, u32[]{:S(2)}, u32[]{:S(2)}) collective-permute-start(f32[64,512]{1,0:T(8,128)S(1)} %bitcast.27), channel_id=1, source_target_pairs={{0,24},{8,0},{16,8},{24,16},{1,25},{9,1},{17,9},{25,17},{2,26},{10... | collective-permute-start | bytes 393224 | tf_op jit(solution)/shard_map/ppermute | solution.py:133
  45.9 20.4 %copy-start.3 = (bf16[1,4096,512]{2,1,0:T(8,128)(2,1)S(1)}, bf16[1,4096,512]{2,1,0:T(8,128)(2,1)}, u32[]{:S(2)}) copy-start(bf16[1,4096,512]{2,1,0:T(8,128)(2,1)} %param.10) | copy-start | bytes 12582916
  45.9 4.8 %collective-permute-start.10 = (bf16[64,512]{1,0:T(8,128)(2,1)S(1)}, bf16[64,512]{1,0:T(8,128)(2,1)S(1)}, u32[]{:S(2)}, u32[]{:S(2)}) collective-permute-start(bf16[64,512]{1,0:T(8,128)(2,1)S(1)} %get-tuple-element.8), channel_id=1, source_target_pairs={{0,16},{8,24},{16,0},{24,8},{1,17},{9,25},{17,1},{25,9},{2,18},{10... | collective-permute-start | bytes 196616 | tf_op jit(solution)/shard_map/ppermute | solution.py:17
  47.2 5.8 %collective-permute-start.16 = (bf16[64,1024]{1,0:T(8,128)(2,1)S(1)}, bf16[64,1024]{1,0:T(8,128)(2,1)S(1)}, u32[]{:S(2)}, u32[]{:S(2)}) collective-permute-start(bf16[64,1024]{1,0:T(8,128)(2,1)S(1)} %pad_maximum_fusion.1), channel_id=1, source_target_pairs={{0,16},{8,24},{16,0},{24,8},{1,17},{9,25},{17,1},{25,9},{2,18},{10... | collective-permute-start | bytes 393224 | tf_op jit(solution)/shard_map/ppermute | solution.py:17
  51.1 4.3 %collective-permute-start.11 = (bf16[64,512]{1,0:T(8,128)(2,1)S(1)}, bf16[64,512]{1,0:T(8,128)(2,1)S(1)}, u32[]{:S(2)}, u32[]{:S(2)}) collective-permute-start(bf16[64,512]{1,0:T(8,128)(2,1)S(1)} %select_convert_fusion.1), channel_id=1, source_target_pairs={{0,1},{1,0},{2,3},{3,2},{4,5},{5,4},{6,7},{7,6},{8,9},{9,8},{10,11... | collective-permute-start | bytes 196616 | tf_op jit(solution)/shard_map/ppermute | solution.py:17
  53.1 2.9 %collective-permute-start.18 = (bf16[64,1024]{1,0:T(8,128)(2,1)S(1)}, bf16[64,1024]{1,0:T(8,128)(2,1)S(1)}, u32[]{:S(2)}, u32[]{:S(2)}) collective-permute-start(bf16[64,1024]{1,0:T(8,128)(2,1)S(1)} %get-tuple-element.25), channel_id=1, source_target_pairs={{0,8},{8,0},{16,24},{24,16},{1,9},{9,1},{17,25},{25,17},{2,10},{10... | collective-permute-start | bytes 393224 | tf_op jit(solution)/shard_map/ppermute | solution.py:17
  53.2 9.3 %collective-permute-start.17 = (bf16[64,1024]{1,0:T(8,128)(2,1)S(1)}, bf16[64,1024]{1,0:T(8,128)(2,1)S(1)}, u32[]{:S(2)}, u32[]{:S(2)}) collective-permute-start(bf16[64,1024]{1,0:T(8,128)(2,1)S(1)} %get-tuple-element.24), channel_id=1, source_target_pairs={{0,8},{8,0},{16,24},{24,16},{1,9},{9,1},{17,25},{25,17},{2,10},{10... | collective-permute-start | bytes 393224 | tf_op jit(solution)/shard_map/ppermute | solution.py:17
  55.5 4.3 %collective-permute-start.12 = (bf16[64,512]{1,0:T(8,128)(2,1)S(1)}, bf16[64,512]{1,0:T(8,128)(2,1)S(1)}, u32[]{:S(2)}, u32[]{:S(2)}) collective-permute-start(bf16[64,512]{1,0:T(8,128)(2,1)S(1)} %add_convert_fusion.3), channel_id=1, source_target_pairs={{0,2},{1,3},{2,0},{3,1},{4,6},{5,7},{6,4},{7,5},{8,10},{9,11},{10,... | collective-permute-start | bytes 196616 | tf_op jit(solution)/shard_map/ppermute | solution.py:17
  59.8 5.8 %collective-permute-start.13 = (bf16[64,512]{1,0:T(8,128)(2,1)S(1)}, bf16[64,512]{1,0:T(8,128)(2,1)S(1)}, u32[]{:S(2)}, u32[]{:S(2)}) collective-permute-start(bf16[64,512]{1,0:T(8,128)(2,1)S(1)} %add_convert_fusion.2), channel_id=1, source_target_pairs={{0,4},{1,5},{2,6},{3,7},{4,0},{5,1},{6,2},{7,3},{8,12},{9,13},{10,... | collective-permute-start | bytes 196616 | tf_op jit(solution)/shard_map/ppermute | solution.py:17
  65.7 4.3 %collective-permute-start.14 = (bf16[64,512]{1,0:T(8,128)(2,1)S(1)}, bf16[64,512]{1,0:T(8,128)(2,1)S(1)}, u32[]{:S(2)}, u32[]{:S(2)}) collective-permute-start(bf16[64,512]{1,0:T(8,128)(2,1)S(1)} %fusion.38), channel_id=1, source_target_pairs={{0,1},{1,0},{2,3},{3,2},{4,5},{5,4},{6,7},{7,6},{8,9},{9,8},{10,11... | collective-permute-start | bytes 196616 | tf_op jit(solution)/shard_map/ppermute | solution.py:17
  70.3 1.4 %collective-permute-start.19 = (f32[64,512]{1,0:T(8,128)S(1)}, f32[64,512]{1,0:T(8,128)S(1)}, u32[]{:S(2)}, u32[]{:S(2)}) collective-permute-start(f32[64,512]{1,0:T(8,128)S(1)} %convolution_add_fusion), channel_id=1, source_target_pairs={{0,8},{8,0},{16,24},{24,16},{1,9},{9,1},{17,25},{25,17},{2,10},{10... | collective-permute-start | bytes 393224 | tf_op jit(solution)/shard_map/ppermute | solution.py:17
  71.8 4.9 %collective-permute-start.20 = (bf16[64,512]{1,0:T(8,128)(2,1)S(1)}, bf16[64,512]{1,0:T(8,128)(2,1)S(1)}, u32[]{:S(2)}, u32[]{:S(2)}) collective-permute-start(bf16[64,512]{1,0:T(8,128)(2,1)S(1)} %get-tuple-element.6), channel_id=1, source_target_pairs={{0,16},{8,24},{16,0},{24,8},{1,17},{9,25},{17,1},{25,9},{2,18},{10... | collective-permute-start | bytes 196616 | tf_op jit(solution)/shard_map/ppermute | solution.py:17
  74.3 24.8 %collective-permute-start.25 = (f32[64,512]{1,0:T(8,128)S(1)}, f32[64,512]{1,0:T(8,128)S(1)}, u32[]{:S(2)}, u32[]{:S(2)}) collective-permute-start(f32[64,512]{1,0:T(8,128)S(1)} %select_add_fusion.1), channel_id=1, source_target_pairs={{0,24},{8,0},{16,8},{24,16},{1,25},{9,1},{17,9},{25,17},{2,26},{10... | collective-permute-start | bytes 393224 | tf_op jit(solution)/shard_map/ppermute | solution.py:133
  77.0 4.3 %collective-permute-start.21 = (bf16[64,512]{1,0:T(8,128)(2,1)S(1)}, bf16[64,512]{1,0:T(8,128)(2,1)S(1)}, u32[]{:S(2)}, u32[]{:S(2)}) collective-permute-start(bf16[64,512]{1,0:T(8,128)(2,1)S(1)} %select_convert_fusion), channel_id=1, source_target_pairs={{0,1},{1,0},{2,3},{3,2},{4,5},{5,4},{6,7},{7,6},{8,9},{9,8},{10,11... | collective-permute-start | bytes 196616 | tf_op jit(solution)/shard_map/ppermute | solution.py:17
  77.6 5.0 %collective-permute-start.26 = (bf16[64,1024]{1,0:T(8,128)(2,1)S(1)}, bf16[64,1024]{1,0:T(8,128)(2,1)S(1)}, u32[]{:S(2)}, u32[]{:S(2)}) collective-permute-start(bf16[64,1024]{1,0:T(8,128)(2,1)S(1)} %pad_maximum_fusion.2), channel_id=1, source_target_pairs={{0,16},{8,24},{16,0},{24,8},{1,17},{9,25},{17,1},{25,9},{2,18},{10... | collective-permute-start | bytes 393224 | tf_op jit(solution)/shard_map/ppermute | solution.py:17
  81.4 4.3 %collective-permute-start.22 = (bf16[64,512]{1,0:T(8,128)(2,1)S(1)}, bf16[64,512]{1,0:T(8,128)(2,1)S(1)}, u32[]{:S(2)}, u32[]{:S(2)}) collective-permute-start(bf16[64,512]{1,0:T(8,128)(2,1)S(1)} %add_convert_fusion.1), channel_id=1, source_target_pairs={{0,2},{1,3},{2,0},{3,1},{4,6},{5,7},{6,4},{7,5},{8,10},{9,11},{10,... | collective-permute-start | bytes 196616 | tf_op jit(solution)/shard_map/ppermute | solution.py:17
  82.7 5.1 %collective-permute-start.28 = (bf16[64,1024]{1,0:T(8,128)(2,1)S(1)}, bf16[64,1024]{1,0:T(8,128)(2,1)S(1)}, u32[]{:S(2)}, u32[]{:S(2)}) collective-permute-start(bf16[64,1024]{1,0:T(8,128)(2,1)S(1)} %get-tuple-element.19), channel_id=1, source_target_pairs={{0,8},{8,0},{16,24},{24,16},{1,9},{9,1},{17,25},{25,17},{2,10},{10... | collective-permute-start | bytes 393224 | tf_op jit(solution)/shard_map/ppermute | solution.py:17
  82.8 9.0 %collective-permute-start.27 = (bf16[64,1024]{1,0:T(8,128)(2,1)S(1)}, bf16[64,1024]{1,0:T(8,128)(2,1)S(1)}, u32[]{:S(2)}, u32[]{:S(2)}) collective-permute-start(bf16[64,1024]{1,0:T(8,128)(2,1)S(1)} %get-tuple-element.18), channel_id=1, source_target_pairs={{0,8},{8,0},{16,24},{24,16},{1,9},{9,1},{17,25},{25,17},{2,10},{10... | collective-permute-start | bytes 393224 | tf_op jit(solution)/shard_map/ppermute | solution.py:17
  85.7 5.4 %collective-permute-start.23 = (bf16[64,512]{1,0:T(8,128)(2,1)S(1)}, bf16[64,512]{1,0:T(8,128)(2,1)S(1)}, u32[]{:S(2)}, u32[]{:S(2)}) collective-permute-start(bf16[64,512]{1,0:T(8,128)(2,1)S(1)} %add_convert_fusion), channel_id=1, source_target_pairs={{0,4},{1,5},{2,6},{3,7},{4,0},{5,1},{6,2},{7,3},{8,12},{9,13},{10,... | collective-permute-start | bytes 196616 | tf_op jit(solution)/shard_map/ppermute | solution.py:17
  91.2 4.3 %collective-permute-start.24 = (bf16[64,512]{1,0:T(8,128)(2,1)S(1)}, bf16[64,512]{1,0:T(8,128)(2,1)S(1)}, u32[]{:S(2)}, u32[]{:S(2)}) collective-permute-start(bf16[64,512]{1,0:T(8,128)(2,1)S(1)} %fusion.37), channel_id=1, source_target_pairs={{0,1},{1,0},{2,3},{3,2},{4,5},{5,4},{6,7},{7,6},{8,9},{9,8},{10,11... | collective-permute-start | bytes 196616 | tf_op jit(solution)/shard_map/ppermute | solution.py:17
  91.8 5.7 %collective-permute-start.30 = (bf16[64,512]{1,0:T(8,128)(2,1)S(1)}, bf16[64,512]{1,0:T(8,128)(2,1)S(1)}, u32[]{:S(2)}, u32[]{:S(2)}) collective-permute-start(bf16[64,512]{1,0:T(8,128)(2,1)S(1)} %fusion.37), channel_id=1, source_target_pairs={{0,17},{1,16},{2,19},{3,18},{4,21},{5,20},{6,23},{7,22},{8,25},{9,... | collective-permute-start | bytes 196616 | tf_op jit(solution)/shard_map/ppermute | solution.py:24
  94.7 4.3 %collective-permute-start.31 = (bf16[64,512]{1,0:T(8,128)(2,1)S(1)}, bf16[64,512]{1,0:T(8,128)(2,1)S(1)}, u32[]{:S(2)}, u32[]{:S(2)}) collective-permute-start(bf16[64,512]{1,0:T(8,128)(2,1)S(1)} %fusion.37), channel_id=1, source_target_pairs={{0,16},{8,24},{16,0},{24,8},{1,17},{9,25},{17,1},{25,9},{2,18},{10... | collective-permute-start | bytes 196616 | tf_op jit(solution)/shard_map/ppermute | solution.py:17
  99.0 2.5 %collective-permute-start.33 = (bf16[64,1024]{1,0:T(8,128)(2,1)S(1)}, bf16[64,1024]{1,0:T(8,128)(2,1)S(1)}, u32[]{:S(2)}, u32[]{:S(2)}) collective-permute-start(bf16[64,1024]{1,0:T(8,128)(2,1)S(1)} %get-tuple-element.13), channel_id=1, source_target_pairs={{0,8},{8,0},{16,24},{24,16},{1,9},{9,1},{17,25},{25,17},{2,10},{10... | collective-permute-start | bytes 393224 | tf_op jit(solution)/shard_map/ppermute | solution.py:17
  99.9 3.3 %collective-permute-start.29 = (f32[64,512]{1,0:T(8,128)S(1)}, f32[64,512]{1,0:T(8,128)S(1)}, u32[]{:S(2)}, u32[]{:S(2)}) collective-permute-start(f32[64,512]{1,0:T(8,128)S(1)} %select_add_fusion), channel_id=1, source_target_pairs={{0,24},{8,0},{16,8},{24,16},{1,25},{9,1},{17,9},{25,17},{2,26},{10... | collective-permute-start | bytes 393224 | tf_op jit(solution)/shard_map/ppermute | solution.py:133
  100.7 1.3 %collective-permute-start.32 = (bf16[64,1024]{1,0:T(8,128)(2,1)S(1)}, bf16[64,1024]{1,0:T(8,128)(2,1)S(1)}, u32[]{:S(2)}, u32[]{:S(2)}) collective-permute-start(bf16[64,1024]{1,0:T(8,128)(2,1)S(1)} %get-tuple-element.12), channel_id=1, source_target_pairs={{0,8},{8,0},{16,24},{24,16},{1,9},{9,1},{17,25},{25,17},{2,10},{10... | collective-permute-start | bytes 393224 | tf_op jit(solution)/shard_map/ppermute | solution.py:17
